TPU v7x, 32 devices: a whole 2x2x4 slice. The times are simulated.
32 devices in a mesh: dp: 4 (over y, core), seq: 2 (over x), head: 4 (over z).
Axes of the slice: x: 2, y: 2, z: 4, core: 2. Of those that a mesh axis runs over, the one named last changes fastest.
Arguments:
- queries: bfloat16 [4, 512, 1536], P('dp', 'seq', 'head'), may hold values from -160 to 160
- key_cache: bfloat16 [4, 512, 512], P('dp', 'seq', 'head'), may hold values from -7 to 7
- value_cache: bfloat16 [4, 512, 512], P('dp', 'seq', 'head'), may hold values from -6 to 6
- out_grad: bfloat16 [4, 512, 1536], P('dp', 'seq', 'head'), may hold values from -6 to 6
- doc_ids: int32 [4, 512], P('dp', 'seq'), may hold values from 0 to 1, never falling along the last dimension, each value on 1 to 511 neighbouring positions
- layer_input: bfloat16 [4, 512, 3072], P('dp', ('seq', 'head')), may hold values from -6 to 6
- key_proj: bfloat16 [3072, 512], P(None, 'head'), may hold values from -0.109375 to 0.109375
- value_proj: bfloat16 [3072, 512], P(None, 'head'), may hold values from -0.109375 to 0.109375
Outputs:
- query_grad: bfloat16 [4, 512, 1536], P('dp', 'seq', 'head')
- input_grad: bfloat16 [4, 512, 3072], P('dp', ('seq', 'head'))
- grad_keyproj: float32 [3072, 512], P(None, 'head')
- grad_valueproj: float32 [3072, 512], P(None, 'head')
Inputs may be any that keep to these rules, and one draw needn't show every extreme that they name: `doc_ids`: document numbers never fall along a sequence; a document spans 1 to 511 positions.
All inputs are finite; a program needn't handle non-finite values.
Results may differ from a plain program's by a relative error of at most 0.02.
Values may be sent and summed in bfloat16 or wider, within the bound.
No kernel may reach another device: no remote copies, remote signals or barrier semaphores. Data moves between devices by JAX's collectives and lax.ppermute only.
A program may use at most 64 MiB of HBM per device.

v0:
```python
import functools

import jax
import jax.numpy as jnp
from jax import lax
from jax.experimental import pallas as pl
from jax.experimental.pallas import tpu as pltpu
from jax.sharding import PartitionSpec as P

HD = 128
MASKED = -1e30
F32 = jnp.float32
BF16 = jnp.bfloat16
VMEM = pl.BlockSpec(memory_space=pltpu.VMEM)
SMEM = pl.BlockSpec(memory_space=pltpu.SMEM)
ANY = pl.BlockSpec(memory_space=pl.ANY)


def dot(a, b, ca, cb):
    return lax.dot_general(a, b, (((ca,), (cb,)), ((), ())), preferred_element_type=F32)


def scalars(*values):
    return jnp.stack([jnp.asarray(v, jnp.int32) for v in values])


def attention_kernel(blocks, group, at_ref, q_ref, g_ref, *refs):
    kv_refs, refs = refs[:blocks], refs[blocks:]
    dq_ref, own_ref, *prev_refs = refs
    rows = q_ref.shape[0]
    k_refs = [ref.at[:rows, :HD] for ref in kv_refs]
    v_refs = [ref.at[:rows, HD:] for ref in kv_refs]
    doc_refs = [ref.at[rows:, :rows] for ref in kv_refs]
    scale = HD**-0.5
    query_doc = doc_refs[0][...].astype(F32)
    allowed = []
    for b in range(blocks):
        key_doc = doc_refs[b][...].astype(F32)
        if b:
            key_doc = jnp.where(at_ref[3] >= b, key_doc, -1.0)
        same = jnp.broadcast_to(key_doc, (HD, rows)).T[:, :1] == query_doc
        if b == 0:
            key_pos = lax.broadcasted_iota(jnp.int32, (rows, rows), 0)
            query_pos = lax.broadcasted_iota(jnp.int32, (rows, rows), 1)
            same = same & (key_pos <= query_pos)
        allowed.append(same)
    dk = [jnp.zeros((rows, HD), F32) for _ in range(blocks)]
    dv = [jnp.zeros((rows, HD), F32) for _ in range(blocks)]
    for h in range(group):
        cols = slice(h * HD, (h + 1) * HD)
        q, g = q_ref[:, cols], g_ref[:, cols]
        scores = [
            jnp.where(allowed[b], dot(k_refs[b][...], q, 1, 1) * scale, MASKED)
            for b in range(blocks)
        ]
        top = functools.reduce(jnp.maximum, [jnp.max(x, axis=0, keepdims=True) for x in scores])
        parts = [jnp.exp(x - top) for x in scores]
        total = sum(jnp.sum(x, axis=0, keepdims=True) for x in parts)
        inverse = 1.0 / total
        weights = [x * inverse for x in parts]
        wgrads = [dot(v_refs[b][...], g, 1, 1) for b in range(blocks)]
        delta = sum(jnp.sum(w * d, axis=0, keepdims=True) for w, d in zip(weights, wgrads))
        dq = jnp.zeros((rows, HD), F32)
        for b in range(blocks):
            ds = (weights[b] * (wgrads[b] - delta) * scale).astype(BF16)
            dq += dot(ds, k_refs[b][...], 0, 0)
            dk[b] += dot(ds, q, 1, 0)
            dv[b] += dot(weights[b].astype(BF16), g, 1, 0)
        dq_ref[:, cols] = dq.astype(BF16)
    own_ref[:, :HD] = dk[0]
    own_ref[:, HD:] = dv[0]
    for b in range(1, blocks):
        prev_refs[b - 1][:, :HD] = dk[b].astype(BF16)
        prev_refs[b - 1][:, HD:] = dv[b].astype(BF16)


def attention(at, q, g, packs):
    rows, width = q.shape
    blocks = len(packs)
    outs = [
        jax.ShapeDtypeStruct((rows, width), BF16),
        jax.ShapeDtypeStruct((rows, 2 * HD), F32),
    ] + [jax.ShapeDtypeStruct((rows, 2 * HD), BF16)] * (blocks - 1)
    return pl.pallas_call(
        functools.partial(attention_kernel, blocks, width // HD),
        out_shape=outs,
        in_specs=[SMEM] + [VMEM] * (2 + blocks),
        name="attention",
        cost_estimate=pl.CostEstimate(
            flops=10 * rows * rows * blocks * width,
            transcendentals=rows * rows * blocks * width // HD,
            bytes_accessed=8 * rows * width,
        ),
    )(at, q, g, *packs)


def grads_kernel(slots, sub, fars, at_ref, *refs):
    count = len(slots)
    x_refs, refs = refs[: count + fars], refs[count + fars :]
    own_ref, other_ref, *add_refs, out_ref = refs
    z = at_ref[0]
    half = own_ref.shape[0] * sub
    total = jnp.zeros(out_ref.shape, F32)
    for ref in add_refs:
        total += ref[...]
    for i, r in enumerate(slots):
        x = x_refs[i][...]
        if fars and i == count - 1:
            x = jnp.where((z == 0) | (z == r), x_refs[count][...], x)
        start = pl.multiple_of((z ^ r) * sub, sub)
        pieces = [
            ref[:, pl.ds(start, sub), :].reshape(half, out_ref.shape[1])
            for ref in (own_ref, other_ref)
        ]
        total += dot(x, jnp.concatenate(pieces, axis=0), 0, 0)
    out_ref[...] = total.astype(out_ref.dtype)


def grads(at, xs, slots, own, other, adds, dtype):
    sub = xs[0].shape[0] // (2 * own.shape[0])
    size, width = xs[0].shape[1], own.shape[2]
    return pl.pallas_call(
        functools.partial(grads_kernel, tuple(slots), sub, len(xs) - len(slots)),
        out_shape=jax.ShapeDtypeStruct((size, width), dtype),
        in_specs=[SMEM] + [VMEM] * (len(xs) + 2 + len(adds)),
        cost_estimate=pl.CostEstimate(
            flops=2 * len(xs) * xs[0].size * width, transcendentals=0, bytes_accessed=2 * xs[0].size
        ),
    )(at, *xs, own, other, *adds)


def input_kernel(heads, own_ref, other_ref, *refs):
    row_refs, out_refs = refs[:heads], refs[heads:]
    size, sub = own_ref.shape[1], out_refs[0].shape[0]
    for j, w_ref in enumerate((own_ref, other_ref)):
        part = sum(dot(row_refs[r][...], w_ref[r], 1, 1) for r in range(heads))
        for o, out_ref in enumerate(out_refs):
            out_ref[:, j * size : (j + 1) * size] = part[o * sub : (o + 1) * sub].astype(BF16)


def input_parts(w_own, w_other, rows, cells):
    heads, size, sub = len(rows), w_own.shape[1], rows[0].shape[0] // cells
    return pl.pallas_call(
        functools.partial(input_kernel, heads),
        out_shape=[jax.ShapeDtypeStruct((sub, 2 * size), BF16)] * cells,
        in_specs=[VMEM] * (heads + 2),
        name="input_grads",
        cost_estimate=pl.CostEstimate(
            flops=4 * cells * sub * w_own.size, transcendentals=0, bytes_accessed=4 * w_own.size
        ),
    )(w_own, w_other, *rows)


def place_kernel(cells, at_ref, *refs):
    size = refs[0].shape[1] // 2
    out_ref = refs[cells]
    for o in range(cells):
        base = (at_ref[1] ^ o) * 2
        for j, core in ((0, at_ref[2]), (1, 1 - at_ref[2])):
            start = (base + core) * size
            if size % HD == 0:
                start = pl.multiple_of(start, HD)
            out_ref[:, pl.ds(start, size)] = refs[o][:, j * size : (j + 1) * size]


def place(at, pieces):
    cells, (sub, slab) = len(pieces), pieces[0].shape
    if slab % (2 * HD):
        out = jnp.zeros((sub, slab * cells), BF16)
        for o, piece in enumerate(pieces):
            for j, half in enumerate(jnp.split(piece, 2, axis=1)):
                start = ((at[1] ^ o) * 2 + (at[2] ^ j)) * (slab // 2)
                out = lax.dynamic_update_slice_in_dim(out, half, start, 1)
        return out
    return pl.pallas_call(
        functools.partial(place_kernel, cells),
        out_shape=jax.ShapeDtypeStruct((sub, slab * cells), BF16),
        in_specs=[SMEM] + [VMEM] * cells,
        name="place",
    )(at, *pieces)


def spread_kernel(places, at_ref, *refs):
    pieces, (key_ref, value_ref, *bufs, sems) = refs[: len(places)], refs[-5:]
    size = pieces[0].shape[0]
    waits = []
    for i, ((o, flip), piece) in enumerate(zip(places, pieces)):
        base = pl.multiple_of(((at_ref[1] ^ o) * 2 + (at_ref[2] ^ flip)) * size, 8)
        for n, (out_ref, buf) in enumerate(zip((key_ref, value_ref), bufs)):
            buf[i] = piece[:, n * HD : (n + 1) * HD].astype(F32)
            copy = pltpu.make_async_copy(
                buf.at[i], out_ref.at[pl.ds(base, size), :], sems.at[n, i]
            )
            copy.start()
            waits.append(copy)
    for copy in waits:
        copy.wait()


def spread(at, total, items, outs=()):
    count, size = len(items), items[0][2].shape[0]
    shape = jax.ShapeDtypeStruct((total, HD), F32)
    buf = pltpu.VMEM((count, size, HD), F32)
    return pl.pallas_call(
        functools.partial(spread_kernel, tuple(item[:2] for item in items)),
        out_shape=[shape, shape],
        in_specs=[SMEM] + [VMEM] * count + [ANY] * len(outs),
        out_specs=[ANY, ANY],
        scratch_shapes=[buf, buf, pltpu.SemaphoreType.DMA((2, count))],
        input_output_aliases={1 + count + n: n for n in range(len(outs))},
    )(at, *[item[2] for item in items], *outs)


def swap_pairs(n, m):
    return [(i, i ^ m) for i in range(n)]


def far_first(count):
    return sorted(range(1, count), key=lambda m: (-bin(m).count("1"), -m))


def line_exchange(x):
    n = lax.axis_size("head")
    slots = {0: x}
    for r in head_offsets(n):
        pairs = swap_pairs(n, r)
        if n == 4 and r == 3:
            pairs = [(0, 0), (1, 2), (2, 1), (3, 3)]
        slots[r] = lax.ppermute(x, "head", pairs)
    out = [slots[r] for r in range(n)]
    if n == 4:
        out.append(lax.ppermute(slots[2], "head", swap_pairs(n, 1)))
    return out


def head_offsets(n):
    return [2, 1, 3] if n == 4 else list(range(1, n))


def shards(queries, key_cache, value_cache, out_grad, doc_ids, layer_input, key_proj, value_proj):
    dp, seq, heads = (lax.axis_size(a) for a in ("dp", "seq", "head"))
    d, s, z = (lax.axis_index(a) for a in ("dp", "seq", "head"))
    plane, cells = dp * seq, dp // 2 * seq
    core, cell = d % 2, d // 2 * seq + s
    rows, _ = queries.shape[1:]
    d_model = layer_input.shape[2]
    size = d_model // plane
    sub = rows // heads
    both = ("dp", "seq")

    def member(o, c):
        return (o // seq * 2 + c) * seq + o % seq

    def cell_gather(x):
        got = {0: x}
        for o in far_first(cells):
            got[o] = lax.ppermute(x, both, swap_pairs(plane, member(o, 0)))
        return [got[o] for o in range(cells)]

    def core_swap(x):
        return lax.ppermute(x, "dp", swap_pairs(dp, 1))

    pack = jnp.concatenate([key_cache[0], value_cache[0]], axis=1)
    lanes = max(rows, 2 * HD)
    pack = jnp.concatenate(
        [
            jnp.pad(pack, ((0, 0), (0, lanes - 2 * HD))),
            jnp.pad(doc_ids.astype(BF16), ((0, 0), (0, lanes - rows))),
        ],
        axis=0,
    )
    packs = [pack]
    for r in range(1, seq):
        pairs = [(i, (i + r) % seq) for i in range(seq)]
        packs.append(lax.ppermute(pack, "seq", pairs))

    x = layer_input[0]
    got = []
    for o in range(cells):
        piece = lax.dynamic_slice_in_dim(x, (cell ^ o) * 2 * size, 2 * size, 1)
        if o:
            piece = lax.ppermute(piece, both, swap_pairs(plane, member(o, 0)))
        got.append(piece)
    got = jnp.concatenate(got, axis=0)
    mine = lax.dynamic_slice_in_dim(got, core * size, size, 1)
    theirs = lax.dynamic_slice_in_dim(got, (1 - core) * size, size, 1)
    x_plane = jnp.concatenate([mine, core_swap(theirs)], axis=0)

    own_slice = (cell * 2 + core) * size
    w_slice = jnp.concatenate(
        [lax.dynamic_slice_in_dim(w, own_slice, size, 0) for w in (key_proj, value_proj)], axis=1
    )
    w_slots = line_exchange(w_slice)
    x_slots = line_exchange(x_plane)
    at = scalars(z, cell, core, s)

    query_grad, own_terms, *prev_terms = attention(at, queries[0], out_grad[0], packs)
    dkv = own_terms
    for r in range(1, seq):
        pairs = [(i, (i - r) % seq) for i in range(seq)]
        dkv = dkv + lax.ppermute(prev_terms[r - 1], "seq", pairs).astype(F32)
    dkv = dkv.astype(BF16)

    dkv_own = jnp.stack(cell_gather(dkv))
    dkv_other = core_swap(dkv_own)
    head_rows = []
    for r in range(heads):
        piece = lax.dynamic_slice_in_dim(dkv_own, (z ^ r) * sub, sub, 1)
        piece = piece.reshape(cells * sub, 2 * HD)
        head_rows.append(lax.ppermute(piece, "head", swap_pairs(heads, r)) if r else piece)

    slots = list(range(heads))
    part = grads(at, x_slots[: heads - 1], slots[:-1], dkv_own, dkv_other, [], F32)
    grad = grads(at, x_slots[heads - 1 :], slots[-1:], dkv_own, dkv_other, [part], BF16)
    grad_own = cell_gather(grad)
    items = [(o, 0, g) for o, g in enumerate(grad_own)]
    items += [(o, 1, core_swap(g)) for o, g in enumerate(grad_own)]
    outs = spread(at, d_model, [i for i in items if i[0] == 0])
    grad_keyproj, grad_valueproj = spread(at, d_model, [i for i in items if i[0]], outs)

    if len(w_slots) > heads:
        outer = (z == 0) | (z == heads - 1)
        w_slots = w_slots[: heads - 1] + [jnp.where(outer, w_slots[heads], w_slots[heads - 1])]
    w_own = jnp.stack(w_slots)
    parts = list(input_parts(w_own, core_swap(w_own), head_rows, cells))
    for o in far_first(cells):
        parts[o] = lax.ppermute(parts[o], both, swap_pairs(plane, member(o, 0)))
    input_grad = place(at, parts)
    return query_grad[None], input_grad[None], grad_keyproj, grad_valueproj


def solution(mesh):
    return jax.shard_map(
        shards,
        mesh=mesh,
        in_specs=(
            P("dp", "seq", "head"),
            P("dp", "seq", "head"),
            P("dp", "seq", "head"),
            P("dp", "seq", "head"),
            P("dp", "seq"),
            P("dp", ("seq", "head"), None),
            P(None, "head"),
            P(None, "head"),
        ),
        out_specs=(
            P("dp", "seq", "head"),
            P("dp", ("seq", "head"), None),
            P(None, "head"),
            P(None, "head"),
        ),
        check_vma=False,
    )
```

profile of v0, /device:TPU:0, one launch (start us, length us, event | category | flops | bytes accessed | tf_op | source)
XLA Modules:
  0.0 94.5 jit_solution(6897192849297074317)
XLA Ops:
  1.4 0.9 pad_maximum_fusion.5.refs_0_
  2.3 3.0 %collective-permute-start = (bf16[257,256]{1,0:T(8,128)(2,1)S(1)}, bf16[257,256]{1,0:T(8,128)(2,1)S(1)}, u32[]{:S(2)}, u32[]{:S(2)}) collective-permute-start(bf16[257,256]{1,0:T(8,128)(2,1)S(1)} %pad_maximum_fusion.5.refs_0_), channel_id=1, source_target_pairs={{0,4},{4,0},{1,5},{5,1},{2,6},{6,2},{3,7},{7,3},{8,12},{12,8},{9,1... | collective-permute-start | bytes 394760 | tf_op jit(solution)/shard_map/ppermute | solution.py:275
  5.3 1.0 %constant_dynamic-slice_fusion.6 = (bf16[384,128]{1,0:T(8,128)(2,1)S(1)}, bf16[384,128]{1,0:T(8,128)(2,1)S(1)}) fusion(bf16[3072,128]{1,0:T(8,128)(2,1)} %param.15, s32[]{:T(128)S(6)} %select_n.55, bf16[3072,128]{1,0:T(8,128)(2,1)} %param.14), kind=kLoop, calls=%fused_computation.18 | loop fusion | bytes 393220 | tf_op jit(solution)/shard_map/dynamic_slice | solution.py:291
  6.3 2.7 %collective-permute-start.2 = (bf16[384,256]{1,0:T(8,128)(2,1)S(1)}, bf16[384,256]{1,0:T(8,128)(2,1)S(1)}, u32[]{:S(2)}, u32[]{:S(2)}) collective-permute-start(bf16[384,256]{1,0:T(8,128)(2,1)S(1)} %get-tuple-element.37), channel_id=1, source_target_pairs={{0,2},{1,3},{2,0},{3,1},{4,6},{5,7},{6,4},{7,5},{8,10},{9,11},{10,... | collective-permute-start | bytes 589832 | tf_op jit(solution)/shard_map/ppermute | solution.py:229
  9.6 2.4 %collective-permute-start.18 = (bf16[64,768]{1,0:T(8,128)(2,1)S(1)}, bf16[64,768]{1,0:T(8,128)(2,1)S(1)}, u32[]{:S(2)}, u32[]{:S(2)}) collective-permute-start(bf16[64,768]{1,0:T(8,128)(2,1)S(1)} %get-tuple-element.34), channel_id=1, source_target_pairs={{0,20},{4,16},{8,28},{12,24},{16,4},{20,0},{24,12},{28,8},{1,21},{... | collective-permute-start | bytes 294920 | tf_op jit(solution)/shard_map/ppermute | solution.py:282
  13.2 1.6 %collective-permute-start.1 = (bf16[384,256]{1,0:T(8,128)(2,1)S(1)}, bf16[384,256]{1,0:T(8,128)(2,1)S(1)}, u32[]{:S(2)}, u32[]{:S(2)}) collective-permute-start(bf16[384,256]{1,0:T(8,128)(2,1)S(1)} %get-tuple-element.37), channel_id=1, source_target_pairs={{0,1},{1,0},{2,3},{3,2},{4,5},{5,4},{6,7},{7,6},{8,9},{9,8},{10,11... | collective-permute-start | bytes 589832 | tf_op jit(solution)/shard_map/ppermute | solution.py:229
  14.8 4.0 %attention.1 = (bf16[256,384]{1,0:T(8,128)(2,1)}, f32[256,256]{1,0:T(8,128)}, bf16[256,256]{1,0:T(8,128)(2,1)}) custom-call(s32[4]{0:T(128)} %pad_add_fusion.at_ref, bf16[256,384]{1,0:T(8,128)(2,1)} %bitcast.42, bf16[256,384]{1,0:T(8,128)(2,1)} %bitcast.43, bf16[257,256]{1,0:T(8,128)(2,1)} %copy-done.15, bf16[257,256]{1,0:T(8,128)(2,1)} %copy-done.20), custom_call_target="tpu_custom_call" | custom-call | flops 503316480 | bytes 786432 | tf_op jit(solution)/shard_map/attention/pallas_call | solution.py:84
  20.4 2.5 %collective-permute-start.3 = (bf16[384,256]{1,0:T(8,128)(2,1)S(1)}, bf16[384,256]{1,0:T(8,128)(2,1)S(1)}, u32[]{:S(2)}, u32[]{:S(2)}) collective-permute-start(bf16[384,256]{1,0:T(8,128)(2,1)S(1)} %collective-permute-done.2), channel_id=1, source_target_pairs={{0,1},{1,0},{2,3},{3,2},{4,5},{5,4},{6,7},{7,6},{8,9},{9,8},{10,11... | collective-permute-start | bytes 589832 | tf_op jit(solution)/shard_map/ppermute | solution.py:232
  22.9 2.0 %collective-permute-done.6 = bf16[256,256]{1,0:T(8,128)(2,1)S(1)} collective-permute-done((bf16[256,256]{1,0:T(8,128)(2,1)}, bf16[256,256]{1,0:T(8,128)(2,1)S(1)}, u32[]{:S(2)}, u32[]{:S(2)}) %collective-permute-start.6) | collective-permute-done | bytes 131104 | tf_op jit(solution)/shard_map/ppermute | solution.py:301
  24.9 1.6 %collective-permute-start.9 = (bf16[256,256]{1,0:T(8,128)(2,1)S(1)}, bf16[256,256]{1,0:T(8,128)(2,1)S(1)}, u32[]{:S(2)}, u32[]{:S(2)}) collective-permute-start(bf16[256,256]{1,0:T(8,128)(2,1)S(1)} %add_convert_fusion), channel_id=1, source_target_pairs={{0,20},{4,16},{8,28},{12,24},{16,4},{20,0},{24,12},{28,8},{1,21},{... | collective-permute-start | bytes 393224 | tf_op jit(solution)/shard_map/ppermute | solution.py:257
  27.0 1.6 %collective-permute-start.7 = (bf16[256,256]{1,0:T(8,128)(2,1)S(1)}, bf16[256,256]{1,0:T(8,128)(2,1)S(1)}, u32[]{:S(2)}, u32[]{:S(2)}) collective-permute-start(bf16[256,256]{1,0:T(8,128)(2,1)S(1)} %add_convert_fusion), channel_id=1, source_target_pairs={{0,4},{4,0},{8,12},{12,8},{16,20},{20,16},{24,28},{28,24},{1,5},{5... | collective-permute-start | bytes 393224 | tf_op jit(solution)/shard_map/ppermute | solution.py:257
  28.6 3.3 %collective-permute-start.21 = (bf16[512,384]{1,0:T(8,128)(2,1)S(1)}, bf16[512,384]{1,0:T(8,128)(2,1)S(1)}, u32[]{:S(2)}, u32[]{:S(2)}) collective-permute-start(bf16[512,384]{1,0:T(8,128)(2,1)S(1)} %pad_maximum_fusion.3.refs_0_), channel_id=1, source_target_pairs={{0,2},{1,3},{2,0},{3,1},{4,6},{5,7},{6,4},{7,5},{8,10},{9,11},{10,... | collective-permute-start | bytes 1179656 | tf_op jit(solution)/shard_map/ppermute | solution.py:229
  32.8 2.2 %collective-permute-start.24 = (bf16[512,384]{1,0:T(8,128)(2,1)S(1)}, bf16[512,384]{1,0:T(8,128)(2,1)}, u32[]{:S(2)}, u32[]{:S(2)}) collective-permute-start(bf16[512,384]{1,0:T(8,128)(2,1)S(1)} %pad_maximum_fusion.3.refs_0_), channel_id=1, source_target_pairs={{0,1},{1,0},{2,3},{3,2},{4,5},{5,4},{6,7},{7,6},{8,9},{9,8},{10,11... | collective-permute-start | bytes 1179656 | tf_op jit(solution)/shard_map/ppermute | solution.py:229
  35.0 1.4 %collective-permute-start.20 = (bf16[512,384]{1,0:T(8,128)(2,1)S(1)}, bf16[512,384]{1,0:T(8,128)(2,1)}, u32[]{:S(2)}, u32[]{:S(2)}) collective-permute-start(bf16[512,384]{1,0:T(8,128)(2,1)S(1)} %pad_maximum_fusion.3.refs_0_), channel_id=1, source_target_pairs={{0,0},{1,2},{2,1},{3,3},{4,4},{5,6},{6,5},{7,7},{8,8},{9,10},{10,9... | collective-permute-start | bytes 1179656 | tf_op jit(solution)/shard_map/ppermute | solution.py:229
  36.4 13.2 %collective-permute-done.21.refs_2_ = bf16[512,384]{1,0:T(8,128)(2,1)S(1)} collective-permute-done((bf16[512,384]{1,0:T(8,128)(2,1)S(1)}, bf16[512,384]{1,0:T(8,128)(2,1)S(1)}, u32[]{:S(2)}, u32[]{:S(2)}) %collective-permute-start.21) | collective-permute-done | bytes 393248 | tf_op jit(solution)/shard_map/ppermute | solution.py:229
  50.5 2.0 %collective-permute-done.24.refs_1_ = bf16[512,384]{1,0:T(8,128)(2,1)} collective-permute-done((bf16[512,384]{1,0:T(8,128)(2,1)S(1)}, bf16[512,384]{1,0:T(8,128)(2,1)}, u32[]{:S(2)}, u32[]{:S(2)}) %collective-permute-start.24) | collective-permute-done | bytes 393248 | tf_op jit(solution)/shard_map/ppermute | solution.py:229
  52.5 0.9 collective-permute-start.11
  53.4 1.6 %collective-permute-start.12 = (bf16[256,256]{1,0:T(8,128)(2,1)}, bf16[256,256]{1,0:T(8,128)(2,1)}, u32[]{:S(2)}, u32[]{:S(2)}) collective-permute-start(bf16[256,256]{1,0:T(8,128)(2,1)} %bitcast.20), channel_id=1, source_target_pairs={{0,3},{1,2},{2,1},{3,0},{4,7},{5,6},{6,5},{7,4},{8,11},{9,10},{10,... | collective-permute-start | bytes 393224 | tf_op jit(solution)/shard_map/ppermute | solution.py:310
  54.9 7.4 %collective-permute-start.10 = (bf16[256,256]{1,0:T(8,128)(2,1)}, bf16[256,256]{1,0:T(8,128)(2,1)}, u32[]{:S(2)}, u32[]{:S(2)}) collective-permute-start(bf16[256,256]{1,0:T(8,128)(2,1)} %bitcast.18), channel_id=1, source_target_pairs={{0,1},{1,0},{2,3},{3,2},{4,5},{5,4},{6,7},{7,6},{8,9},{9,8},{10,11... | collective-permute-start | bytes 393224 | tf_op jit(solution)/shard_map/ppermute | solution.py:310
  62.3 2.8 %shard_map.111.refs_4_ = f32[384,256]{1,0:T(8,128)} custom-call(s32[4]{0:T(128)} %pad_add_fusion.at_ref, bf16[512,384]{1,0:T(8,128)(2,1)} %copy-done.3, bf16[512,384]{1,0:T(8,128)(2,1)} %collective-permute-done.24.refs_1_, bf16[512,384]{1,0:T(8,128)(2,1)} %copy-done.6, bf16[4,256,256]{2,1,0:T(8,128)(2,1)} %copy-done, bf16[4,256,256]{2,1,0:T(8,128)(2,1)} %copy-done.2), custom_call_target="tpu_custom_call" | custom-call | flops 301989888 | bytes 393216 | tf_op jit(solution)/shard_map/pallas_call | solution.py:122
  65.2 2.1 %collective-permute-done.22.refs_1_ = bf16[512,384]{1,0:T(8,128)(2,1)} collective-permute-done((bf16[512,384]{1,0:T(8,128)(2,1)S(1)}, bf16[512,384]{1,0:T(8,128)(2,1)}, u32[]{:S(2)}, u32[]{:S(2)}) %collective-permute-start.22) | collective-permute-done | bytes 393248 | tf_op jit(solution)/shard_map/ppermute | solution.py:232
  67.3 2.6 %shard_map.112.refs_0_ = bf16[384,256]{1,0:T(8,128)(2,1)} custom-call(s32[4]{0:T(128)} %pad_add_fusion.at_ref, bf16[512,384]{1,0:T(8,128)(2,1)} %collective-permute-done.20.refs_0_, bf16[512,384]{1,0:T(8,128)(2,1)} %collective-permute-done.22.refs_1_, bf16[4,256,256]{2,1,0:T(8,128)(2,1)} %copy-done, bf16[4,256,256]{2,1,0:T(8,128)(2,1)} %copy-done.2, ...), custom_call_target="tpu_custom_call" | custom-call | flops 201326592 | bytes 393216 | tf_op jit(solution)/shard_map/pallas_call | solution.py:122
  69.9 2.1 %collective-permute-start.27 = (bf16[384,256]{1,0:T(8,128)(2,1)}, bf16[384,256]{1,0:T(8,128)(2,1)S(1)}, u32[]{:S(2)}, u32[]{:S(2)}) collective-permute-start(bf16[384,256]{1,0:T(8,128)(2,1)} %shard_map.112.refs_0_), channel_id=1, source_target_pairs={{0,20},{4,16},{8,28},{12,24},{16,4},{20,0},{24,12},{28,8},{1,21},{... | collective-permute-start | bytes 589832 | tf_op jit(solution)/shard_map/ppermute | solution.py:257
  74.3 2.9 %input_grads.1 = (bf16[64,768]{1,0:T(8,128)(2,1)}, bf16[64,768]{1,0:T(8,128)(2,1)}, bf16[64,768]{1,0:T(8,128)(2,1)}, bf16[64,768]{1,0:T(8,128)(2,1)}) custom-call(bf16[4,384,256]{2,1,0:T(8,128)(2,1)} %copy-done.1, bf16[4,384,256]{2,1,0:T(8,128)(2,1)} %copy-done.4, bf16[256,256]{1,0:T(8,128)(2,1)} %bitcast.32, ...), custom_call_target="tpu_custom_call" | custom-call | flops 402653184 | bytes 1572864 | tf_op jit(solution)/shard_map/input_grads/pallas_call | solution.py:143
  77.2 1.2 %collective-permute-start.13 = (bf16[64,768]{1,0:T(8,128)(2,1)}, bf16[64,768]{1,0:T(8,128)(2,1)S(1)}, u32[]{:S(2)}, u32[]{:S(2)}) collective-permute-start(bf16[64,768]{1,0:T(8,128)(2,1)} %get-tuple-element.19), channel_id=1, source_target_pairs={{0,4},{4,0},{8,12},{12,8},{16,20},{20,16},{24,28},{28,24},{1,5},{5... | collective-permute-start | bytes 294920 | tf_op jit(solution)/shard_map/ppermute | solution.py:327
  79.3 1.6 %collective-permute-start.14 = (bf16[64,768]{1,0:T(8,128)(2,1)}, bf16[64,768]{1,0:T(8,128)(2,1)S(1)}, u32[]{:S(2)}, u32[]{:S(2)}) collective-permute-start(bf16[64,768]{1,0:T(8,128)(2,1)} %get-tuple-element.20), channel_id=1, source_target_pairs={{0,16},{4,20},{8,24},{12,28},{16,0},{20,4},{24,8},{28,12},{1,17},{... | collective-permute-start | bytes 294920 | tf_op jit(solution)/shard_map/ppermute | solution.py:327
  80.9 1.7 %collective-permute-done.13.refs_1_ = bf16[64,768]{1,0:T(8,128)(2,1)S(1)} collective-permute-done((bf16[64,768]{1,0:T(8,128)(2,1)}, bf16[64,768]{1,0:T(8,128)(2,1)S(1)}, u32[]{:S(2)}, u32[]{:S(2)}) %collective-permute-start.13) | collective-permute-done | bytes 98336 | tf_op jit(solution)/shard_map/ppermute | solution.py:327
  82.6 2.1 %collective-permute-start.15 = (bf16[64,768]{1,0:T(8,128)(2,1)}, bf16[64,768]{1,0:T(8,128)(2,1)S(1)}, u32[]{:S(2)}, u32[]{:S(2)}) collective-permute-start(bf16[64,768]{1,0:T(8,128)(2,1)} %get-tuple-element.21), channel_id=1, source_target_pairs={{0,20},{4,16},{8,28},{12,24},{16,4},{20,0},{24,12},{28,8},{1,21},{... | collective-permute-start | bytes 294920 | tf_op jit(solution)/shard_map/ppermute | solution.py:327
  84.8 1.9 %shard_map.113 = (f32[3072,128]{1,0:T(8,128)}, f32[3072,128]{1,0:T(8,128)}) custom-call(s32[4]{0:T(128)} %pad_add_fusion.at_ref, bf16[384,256]{1,0:T(8,128)(2,1)} %shard_map.112.refs_0_, bf16[384,256]{1,0:T(8,128)(2,1)} %copy-done.14), custom_call_target="tpu_custom_call" | custom-call | tf_op jit(solution)/shard_map/pallas_call | solution.py:204
  86.8 1.6 %collective-permute-done.15.refs_3_ = bf16[64,768]{1,0:T(8,128)(2,1)S(1)} collective-permute-done((bf16[64,768]{1,0:T(8,128)(2,1)}, bf16[64,768]{1,0:T(8,128)(2,1)S(1)}, u32[]{:S(2)}, u32[]{:S(2)}) %collective-permute-start.15) | collective-permute-done | bytes 98336 | tf_op jit(solution)/shard_map/ppermute | solution.py:327
  89.0 1.8 %place.1 = bf16[64,3072]{1,0:T(8,128)(2,1)} custom-call(s32[4]{0:T(128)} %pad_add_fusion.at_ref, bf16[64,768]{1,0:T(8,128)(2,1)} %get-tuple-element.18.refs_0_, bf16[64,768]{1,0:T(8,128)(2,1)} %copy-done.17, bf16[64,768]{1,0:T(8,128)(2,1)} %copy-done.18, bf16[64,768]{1,0:T(8,128)(2,1)} %copy-done.19), custom_call_target="tpu_custom_call" | custom-call | tf_op jit(solution)/shard_map/place/pallas_call | solution.py:175
  91.6 2.8 %shard_map.114 = (f32[3072,128]{1,0:T(8,128)}, f32[3072,128]{1,0:T(8,128)}) custom-call(s32[4]{0:T(128)} %pad_add_fusion.at_ref, bf16[384,256]{1,0:T(8,128)(2,1)} %copy-done.10, bf16[384,256]{1,0:T(8,128)(2,1)} %copy-done.9, bf16[384,256]{1,0:T(8,128)(2,1)} %copy-done.8, bf16[384,256]{1,0:T(8,128)(2,1)} %copy-done.13, ...), custom_call_target="tpu_custom_call", output_to_operand_aliasing={{0}: (7, {}), {1}: (8, {})} | custom-call | tf_op jit(solution)/shard_map/pallas_call | solution.py:204
  (95 shorter events, 10.9 us)
Async XLA Ops:
  2.3 10.9 %collective-permute-start = (bf16[257,256]{1,0:T(8,128)(2,1)S(1)}, bf16[257,256]{1,0:T(8,128)(2,1)S(1)}, u32[]{:S(2)}, u32[]{:S(2)}) collective-permute-start(bf16[257,256]{1,0:T(8,128)(2,1)S(1)} %pad_maximum_fusion.5.refs_0_), channel_id=1, source_target_pairs={{0,4},{4,0},{1,5},{5,1},{2,6},{6,2},{3,7},{7,3},{8,12},{12,8},{9,1... | collective-permute-start | bytes 394760 | tf_op jit(solution)/shard_map/ppermute | solution.py:275
  6.3 14.1 %collective-permute-start.2 = (bf16[384,256]{1,0:T(8,128)(2,1)S(1)}, bf16[384,256]{1,0:T(8,128)(2,1)S(1)}, u32[]{:S(2)}, u32[]{:S(2)}) collective-permute-start(bf16[384,256]{1,0:T(8,128)(2,1)S(1)} %get-tuple-element.37), channel_id=1, source_target_pairs={{0,2},{1,3},{2,0},{3,1},{4,6},{5,7},{6,4},{7,5},{8,10},{9,11},{10,... | collective-permute-start | bytes 589832 | tf_op jit(solution)/shard_map/ppermute | solution.py:229
  9.0 9.8 %collective-permute-start.16 = (bf16[64,768]{1,0:T(8,128)(2,1)S(1)}, bf16[64,768]{1,0:T(8,128)(2,1)S(1)}, u32[]{:S(2)}, u32[]{:S(2)}) collective-permute-start(bf16[64,768]{1,0:T(8,128)(2,1)S(1)} %get-tuple-element.33), channel_id=1, source_target_pairs={{0,4},{4,0},{8,12},{12,8},{16,20},{20,16},{24,28},{28,24},{1,5},{5... | collective-permute-start | bytes 294920 | tf_op jit(solution)/shard_map/ppermute | solution.py:282
  9.6 10.0 %collective-permute-start.18 = (bf16[64,768]{1,0:T(8,128)(2,1)S(1)}, bf16[64,768]{1,0:T(8,128)(2,1)S(1)}, u32[]{:S(2)}, u32[]{:S(2)}) collective-permute-start(bf16[64,768]{1,0:T(8,128)(2,1)S(1)} %get-tuple-element.34), channel_id=1, source_target_pairs={{0,20},{4,16},{8,28},{12,24},{16,4},{20,0},{24,12},{28,8},{1,21},{... | collective-permute-start | bytes 294920 | tf_op jit(solution)/shard_map/ppermute | solution.py:282
  12.1 8.2 %collective-permute-start.17 = (bf16[64,768]{1,0:T(8,128)(2,1)S(1)}, bf16[64,768]{1,0:T(8,128)(2,1)S(1)}, u32[]{:S(2)}, u32[]{:S(2)}) collective-permute-start(bf16[64,768]{1,0:T(8,128)(2,1)S(1)} %get-tuple-element.35), channel_id=1, source_target_pairs={{0,16},{4,20},{8,24},{12,28},{16,0},{20,4},{24,8},{28,12},{1,17},{... | collective-permute-start | bytes 294920 | tf_op jit(solution)/shard_map/ppermute | solution.py:282
  13.2 18.8 %collective-permute-start.1 = (bf16[384,256]{1,0:T(8,128)(2,1)S(1)}, bf16[384,256]{1,0:T(8,128)(2,1)S(1)}, u32[]{:S(2)}, u32[]{:S(2)}) collective-permute-start(bf16[384,256]{1,0:T(8,128)(2,1)S(1)} %get-tuple-element.37), channel_id=1, source_target_pairs={{0,1},{1,0},{2,3},{3,2},{4,5},{5,4},{6,7},{7,6},{8,9},{9,8},{10,11... | collective-permute-start | bytes 589832 | tf_op jit(solution)/shard_map/ppermute | solution.py:229
  18.8 8.2 %collective-permute-start.4 = (bf16[384,256]{1,0:T(8,128)(2,1)S(1)}, bf16[384,256]{1,0:T(8,128)(2,1)S(1)}, u32[]{:S(2)}, u32[]{:S(2)}) collective-permute-start(bf16[384,256]{1,0:T(8,128)(2,1)S(1)} %get-tuple-element.37), channel_id=1, source_target_pairs={{0,0},{1,2},{2,1},{3,3},{4,4},{5,6},{6,5},{7,7},{8,8},{9,10},{10,9... | collective-permute-start | bytes 589832 | tf_op jit(solution)/shard_map/ppermute | solution.py:229
  19.6 5.2 %collective-permute-start.6 = (bf16[256,256]{1,0:T(8,128)(2,1)}, bf16[256,256]{1,0:T(8,128)(2,1)S(1)}, u32[]{:S(2)}, u32[]{:S(2)}) collective-permute-start(bf16[256,256]{1,0:T(8,128)(2,1)} %get-tuple-element.17), channel_id=1, source_target_pairs={{0,4},{4,0},{1,5},{5,1},{2,6},{6,2},{3,7},{7,3},{8,12},{12,8},{9,1... | collective-permute-start | bytes 393224 | tf_op jit(solution)/shard_map/ppermute | solution.py:301
  20.3 6.2 %collective-permute-start.19 = (bf16[256,384]{1,0:T(8,128)(2,1)S(1)}, bf16[256,384]{1,0:T(8,128)(2,1)S(1)}, u32[]{:S(2)}, u32[]{:S(2)}) collective-permute-start(bf16[256,384]{1,0:T(8,128)(2,1)S(1)} %get-tuple-element.31), channel_id=1, source_target_pairs={{0,8},{8,0},{16,24},{24,16},{1,9},{9,1},{17,25},{25,17},{2,10},{10... | collective-permute-start | bytes 589832 | tf_op jit(solution)/shard_map/ppermute | solution.py:261
  20.4 8.2 %collective-permute-start.3 = (bf16[384,256]{1,0:T(8,128)(2,1)S(1)}, bf16[384,256]{1,0:T(8,128)(2,1)S(1)}, u32[]{:S(2)}, u32[]{:S(2)}) collective-permute-start(bf16[384,256]{1,0:T(8,128)(2,1)S(1)} %collective-permute-done.2), channel_id=1, source_target_pairs={{0,1},{1,0},{2,3},{3,2},{4,5},{5,4},{6,7},{7,6},{8,9},{9,8},{10,11... | collective-permute-start | bytes 589832 | tf_op jit(solution)/shard_map/ppermute | solution.py:232
  24.9 7.3 %collective-permute-start.9 = (bf16[256,256]{1,0:T(8,128)(2,1)S(1)}, bf16[256,256]{1,0:T(8,128)(2,1)S(1)}, u32[]{:S(2)}, u32[]{:S(2)}) collective-permute-start(bf16[256,256]{1,0:T(8,128)(2,1)S(1)} %add_convert_fusion), channel_id=1, source_target_pairs={{0,20},{4,16},{8,28},{12,24},{16,4},{20,0},{24,12},{28,8},{1,21},{... | collective-permute-start | bytes 393224 | tf_op jit(solution)/shard_map/ppermute | solution.py:257
  26.5 6.1 %collective-permute-start.8 = (bf16[256,256]{1,0:T(8,128)(2,1)S(1)}, bf16[256,256]{1,0:T(8,128)(2,1)S(1)}, u32[]{:S(2)}, u32[]{:S(2)}) collective-permute-start(bf16[256,256]{1,0:T(8,128)(2,1)S(1)} %add_convert_fusion), channel_id=1, source_target_pairs={{0,16},{4,20},{8,24},{12,28},{16,0},{20,4},{24,8},{28,12},{1,17},{... | collective-permute-start | bytes 393224 | tf_op jit(solution)/shard_map/ppermute | solution.py:257
  27.0 5.5 %collective-permute-start.7 = (bf16[256,256]{1,0:T(8,128)(2,1)S(1)}, bf16[256,256]{1,0:T(8,128)(2,1)S(1)}, u32[]{:S(2)}, u32[]{:S(2)}) collective-permute-start(bf16[256,256]{1,0:T(8,128)(2,1)S(1)} %add_convert_fusion), channel_id=1, source_target_pairs={{0,4},{4,0},{8,12},{12,8},{16,20},{20,16},{24,28},{28,24},{1,5},{5... | collective-permute-start | bytes 393224 | tf_op jit(solution)/shard_map/ppermute | solution.py:257
  28.6 21.0 %collective-permute-start.21 = (bf16[512,384]{1,0:T(8,128)(2,1)S(1)}, bf16[512,384]{1,0:T(8,128)(2,1)S(1)}, u32[]{:S(2)}, u32[]{:S(2)}) collective-permute-start(bf16[512,384]{1,0:T(8,128)(2,1)S(1)} %pad_maximum_fusion.3.refs_0_), channel_id=1, source_target_pairs={{0,2},{1,3},{2,0},{3,1},{4,6},{5,7},{6,4},{7,5},{8,10},{9,11},{10,... | collective-permute-start | bytes 1179656 | tf_op jit(solution)/shard_map/ppermute | solution.py:229
  32.1 41.3 %collective-permute-start.5 = (bf16[4,384,256]{2,1,0:T(8,128)(2,1)S(1)}, bf16[4,384,256]{2,1,0:T(8,128)(2,1)S(1)}, u32[]{:S(2)}, u32[]{:S(2)}) collective-permute-start(bf16[4,384,256]{2,1,0:T(8,128)(2,1)S(1)} %pad_maximum_fusion.own_ref), channel_id=1, source_target_pairs={{0,8},{8,0},{16,24},{24,16},{1,9},{9,1},{17,25},{25,17},{2,10},{10... | collective-permute-start | bytes 2359304 | tf_op jit(solution)/shard_map/ppermute | solution.py:261
  32.6 22.3 %collective-permute-start.23 = (bf16[4,256,256]{2,1,0:T(8,128)(2,1)S(1)}, bf16[4,256,256]{2,1,0:T(8,128)(2,1)S(1)}, u32[]{:S(2)}, u32[]{:S(2)}) collective-permute-start(bf16[4,256,256]{2,1,0:T(8,128)(2,1)S(1)} %pad_maximum_fusion.1.refs_3_.refs_2_), channel_id=1, source_target_pairs={{0,8},{8,0},{16,24},{24,16},{1,9},{9,1},{17,25},{25,17},{2,10},{10... | collective-permute-start | bytes 1572872 | tf_op jit(solution)/shard_map/ppermute | solution.py:261
  32.8 19.7 %collective-permute-start.24 = (bf16[512,384]{1,0:T(8,128)(2,1)S(1)}, bf16[512,384]{1,0:T(8,128)(2,1)}, u32[]{:S(2)}, u32[]{:S(2)}) collective-permute-start(bf16[512,384]{1,0:T(8,128)(2,1)S(1)} %pad_maximum_fusion.3.refs_0_), channel_id=1, source_target_pairs={{0,1},{1,0},{2,3},{3,2},{4,5},{5,4},{6,7},{7,6},{8,9},{9,8},{10,11... | collective-permute-start | bytes 1179656 | tf_op jit(solution)/shard_map/ppermute | solution.py:229
  35.0 18.4 %collective-permute-start.20 = (bf16[512,384]{1,0:T(8,128)(2,1)S(1)}, bf16[512,384]{1,0:T(8,128)(2,1)}, u32[]{:S(2)}, u32[]{:S(2)}) collective-permute-start(bf16[512,384]{1,0:T(8,128)(2,1)S(1)} %pad_maximum_fusion.3.refs_0_), channel_id=1, source_target_pairs={{0,0},{1,2},{2,1},{3,3},{4,4},{5,6},{6,5},{7,7},{8,8},{9,10},{10,9... | collective-permute-start | bytes 1179656 | tf_op jit(solution)/shard_map/ppermute | solution.py:229
  49.6 17.7 %collective-permute-start.22 = (bf16[512,384]{1,0:T(8,128)(2,1)S(1)}, bf16[512,384]{1,0:T(8,128)(2,1)}, u32[]{:S(2)}, u32[]{:S(2)}) collective-permute-start(bf16[512,384]{1,0:T(8,128)(2,1)S(1)} %collective-permute-done.21.refs_2_), channel_id=1, source_target_pairs={{0,1},{1,0},{2,3},{3,2},{4,5},{5,4},{6,7},{7,6},{8,9},{9,8},{10,11... | collective-permute-start | bytes 1179656 | tf_op jit(solution)/shard_map/ppermute | solution.py:232
  52.5 19.5 %collective-permute-start.11 = (bf16[256,256]{1,0:T(8,128)(2,1)}, bf16[256,256]{1,0:T(8,128)(2,1)S(1)}, u32[]{:S(2)}, u32[]{:S(2)}) collective-permute-start(bf16[256,256]{1,0:T(8,128)(2,1)} %bitcast.19), channel_id=1, source_target_pairs={{0,2},{1,3},{2,0},{3,1},{4,6},{5,7},{6,4},{7,5},{8,10},{9,11},{10,... | collective-permute-start | bytes 393224 | tf_op jit(solution)/shard_map/ppermute | solution.py:310
  53.4 19.2 %collective-permute-start.12 = (bf16[256,256]{1,0:T(8,128)(2,1)}, bf16[256,256]{1,0:T(8,128)(2,1)}, u32[]{:S(2)}, u32[]{:S(2)}) collective-permute-start(bf16[256,256]{1,0:T(8,128)(2,1)} %bitcast.20), channel_id=1, source_target_pairs={{0,3},{1,2},{2,1},{3,0},{4,7},{5,6},{6,5},{7,4},{8,11},{9,10},{10,... | collective-permute-start | bytes 393224 | tf_op jit(solution)/shard_map/ppermute | solution.py:310
  54.9 18.4 %collective-permute-start.10 = (bf16[256,256]{1,0:T(8,128)(2,1)}, bf16[256,256]{1,0:T(8,128)(2,1)}, u32[]{:S(2)}, u32[]{:S(2)}) collective-permute-start(bf16[256,256]{1,0:T(8,128)(2,1)} %bitcast.18), channel_id=1, source_target_pairs={{0,1},{1,0},{2,3},{3,2},{4,5},{5,4},{6,7},{7,6},{8,9},{9,8},{10,11... | collective-permute-start | bytes 393224 | tf_op jit(solution)/shard_map/ppermute | solution.py:310
  69.9 8.5 %collective-permute-start.27 = (bf16[384,256]{1,0:T(8,128)(2,1)}, bf16[384,256]{1,0:T(8,128)(2,1)S(1)}, u32[]{:S(2)}, u32[]{:S(2)}) collective-permute-start(bf16[384,256]{1,0:T(8,128)(2,1)} %shard_map.112.refs_0_), channel_id=1, source_target_pairs={{0,20},{4,16},{8,28},{12,24},{16,4},{20,0},{24,12},{28,8},{1,21},{... | collective-permute-start | bytes 589832 | tf_op jit(solution)/shard_map/ppermute | solution.py:257
  72.0 6.7 %collective-permute-start.26 = (bf16[384,256]{1,0:T(8,128)(2,1)}, bf16[384,256]{1,0:T(8,128)(2,1)S(1)}, u32[]{:S(2)}, u32[]{:S(2)}) collective-permute-start(bf16[384,256]{1,0:T(8,128)(2,1)} %shard_map.112.refs_0_), channel_id=1, source_target_pairs={{0,16},{4,20},{8,24},{12,28},{16,0},{20,4},{24,8},{28,12},{1,17},{... | collective-permute-start | bytes 589832 | tf_op jit(solution)/shard_map/ppermute | solution.py:257
  72.5 6.6 %collective-permute-start.25 = (bf16[384,256]{1,0:T(8,128)(2,1)}, bf16[384,256]{1,0:T(8,128)(2,1)S(1)}, u32[]{:S(2)}, u32[]{:S(2)}) collective-permute-start(bf16[384,256]{1,0:T(8,128)(2,1)} %shard_map.112.refs_0_), channel_id=1, source_target_pairs={{0,4},{4,0},{8,12},{12,8},{16,20},{20,16},{24,28},{28,24},{1,5},{5... | collective-permute-start | bytes 589832 | tf_op jit(solution)/shard_map/ppermute | solution.py:257
  73.4 5.9 %collective-permute-start.31 = (bf16[384,256]{1,0:T(8,128)(2,1)}, bf16[384,256]{1,0:T(8,128)(2,1)S(1)}, u32[]{:S(2)}, u32[]{:S(2)}) collective-permute-start(bf16[384,256]{1,0:T(8,128)(2,1)} %shard_map.112.refs_0_), channel_id=1, source_target_pairs={{0,8},{8,0},{16,24},{24,16},{1,9},{9,1},{17,25},{25,17},{2,10},{10... | collective-permute-start | bytes 589832 | tf_op jit(solution)/shard_map/ppermute | solution.py:261
  77.2 5.4 %collective-permute-start.13 = (bf16[64,768]{1,0:T(8,128)(2,1)}, bf16[64,768]{1,0:T(8,128)(2,1)S(1)}, u32[]{:S(2)}, u32[]{:S(2)}) collective-permute-start(bf16[64,768]{1,0:T(8,128)(2,1)} %get-tuple-element.19), channel_id=1, source_target_pairs={{0,4},{4,0},{8,12},{12,8},{16,20},{20,16},{24,28},{28,24},{1,5},{5... | collective-permute-start | bytes 294920 | tf_op jit(solution)/shard_map/ppermute | solution.py:327
  78.4 12.4 %collective-permute-start.30 = (bf16[384,256]{1,0:T(8,128)(2,1)S(1)}, bf16[384,256]{1,0:T(8,128)(2,1)S(1)}, u32[]{:S(2)}, u32[]{:S(2)}) collective-permute-start(bf16[384,256]{1,0:T(8,128)(2,1)S(1)} %collective-permute-done.27.refs_2_), channel_id=1, source_target_pairs={{0,8},{8,0},{16,24},{24,16},{1,9},{9,1},{17,25},{25,17},{2,10},{10... | collective-permute-start | bytes 589832 | tf_op jit(solution)/shard_map/ppermute | solution.py:261
  78.8 12.1 %collective-permute-start.29 = (bf16[384,256]{1,0:T(8,128)(2,1)S(1)}, bf16[384,256]{1,0:T(8,128)(2,1)S(1)}, u32[]{:S(2)}, u32[]{:S(2)}) collective-permute-start(bf16[384,256]{1,0:T(8,128)(2,1)S(1)} %collective-permute-done.26.refs_1_), channel_id=1, source_target_pairs={{0,8},{8,0},{16,24},{24,16},{1,9},{9,1},{17,25},{25,17},{2,10},{10... | collective-permute-start | bytes 589832 | tf_op jit(solution)/shard_map/ppermute | solution.py:261
  79.2 11.7 %collective-permute-start.28 = (bf16[384,256]{1,0:T(8,128)(2,1)S(1)}, bf16[384,256]{1,0:T(8,128)(2,1)S(1)}, u32[]{:S(2)}, u32[]{:S(2)}) collective-permute-start(bf16[384,256]{1,0:T(8,128)(2,1)S(1)} %collective-permute-done.25.refs_0_), channel_id=1, source_target_pairs={{0,8},{8,0},{16,24},{24,16},{1,9},{9,1},{17,25},{25,17},{2,10},{10... | collective-permute-start | bytes 589832 | tf_op jit(solution)/shard_map/ppermute | solution.py:261
  79.3 7.4 %collective-permute-start.14 = (bf16[64,768]{1,0:T(8,128)(2,1)}, bf16[64,768]{1,0:T(8,128)(2,1)S(1)}, u32[]{:S(2)}, u32[]{:S(2)}) collective-permute-start(bf16[64,768]{1,0:T(8,128)(2,1)} %get-tuple-element.20), channel_id=1, source_target_pairs={{0,16},{4,20},{8,24},{12,28},{16,0},{20,4},{24,8},{28,12},{1,17},{... | collective-permute-start | bytes 294920 | tf_op jit(solution)/shard_map/ppermute | solution.py:327
  82.6 5.7 %collective-permute-start.15 = (bf16[64,768]{1,0:T(8,128)(2,1)}, bf16[64,768]{1,0:T(8,128)(2,1)S(1)}, u32[]{:S(2)}, u32[]{:S(2)}) collective-permute-start(bf16[64,768]{1,0:T(8,128)(2,1)} %get-tuple-element.21), channel_id=1, source_target_pairs={{0,20},{4,16},{8,28},{12,24},{16,4},{20,0},{24,12},{28,8},{1,21},{... | collective-permute-start | bytes 294920 | tf_op jit(solution)/shard_map/ppermute | solution.py:327
  (21 other events, 173.7 us)
where the time goes:
time: 94.9 us; the launch traced here: 94.5 us
  starting transfers between devices  44.4 us (47%)
  waiting for transfers between devices  23.4 us (25%)
  Pallas kernels  19 us (20%)
  local copies, waits for them, and re-layouts  4.21 us (4%)
  other arithmetic  2.55 us (3%)
    ppermute x6, waiting for transfers between devices, line_exchange(): slots[r] = lax.ppermute(x, 'head', pairs)  15.3 us
    ppermute x6, starting transfers between devices, line_exchange(): slots[r] = lax.ppermute(x, 'head', pairs)  11.9 us
    ppermute x3, starting transfers between devices, shards(): lax.ppermute(piece, 'head', swap_pairs(heads, r))  9.82 us
    ppermute x6, starting transfers between devices, cell_gather(): got[o] = lax.ppermute(x, both, swap_pairs(plane, member(o, 0)))  7.11 us
    pallas_call x2, Pallas kernels, grads(): pl.pallas_call(functools.partial(grads_kernel, tuple(slots), sub, len(xs)...  5.4 us
    ppermute x3, starting transfers between devices, shards(): parts[o] = lax.ppermute(parts[o], both, swap_pairs(plane, member(o, 0)))  4.97 us
    pallas_call x2, Pallas kernels, spread(): pl.pallas_call(functools.partial(spread_kernel, tuple((item[:2] for item...  4.8 us
    pallas_call x1, Pallas kernels, attention(): pl.pallas_call(functools.partial(attention_kernel, blocks, width // HD),...  4.03 us
  transfers between devices with their start and end apart: 32, of which 9 were waited for; matrix products, arithmetic and copies ran while one was open for 3% of the time, Pallas kernels for 17%

commit v1 on v0

--- a/solution.py
+++ b/solution.py
@@ -94,41 +94,6 @@
     )(at, q, g, *packs)
 
 
-def grads_kernel(slots, sub, fars, at_ref, *refs):
-    count = len(slots)
-    x_refs, refs = refs[: count + fars], refs[count + fars :]
-    own_ref, other_ref, *add_refs, out_ref = refs
-    z = at_ref[0]
-    half = own_ref.shape[0] * sub
-    total = jnp.zeros(out_ref.shape, F32)
-    for ref in add_refs:
-        total += ref[...]
-    for i, r in enumerate(slots):
-        x = x_refs[i][...]
-        if fars and i == count - 1:
-            x = jnp.where((z == 0) | (z == r), x_refs[count][...], x)
-        start = pl.multiple_of((z ^ r) * sub, sub)
-        pieces = [
-            ref[:, pl.ds(start, sub), :].reshape(half, out_ref.shape[1])
-            for ref in (own_ref, other_ref)
-        ]
-        total += dot(x, jnp.concatenate(pieces, axis=0), 0, 0)
-    out_ref[...] = total.astype(out_ref.dtype)
-
-
-def grads(at, xs, slots, own, other, adds, dtype):
-    sub = xs[0].shape[0] // (2 * own.shape[0])
-    size, width = xs[0].shape[1], own.shape[2]
-    return pl.pallas_call(
-        functools.partial(grads_kernel, tuple(slots), sub, len(xs) - len(slots)),
-        out_shape=jax.ShapeDtypeStruct((size, width), dtype),
-        in_specs=[SMEM] + [VMEM] * (len(xs) + 2 + len(adds)),
-        cost_estimate=pl.CostEstimate(
-            flops=2 * len(xs) * xs[0].size * width, transcendentals=0, bytes_accessed=2 * xs[0].size
-        ),
-    )(at, *xs, own, other, *adds)
-
-
 def input_kernel(heads, own_ref, other_ref, *refs):
     row_refs, out_refs = refs[:heads], refs[heads:]
     size, sub = own_ref.shape[1], out_refs[0].shape[0]
@@ -151,64 +116,57 @@
     )(w_own, w_other, *rows)
 
 
-def place_kernel(cells, at_ref, *refs):
-    size = refs[0].shape[1] // 2
-    out_ref = refs[cells]
-    for o in range(cells):
-        base = (at_ref[1] ^ o) * 2
-        for j, core in ((0, at_ref[2]), (1, 1 - at_ref[2])):
-            start = (base + core) * size
-            if size % HD == 0:
-                start = pl.multiple_of(start, HD)
-            out_ref[:, pl.ds(start, size)] = refs[o][:, j * size : (j + 1) * size]
-
-
 def place(at, pieces):
     cells, (sub, slab) = len(pieces), pieces[0].shape
-    if slab % (2 * HD):
-        out = jnp.zeros((sub, slab * cells), BF16)
-        for o, piece in enumerate(pieces):
-            for j, half in enumerate(jnp.split(piece, 2, axis=1)):
-                start = ((at[1] ^ o) * 2 + (at[2] ^ j)) * (slab // 2)
-                out = lax.dynamic_update_slice_in_dim(out, half, start, 1)
-        return out
-    return pl.pallas_call(
-        functools.partial(place_kernel, cells),
-        out_shape=jax.ShapeDtypeStruct((sub, slab * cells), BF16),
-        in_specs=[SMEM] + [VMEM] * cells,
-        name="place",
-    )(at, *pieces)
-
-
-def spread_kernel(places, at_ref, *refs):
-    pieces, (key_ref, value_ref, *bufs, sems) = refs[: len(places)], refs[-5:]
+    out = jnp.zeros((sub, slab * cells), BF16)
+    for o, piece in enumerate(pieces):
+        for j, half in enumerate(jnp.split(piece, 2, axis=1)):
+            start = ((at[1] ^ o) * 2 + (at[2] ^ j)) * (slab // 2)
+            out = lax.dynamic_update_slice_in_dim(out, half, start, 1)
+    return out
+
+
+def spread_kernel(places, parts, at_ref, *refs):
+    pieces, refs = refs[: len(places)], refs[len(places) :]
+    part_refs, (key_ref, value_ref, *placed, key_buf, value_buf, sems) = refs[:parts], refs[-6:]
+    if not parts:
+        key_ref, value_ref = refs[-5:-3]
     size = pieces[0].shape[0]
     waits = []
     for i, ((o, flip), piece) in enumerate(zip(places, pieces)):
         base = pl.multiple_of(((at_ref[1] ^ o) * 2 + (at_ref[2] ^ flip)) * size, 8)
-        for n, (out_ref, buf) in enumerate(zip((key_ref, value_ref), bufs)):
+        for n, (out_ref, buf) in enumerate(((key_ref, key_buf), (value_ref, value_buf))):
             buf[i] = piece[:, n * HD : (n + 1) * HD].astype(F32)
             copy = pltpu.make_async_copy(
                 buf.at[i], out_ref.at[pl.ds(base, size), :], sems.at[n, i]
             )
             copy.start()
             waits.append(copy)
+    for o, ref in enumerate(part_refs):
+        for j in range(2):
+            start = pl.multiple_of(((at_ref[1] ^ o) * 2 + (at_ref[2] ^ j)) * size, HD)
+            placed[0][:, pl.ds(start, size)] = ref[:, j * size : (j + 1) * size]
     for copy in waits:
         copy.wait()
 
 
-def spread(at, total, items, outs=()):
+def spread(at, total, items, outs=(), parts=()):
     count, size = len(items), items[0][2].shape[0]
-    shape = jax.ShapeDtypeStruct((total, HD), F32)
+    shapes = [jax.ShapeDtypeStruct((total, HD), F32)] * 2
     buf = pltpu.VMEM((count, size, HD), F32)
+    specs = [ANY, ANY]
+    if parts:
+        shapes.append(jax.ShapeDtypeStruct((parts[0].shape[0], total), BF16))
+        specs.append(VMEM)
+    first = 1 + count + len(parts)
     return pl.pallas_call(
-        functools.partial(spread_kernel, tuple(item[:2] for item in items)),
-        out_shape=[shape, shape],
-        in_specs=[SMEM] + [VMEM] * count + [ANY] * len(outs),
-        out_specs=[ANY, ANY],
+        functools.partial(spread_kernel, tuple(item[:2] for item in items), len(parts)),
+        out_shape=shapes,
+        in_specs=[SMEM] + [VMEM] * (count + len(parts)) + [ANY] * len(outs),
+        out_specs=specs,
         scratch_shapes=[buf, buf, pltpu.SemaphoreType.DMA((2, count))],
-        input_output_aliases={1 + count + n: n for n in range(len(outs))},
-    )(at, *[item[2] for item in items], *outs)
+        input_output_aliases={first + n: n for n in range(len(outs))},
+    )(at, *[item[2] for item in items], *parts, *outs)
 
 
 def swap_pairs(n, m):
@@ -295,37 +253,44 @@
     at = scalars(z, cell, core, s)
 
     query_grad, own_terms, *prev_terms = attention(at, queries[0], out_grad[0], packs)
-    dkv = own_terms
+    terms = []
     for r in range(1, seq):
         pairs = [(i, (i - r) % seq) for i in range(seq)]
-        dkv = dkv + lax.ppermute(prev_terms[r - 1], "seq", pairs).astype(F32)
-    dkv = dkv.astype(BF16)
+        terms.append(lax.ppermute(prev_terms[r - 1], "seq", pairs))
+    dkv = sum([t.astype(F32) for t in terms], own_terms).astype(BF16)
 
     dkv_own = jnp.stack(cell_gather(dkv))
     dkv_other = core_swap(dkv_own)
-    head_rows = []
+    head_rows, both_rows = [], []
     for r in range(heads):
-        piece = lax.dynamic_slice_in_dim(dkv_own, (z ^ r) * sub, sub, 1)
-        piece = piece.reshape(cells * sub, 2 * HD)
-        head_rows.append(lax.ppermute(piece, "head", swap_pairs(heads, r)) if r else piece)
-
-    slots = list(range(heads))
-    part = grads(at, x_slots[: heads - 1], slots[:-1], dkv_own, dkv_other, [], F32)
-    grad = grads(at, x_slots[heads - 1 :], slots[-1:], dkv_own, dkv_other, [part], BF16)
+        own, other = (
+            lax.dynamic_slice_in_dim(t, (z ^ r) * sub, sub, 1).reshape(cells * sub, 2 * HD)
+            for t in (dkv_own, dkv_other)
+        )
+        head_rows.append(lax.ppermute(own, "head", swap_pairs(heads, r)) if r else own)
+        both_rows.append(jnp.concatenate([own, other], axis=0))
+    outer = (z == 0) | (z == heads - 1)
+
+    if len(x_slots) > heads:
+        x_slots = x_slots[: heads - 1] + [jnp.where(outer, x_slots[heads], x_slots[heads - 1])]
+    grad = sum(dot(x_slots[r], both_rows[r], 0, 0) for r in range(heads)).astype(BF16)
     grad_own = cell_gather(grad)
     items = [(o, 0, g) for o, g in enumerate(grad_own)]
     items += [(o, 1, core_swap(g)) for o, g in enumerate(grad_own)]
     outs = spread(at, d_model, [i for i in items if i[0] == 0])
-    grad_keyproj, grad_valueproj = spread(at, d_model, [i for i in items if i[0]], outs)
 
     if len(w_slots) > heads:
-        outer = (z == 0) | (z == heads - 1)
         w_slots = w_slots[: heads - 1] + [jnp.where(outer, w_slots[heads], w_slots[heads - 1])]
     w_own = jnp.stack(w_slots)
     parts = list(input_parts(w_own, core_swap(w_own), head_rows, cells))
     for o in far_first(cells):
         parts[o] = lax.ppermute(parts[o], both, swap_pairs(plane, member(o, 0)))
-    input_grad = place(at, parts)
+    rest = [i for i in items if i[0]]
+    if size % HD:
+        grad_keyproj, grad_valueproj = spread(at, d_model, rest, outs)
+        input_grad = place(at, parts)
+    else:
+        grad_keyproj, grad_valueproj, input_grad = spread(at, d_model, rest, outs, parts)
     return query_grad[None], input_grad[None], grad_keyproj, grad_valueproj
 
 

time: 94.9 us -> 97.8 us (1.031)
  Pallas kernels: 19 us -> 12.6 us
  waiting for transfers between devices: 23.4 us -> 27.8 us
  starting transfers between devices: 44.4 us -> 47.1 us
  matrix products: 0 us -> 1.27 us
    ppermute x2, waiting for transfers between devices: 2.14 us -> 11 us  [line_exchange(): out.append(lax.ppermute(slots[2], 'head', swap_pairs(n, 1)))]
    pallas_call x3 -> x0, Pallas kernels: 7.22 us -> none  [the longest x2 5.4 us: grads(): pl.pallas_call(functools.partial(grads_kernel, tuple(slots), sub, len(xs)...]
    ppermute x2, starting transfers between devices: 2.51 us -> 6.29 us  [line_exchange(): out.append(lax.ppermute(slots[2], 'head', swap_pairs(n, 1)))]
    ppermute x6, waiting for transfers between devices: 15.3 us -> 12.1 us  [line_exchange(): slots[r] = lax.ppermute(x, 'head', pairs)]
    dot_general x0 -> x4, matrix products: none -> 1.27 us  [dot(): lax.dot_general(a, b, (((ca,), (cb,)), ((), ())), preferred_element_type=...]
    dynamic_slice x1, local copies, waits for them, and re-layouts: 0.04 us -> 1.06 us  [shards(): piece = lax.dynamic_slice_in_dim(x, (cell ^ o) * 2 * size, 2 * size, 1)]
    unnamed x42 -> x40, local copies, waits for them, and re-layouts: 2.32 us -> 2.96 us
  transfers between devices with their start and end apart: 32 -> 32, of which waited for: 9 -> 7; matrix products, arithmetic and copies ran while one was open for 3% -> 4% of each run, Pallas kernels for 17% -> 9%
where the time goes in v1:
time: 97.8 us; the launch traced here: 97.4 us
  starting transfers between devices  47.1 us (48%)
  waiting for transfers between devices  27.8 us (28%)
  Pallas kernels  12.6 us (13%)
  local copies, waits for them, and re-layouts  5.1 us (5%)
  other arithmetic  2.47 us (3%)
  matrix products  1.27 us (1%)
  between operations  1.09 us (1%)
    ppermute x6, waiting for transfers between devices, line_exchange(): slots[r] = lax.ppermute(x, 'head', pairs)  12.1 us
    ppermute x2, waiting for transfers between devices, line_exchange(): out.append(lax.ppermute(slots[2], 'head', swap_pairs(n, 1)))  11 us
    ppermute x6, starting transfers between devices, line_exchange(): slots[r] = lax.ppermute(x, 'head', pairs)  11 us
    ppermute x3, starting transfers between devices, shards(): lax.ppermute(own, 'head', swap_pairs(heads, r))  9.61 us
    ppermute x6, starting transfers between devices, cell_gather(): got[o] = lax.ppermute(x, both, swap_pairs(plane, member(o, 0)))  7.11 us
    ppermute x2, starting transfers between devices, line_exchange(): out.append(lax.ppermute(slots[2], 'head', swap_pairs(n, 1)))  6.29 us
    pallas_call x2, Pallas kernels, spread(): pl.pallas_call(functools.partial(spread_kernel, tuple((item[:2] for item...  5.66 us
    ppermute x3, starting transfers between devices, shards(): parts[o] = lax.ppermute(parts[o], both, swap_pairs(plane, member(o, 0)))  5.43 us
  transfers between devices with their start and end apart: 32, of which 7 were waited for; matrix products, arithmetic and copies ran while one was open for 4% of the time, Pallas kernels for 9%

profile of v1, /device:TPU:0, one launch (start us, length us, event | category | flops | bytes accessed | tf_op | source)
XLA Modules:
  0.0 97.4 jit_solution(5775904510093796546)
XLA Ops:
  0.6 0.7 convert_element_type.12
  1.3 0.9 pad_maximum_fusion.5.refs_0_
  2.2 3.0 %collective-permute-start = (bf16[257,256]{1,0:T(8,128)(2,1)S(1)}, bf16[257,256]{1,0:T(8,128)(2,1)S(1)}, u32[]{:S(2)}, u32[]{:S(2)}) collective-permute-start(bf16[257,256]{1,0:T(8,128)(2,1)S(1)} %pad_maximum_fusion.5.refs_0_), channel_id=1, source_target_pairs={{0,4},{4,0},{1,5},{5,1},{2,6},{6,2},{3,7},{7,3},{8,12},{12,8},{9,1... | collective-permute-start | bytes 394760 | tf_op jit(solution)/shard_map/ppermute | solution.py:233
  5.2 1.1 %dynamic-slice_bitcast_fusion.3 = (bf16[64,768]{1,0:T(8,128)(2,1)S(1)}, bf16[64,768]{1,0:T(8,128)(2,1)S(1)}, bf16[64,768]{1,0:T(8,128)(2,1)S(1)}, bf16[64,768]{1,0:T(8,128)(2,1)S(1)}) fusion(bf16[1,64,3072]{2,1,0:T(8,128)(2,1)} %param.13, s32[]{:T(128)S(6)} %select_n.67, s32[]{:T(128)S(6)} %select_n.68, s32[]{:T(128)S(6)} %select_n.70, s32[]{:T(128)S(6)} %select_n.69), kind=kLoop, calls=%fused_computation.31 | loop fusion | bytes 786448 | tf_op jit(solution)/shard_map/dynamic_slice | solution.py:238
  6.5 2.9 %collective-permute-start.3 = (bf16[64,768]{1,0:T(8,128)(2,1)S(1)}, bf16[64,768]{1,0:T(8,128)(2,1)S(1)}, u32[]{:S(2)}, u32[]{:S(2)}) collective-permute-start(bf16[64,768]{1,0:T(8,128)(2,1)S(1)} %get-tuple-element.40), channel_id=1, source_target_pairs={{0,20},{4,16},{8,28},{12,24},{16,4},{20,0},{24,12},{28,8},{1,21},{... | collective-permute-start | bytes 294920 | tf_op jit(solution)/shard_map/ppermute | solution.py:240
  10.4 1.0 constant_dynamic-slice_fusion
  12.1 4.0 %attention.1 = (bf16[256,384]{1,0:T(8,128)(2,1)}, f32[256,256]{1,0:T(8,128)}, bf16[256,256]{1,0:T(8,128)(2,1)}) custom-call(s32[4]{0:T(128)} %pad_add_fusion.at_ref, bf16[256,384]{1,0:T(8,128)(2,1)} %bitcast.59, bf16[256,384]{1,0:T(8,128)(2,1)} %bitcast.60, bf16[257,256]{1,0:T(8,128)(2,1)} %copy-done.12, bf16[257,256]{1,0:T(8,128)(2,1)} %copy-done.19), custom_call_target="tpu_custom_call" | custom-call | flops 503316480 | bytes 786432 | tf_op jit(solution)/shard_map/attention/pallas_call | solution.py:84
  16.4 2.9 %collective-permute-start.21 = (bf16[384,256]{1,0:T(8,128)(2,1)S(1)}, bf16[384,256]{1,0:T(8,128)(2,1)S(1)}, u32[]{:S(2)}, u32[]{:S(2)}) collective-permute-start(bf16[384,256]{1,0:T(8,128)(2,1)S(1)} %get-tuple-element.43), channel_id=1, source_target_pairs={{0,2},{1,3},{2,0},{3,1},{4,6},{5,7},{6,4},{7,5},{8,10},{9,11},{10,... | collective-permute-start | bytes 589832 | tf_op jit(solution)/shard_map/ppermute | solution.py:187
  19.4 1.9 %collective-permute-done.5 = bf16[256,256]{1,0:T(8,128)(2,1)S(1)} collective-permute-done((bf16[256,256]{1,0:T(8,128)(2,1)}, bf16[256,256]{1,0:T(8,128)(2,1)S(1)}, u32[]{:S(2)}, u32[]{:S(2)}) %collective-permute-start.5) | collective-permute-done | bytes 131104 | tf_op jit(solution)/shard_map/ppermute | solution.py:259
  21.3 1.6 %collective-permute-start.8 = (bf16[256,256]{1,0:T(8,128)(2,1)S(1)}, bf16[256,256]{1,0:T(8,128)(2,1)S(1)}, u32[]{:S(2)}, u32[]{:S(2)}) collective-permute-start(bf16[256,256]{1,0:T(8,128)(2,1)S(1)} %add_convert_fusion), channel_id=1, source_target_pairs={{0,20},{4,16},{8,28},{12,24},{16,4},{20,0},{24,12},{28,8},{1,21},{... | collective-permute-start | bytes 393224 | tf_op jit(solution)/shard_map/ppermute | solution.py:215
  23.1 1.7 %collective-permute-start.6 = (bf16[256,256]{1,0:T(8,128)(2,1)S(1)}, bf16[256,256]{1,0:T(8,128)(2,1)S(1)}, u32[]{:S(2)}, u32[]{:S(2)}) collective-permute-start(bf16[256,256]{1,0:T(8,128)(2,1)S(1)} %add_convert_fusion), channel_id=1, source_target_pairs={{0,4},{4,0},{8,12},{12,8},{16,20},{20,16},{24,28},{28,24},{1,5},{5... | collective-permute-start | bytes 393224 | tf_op jit(solution)/shard_map/ppermute | solution.py:215
  25.0 2.0 %collective-permute-done.21 = bf16[384,256]{1,0:T(8,128)(2,1)S(1)} collective-permute-done((bf16[384,256]{1,0:T(8,128)(2,1)S(1)}, bf16[384,256]{1,0:T(8,128)(2,1)S(1)}, u32[]{:S(2)}, u32[]{:S(2)}) %collective-permute-start.21) | collective-permute-done | bytes 196640 | tf_op jit(solution)/shard_map/ppermute | solution.py:187
  27.0 0.7 collective-permute-start.20
  28.7 5.0 %collective-permute-start.22 = (bf16[384,256]{1,0:T(8,128)(2,1)S(1)}, bf16[384,256]{1,0:T(8,128)(2,1)S(1)}, u32[]{:S(2)}, u32[]{:S(2)}) collective-permute-start(bf16[384,256]{1,0:T(8,128)(2,1)S(1)} %collective-permute-done.21), channel_id=1, source_target_pairs={{0,1},{1,0},{2,3},{3,2},{4,5},{5,4},{6,7},{7,6},{8,9},{9,8},{10,11... | collective-permute-start | bytes 589832 | tf_op jit(solution)/shard_map/ppermute | solution.py:190
  34.0 6.0 %collective-permute-start.10 = (bf16[512,384]{1,0:T(8,128)(2,1)S(1)}, bf16[512,384]{1,0:T(8,128)(2,1)S(1)}, u32[]{:S(2)}, u32[]{:S(2)}) collective-permute-start(bf16[512,384]{1,0:T(8,128)(2,1)S(1)} %pad_maximum_fusion.3), channel_id=1, source_target_pairs={{0,1},{1,0},{2,3},{3,2},{4,5},{5,4},{6,7},{7,6},{8,9},{9,8},{10,11... | collective-permute-start | bytes 1179656 | tf_op jit(solution)/shard_map/ppermute | solution.py:187
  40.0 0.7 collective-permute-start.13
  41.0 4.3 %collective-permute-start.26 = (bf16[256,256]{1,0:T(8,128)(2,1)S(1)}, bf16[256,256]{1,0:T(8,128)(2,1)S(1)}, u32[]{:S(2)}, u32[]{:S(2)}) collective-permute-start(bf16[256,256]{1,0:T(8,128)(2,1)S(1)} %bitcast.51), channel_id=1, source_target_pairs={{0,2},{1,3},{2,0},{3,1},{4,6},{5,7},{6,4},{7,5},{8,10},{9,11},{10,... | collective-permute-start | bytes 393224 | tf_op jit(solution)/shard_map/ppermute | solution.py:270
  45.3 10.0 %collective-permute-done.11 = bf16[512,384]{1,0:T(8,128)(2,1)S(1)} collective-permute-done((bf16[512,384]{1,0:T(8,128)(2,1)S(1)}, bf16[512,384]{1,0:T(8,128)(2,1)S(1)}, u32[]{:S(2)}, u32[]{:S(2)}) %collective-permute-start.11) | collective-permute-done | bytes 393248 | tf_op jit(solution)/shard_map/ppermute | solution.py:187
  55.3 1.5 %collective-permute-start.25 = (bf16[256,256]{1,0:T(8,128)(2,1)S(1)}, bf16[256,256]{1,0:T(8,128)(2,1)S(1)}, u32[]{:S(2)}, u32[]{:S(2)}) collective-permute-start(bf16[256,256]{1,0:T(8,128)(2,1)S(1)} %bitcast.47), channel_id=1, source_target_pairs={{0,1},{1,0},{2,3},{3,2},{4,5},{5,4},{6,7},{7,6},{8,9},{9,8},{10,11... | collective-permute-start | bytes 393224 | tf_op jit(solution)/shard_map/ppermute | solution.py:270
  57.1 1.3 %collective-permute-start.12 = (bf16[512,384]{1,0:T(8,128)(2,1)S(1)}, bf16[512,384]{1,0:T(8,128)(2,1)S(1)}, u32[]{:S(2)}, u32[]{:S(2)}) collective-permute-start(bf16[512,384]{1,0:T(8,128)(2,1)S(1)} %collective-permute-done.11), channel_id=1, source_target_pairs={{0,1},{1,0},{2,3},{3,2},{4,5},{5,4},{6,7},{7,6},{8,9},{9,8},{10,11... | collective-permute-start | bytes 1179656 | tf_op jit(solution)/shard_map/ppermute | solution.py:190
  59.0 3.9 %collective-permute-start.27 = (bf16[256,256]{1,0:T(8,128)(2,1)S(1)}, bf16[256,256]{1,0:T(8,128)(2,1)S(1)}, u32[]{:S(2)}, u32[]{:S(2)}) collective-permute-start(bf16[256,256]{1,0:T(8,128)(2,1)S(1)} %bitcast.49), channel_id=1, source_target_pairs={{0,3},{1,2},{2,1},{3,0},{4,7},{5,6},{6,5},{7,4},{8,11},{9,10},{10,... | collective-permute-start | bytes 393224 | tf_op jit(solution)/shard_map/ppermute | solution.py:270
  62.9 11.0 %collective-permute-done.12 = bf16[512,384]{1,0:T(8,128)(2,1)S(1)} collective-permute-done((bf16[512,384]{1,0:T(8,128)(2,1)S(1)}, bf16[512,384]{1,0:T(8,128)(2,1)S(1)}, u32[]{:S(2)}, u32[]{:S(2)}) %collective-permute-start.12) | collective-permute-done | bytes 393248 | tf_op jit(solution)/shard_map/ppermute | solution.py:190
  74.2 2.5 %collective-permute-start.16 = (bf16[384,256]{1,0:T(8,128)(2,1)S(1)}, bf16[384,256]{1,0:T(8,128)(2,1)S(1)}, u32[]{:S(2)}, u32[]{:S(2)}) collective-permute-start(bf16[384,256]{1,0:T(8,128)(2,1)S(1)} %fusion.1.refs_0_), channel_id=1, source_target_pairs={{0,20},{4,16},{8,28},{12,24},{16,4},{20,0},{24,12},{28,8},{1,21},{... | collective-permute-start | bytes 589832 | tf_op jit(solution)/shard_map/ppermute | solution.py:215
  78.5 0.9 copy-done.2
  79.3 2.9 %input_grads.1 = (bf16[64,768]{1,0:T(8,128)(2,1)}, bf16[64,768]{1,0:T(8,128)(2,1)}, bf16[64,768]{1,0:T(8,128)(2,1)}, bf16[64,768]{1,0:T(8,128)(2,1)}) custom-call(bf16[4,384,256]{2,1,0:T(8,128)(2,1)} %copy-done, bf16[4,384,256]{2,1,0:T(8,128)(2,1)} %copy-done.2, bf16[256,256]{1,0:T(8,128)(2,1)} %bitcast.39, bf16[256,256]{1,0:T(8,128)(2,1)} %copy-done.14, ...), custom_call_target="tpu_custom_call" | custom-call | flops 402653184 | bytes 1572864 | tf_op jit(solution)/shard_map/input_grads/pallas_call | solution.py:108
  82.3 1.5 %collective-permute-start.28 = (bf16[64,768]{1,0:T(8,128)(2,1)}, bf16[64,768]{1,0:T(8,128)(2,1)S(1)}, u32[]{:S(2)}, u32[]{:S(2)}) collective-permute-start(bf16[64,768]{1,0:T(8,128)(2,1)} %get-tuple-element.20), channel_id=1, source_target_pairs={{0,4},{4,0},{8,12},{12,8},{16,20},{20,16},{24,28},{28,24},{1,5},{5... | collective-permute-start | bytes 294920 | tf_op jit(solution)/shard_map/ppermute | solution.py:287
  84.4 1.5 %collective-permute-start.29 = (bf16[64,768]{1,0:T(8,128)(2,1)}, bf16[64,768]{1,0:T(8,128)(2,1)S(1)}, u32[]{:S(2)}, u32[]{:S(2)}) collective-permute-start(bf16[64,768]{1,0:T(8,128)(2,1)} %get-tuple-element.21), channel_id=1, source_target_pairs={{0,16},{4,20},{8,24},{12,28},{16,0},{20,4},{24,8},{28,12},{1,17},{... | collective-permute-start | bytes 294920 | tf_op jit(solution)/shard_map/ppermute | solution.py:287
  85.9 1.2 %collective-permute-done.28.refs_7_ = bf16[64,768]{1,0:T(8,128)(2,1)S(1)} collective-permute-done((bf16[64,768]{1,0:T(8,128)(2,1)}, bf16[64,768]{1,0:T(8,128)(2,1)S(1)}, u32[]{:S(2)}, u32[]{:S(2)}) %collective-permute-start.28) | collective-permute-done | bytes 98336 | tf_op jit(solution)/shard_map/ppermute | solution.py:287
  87.1 2.4 %collective-permute-start.30 = (bf16[64,768]{1,0:T(8,128)(2,1)}, bf16[64,768]{1,0:T(8,128)(2,1)S(1)}, u32[]{:S(2)}, u32[]{:S(2)}) collective-permute-start(bf16[64,768]{1,0:T(8,128)(2,1)} %get-tuple-element.22), channel_id=1, source_target_pairs={{0,20},{4,16},{8,28},{12,24},{16,4},{20,0},{24,12},{28,8},{1,21},{... | collective-permute-start | bytes 294920 | tf_op jit(solution)/shard_map/ppermute | solution.py:287
  89.5 1.9 %shard_map.111 = (f32[3072,128]{1,0:T(8,128)}, f32[3072,128]{1,0:T(8,128)}) custom-call(s32[4]{0:T(128)} %pad_add_fusion.at_ref, bf16[384,256]{1,0:T(8,128)(2,1)} %copy-done.10, bf16[384,256]{1,0:T(8,128)(2,1)} %copy-done.11), custom_call_target="tpu_custom_call" | custom-call | tf_op jit(solution)/shard_map/pallas_call | solution.py:162
  91.5 1.3 %collective-permute-done.30.refs_9_ = bf16[64,768]{1,0:T(8,128)(2,1)S(1)} collective-permute-done((bf16[64,768]{1,0:T(8,128)(2,1)}, bf16[64,768]{1,0:T(8,128)(2,1)S(1)}, u32[]{:S(2)}, u32[]{:S(2)}) %collective-permute-start.30) | collective-permute-done | bytes 98336 | tf_op jit(solution)/shard_map/ppermute | solution.py:287
  93.7 3.7 %shard_map.112 = (f32[3072,128]{1,0:T(8,128)}, f32[3072,128]{1,0:T(8,128)}, bf16[64,3072]{1,0:T(8,128)(2,1)}) custom-call(s32[4]{0:T(128)} %pad_add_fusion.at_ref, bf16[384,256]{1,0:T(8,128)(2,1)} %copy-done.6, bf16[384,256]{1,0:T(8,128)(2,1)} %copy-done.5, bf16[384,256]{1,0:T(8,128)(2,1)} %copy-done.4, ...), custom_call_target="tpu_custom_call", output_to_operand_aliasing={{0}: (11, {}), {1}: (12, {})} | custom-call | tf_op jit(solution)/shard_map/pallas_call | solution.py:162
  (95 shorter events, 8.4 us)
Async XLA Ops:
  2.2 9.2 %collective-permute-start = (bf16[257,256]{1,0:T(8,128)(2,1)S(1)}, bf16[257,256]{1,0:T(8,128)(2,1)S(1)}, u32[]{:S(2)}, u32[]{:S(2)}) collective-permute-start(bf16[257,256]{1,0:T(8,128)(2,1)S(1)} %pad_maximum_fusion.5.refs_0_), channel_id=1, source_target_pairs={{0,4},{4,0},{1,5},{5,1},{2,6},{6,2},{3,7},{7,3},{8,12},{12,8},{9,1... | collective-permute-start | bytes 394760 | tf_op jit(solution)/shard_map/ppermute | solution.py:233
  6.3 13.0 %collective-permute-start.1 = (bf16[64,768]{1,0:T(8,128)(2,1)S(1)}, bf16[64,768]{1,0:T(8,128)(2,1)S(1)}, u32[]{:S(2)}, u32[]{:S(2)}) collective-permute-start(bf16[64,768]{1,0:T(8,128)(2,1)S(1)} %get-tuple-element.39), channel_id=1, source_target_pairs={{0,4},{4,0},{8,12},{12,8},{16,20},{20,16},{24,28},{28,24},{1,5},{5... | collective-permute-start | bytes 294920 | tf_op jit(solution)/shard_map/ppermute | solution.py:240
  6.5 12.9 %collective-permute-start.3 = (bf16[64,768]{1,0:T(8,128)(2,1)S(1)}, bf16[64,768]{1,0:T(8,128)(2,1)S(1)}, u32[]{:S(2)}, u32[]{:S(2)}) collective-permute-start(bf16[64,768]{1,0:T(8,128)(2,1)S(1)} %get-tuple-element.40), channel_id=1, source_target_pairs={{0,20},{4,16},{8,28},{12,24},{16,4},{20,0},{24,12},{28,8},{1,21},{... | collective-permute-start | bytes 294920 | tf_op jit(solution)/shard_map/ppermute | solution.py:240
  9.4 10.0 %collective-permute-start.2 = (bf16[64,768]{1,0:T(8,128)(2,1)S(1)}, bf16[64,768]{1,0:T(8,128)(2,1)S(1)}, u32[]{:S(2)}, u32[]{:S(2)}) collective-permute-start(bf16[64,768]{1,0:T(8,128)(2,1)S(1)} %get-tuple-element.41), channel_id=1, source_target_pairs={{0,16},{4,20},{8,24},{12,28},{16,0},{20,4},{24,8},{28,12},{1,17},{... | collective-permute-start | bytes 294920 | tf_op jit(solution)/shard_map/ppermute | solution.py:240
  16.1 5.2 %collective-permute-start.5 = (bf16[256,256]{1,0:T(8,128)(2,1)}, bf16[256,256]{1,0:T(8,128)(2,1)S(1)}, u32[]{:S(2)}, u32[]{:S(2)}) collective-permute-start(bf16[256,256]{1,0:T(8,128)(2,1)} %get-tuple-element.18), channel_id=1, source_target_pairs={{0,4},{4,0},{1,5},{5,1},{2,6},{6,2},{3,7},{7,3},{8,12},{12,8},{9,1... | collective-permute-start | bytes 393224 | tf_op jit(solution)/shard_map/ppermute | solution.py:259
  16.4 10.6 %collective-permute-start.21 = (bf16[384,256]{1,0:T(8,128)(2,1)S(1)}, bf16[384,256]{1,0:T(8,128)(2,1)S(1)}, u32[]{:S(2)}, u32[]{:S(2)}) collective-permute-start(bf16[384,256]{1,0:T(8,128)(2,1)S(1)} %get-tuple-element.43), channel_id=1, source_target_pairs={{0,2},{1,3},{2,0},{3,1},{4,6},{5,7},{6,4},{7,5},{8,10},{9,11},{10,... | collective-permute-start | bytes 589832 | tf_op jit(solution)/shard_map/ppermute | solution.py:187
  21.3 6.4 %collective-permute-start.8 = (bf16[256,256]{1,0:T(8,128)(2,1)S(1)}, bf16[256,256]{1,0:T(8,128)(2,1)S(1)}, u32[]{:S(2)}, u32[]{:S(2)}) collective-permute-start(bf16[256,256]{1,0:T(8,128)(2,1)S(1)} %add_convert_fusion), channel_id=1, source_target_pairs={{0,20},{4,16},{8,28},{12,24},{16,4},{20,0},{24,12},{28,8},{1,21},{... | collective-permute-start | bytes 393224 | tf_op jit(solution)/shard_map/ppermute | solution.py:215
  22.9 5.8 %collective-permute-start.7 = (bf16[256,256]{1,0:T(8,128)(2,1)S(1)}, bf16[256,256]{1,0:T(8,128)(2,1)S(1)}, u32[]{:S(2)}, u32[]{:S(2)}) collective-permute-start(bf16[256,256]{1,0:T(8,128)(2,1)S(1)} %add_convert_fusion), channel_id=1, source_target_pairs={{0,16},{4,20},{8,24},{12,28},{16,0},{20,4},{24,8},{28,12},{1,17},{... | collective-permute-start | bytes 393224 | tf_op jit(solution)/shard_map/ppermute | solution.py:215
  23.1 10.6 %collective-permute-start.6 = (bf16[256,256]{1,0:T(8,128)(2,1)S(1)}, bf16[256,256]{1,0:T(8,128)(2,1)S(1)}, u32[]{:S(2)}, u32[]{:S(2)}) collective-permute-start(bf16[256,256]{1,0:T(8,128)(2,1)S(1)} %add_convert_fusion), channel_id=1, source_target_pairs={{0,4},{4,0},{8,12},{12,8},{16,20},{20,16},{24,28},{28,24},{1,5},{5... | collective-permute-start | bytes 393224 | tf_op jit(solution)/shard_map/ppermute | solution.py:215
  24.9 8.9 %collective-permute-start.4 = (bf16[256,384]{1,0:T(8,128)(2,1)S(1)}, bf16[256,384]{1,0:T(8,128)(2,1)S(1)}, u32[]{:S(2)}, u32[]{:S(2)}) collective-permute-start(bf16[256,384]{1,0:T(8,128)(2,1)S(1)} %get-tuple-element.37), channel_id=1, source_target_pairs={{0,8},{8,0},{16,24},{24,16},{1,9},{9,1},{17,25},{25,17},{2,10},{10... | collective-permute-start | bytes 589832 | tf_op jit(solution)/shard_map/ppermute | solution.py:219
  27.0 13.6 %collective-permute-start.20 = (bf16[384,256]{1,0:T(8,128)(2,1)S(1)}, bf16[384,256]{1,0:T(8,128)(2,1)S(1)}, u32[]{:S(2)}, u32[]{:S(2)}) collective-permute-start(bf16[384,256]{1,0:T(8,128)(2,1)S(1)} %get-tuple-element.43), channel_id=1, source_target_pairs={{0,1},{1,0},{2,3},{3,2},{4,5},{5,4},{6,7},{7,6},{8,9},{9,8},{10,11... | collective-permute-start | bytes 589832 | tf_op jit(solution)/shard_map/ppermute | solution.py:187
  27.8 6.2 %collective-permute-start.23 = (bf16[384,256]{1,0:T(8,128)(2,1)S(1)}, bf16[384,256]{1,0:T(8,128)(2,1)S(1)}, u32[]{:S(2)}, u32[]{:S(2)}) collective-permute-start(bf16[384,256]{1,0:T(8,128)(2,1)S(1)} %get-tuple-element.43), channel_id=1, source_target_pairs={{0,0},{1,2},{2,1},{3,3},{4,4},{5,6},{6,5},{7,7},{8,8},{9,10},{10,9... | collective-permute-start | bytes 589832 | tf_op jit(solution)/shard_map/ppermute | solution.py:187
  28.7 11.3 %collective-permute-start.22 = (bf16[384,256]{1,0:T(8,128)(2,1)S(1)}, bf16[384,256]{1,0:T(8,128)(2,1)S(1)}, u32[]{:S(2)}, u32[]{:S(2)}) collective-permute-start(bf16[384,256]{1,0:T(8,128)(2,1)S(1)} %collective-permute-done.21), channel_id=1, source_target_pairs={{0,1},{1,0},{2,3},{3,2},{4,5},{5,4},{6,7},{7,6},{8,9},{9,8},{10,11... | collective-permute-start | bytes 589832 | tf_op jit(solution)/shard_map/ppermute | solution.py:190
  33.8 7.2 %collective-permute-start.9 = (bf16[4,256,256]{2,1,0:T(8,128)(2,1)S(1)}, bf16[4,256,256]{2,1,0:T(8,128)(2,1)S(1)}, u32[]{:S(2)}, u32[]{:S(2)}) collective-permute-start(bf16[4,256,256]{2,1,0:T(8,128)(2,1)S(1)} %pad_maximum_fusion.1), channel_id=1, source_target_pairs={{0,8},{8,0},{16,24},{24,16},{1,9},{9,1},{17,25},{25,17},{2,10},{10... | collective-permute-start | bytes 1572872 | tf_op jit(solution)/shard_map/ppermute | solution.py:219
  33.9 21.4 %collective-permute-start.11 = (bf16[512,384]{1,0:T(8,128)(2,1)S(1)}, bf16[512,384]{1,0:T(8,128)(2,1)S(1)}, u32[]{:S(2)}, u32[]{:S(2)}) collective-permute-start(bf16[512,384]{1,0:T(8,128)(2,1)S(1)} %pad_maximum_fusion.3), channel_id=1, source_target_pairs={{0,2},{1,3},{2,0},{3,1},{4,6},{5,7},{6,4},{7,5},{8,10},{9,11},{10,... | collective-permute-start | bytes 1179656 | tf_op jit(solution)/shard_map/ppermute | solution.py:187
  34.0 23.1 %collective-permute-start.10 = (bf16[512,384]{1,0:T(8,128)(2,1)S(1)}, bf16[512,384]{1,0:T(8,128)(2,1)S(1)}, u32[]{:S(2)}, u32[]{:S(2)}) collective-permute-start(bf16[512,384]{1,0:T(8,128)(2,1)S(1)} %pad_maximum_fusion.3), channel_id=1, source_target_pairs={{0,1},{1,0},{2,3},{3,2},{4,5},{5,4},{6,7},{7,6},{8,9},{9,8},{10,11... | collective-permute-start | bytes 1179656 | tf_op jit(solution)/shard_map/ppermute | solution.py:187
  40.0 19.0 %collective-permute-start.13 = (bf16[512,384]{1,0:T(8,128)(2,1)S(1)}, bf16[512,384]{1,0:T(8,128)(2,1)S(1)}, u32[]{:S(2)}, u32[]{:S(2)}) collective-permute-start(bf16[512,384]{1,0:T(8,128)(2,1)S(1)} %pad_maximum_fusion.3), channel_id=1, source_target_pairs={{0,0},{1,2},{2,1},{3,3},{4,4},{5,6},{6,5},{7,7},{8,8},{9,10},{10,9... | collective-permute-start | bytes 1179656 | tf_op jit(solution)/shard_map/ppermute | solution.py:187
  40.8 37.0 %collective-permute-start.24 = (bf16[4,384,256]{2,1,0:T(8,128)(2,1)S(1)}, bf16[4,384,256]{2,1,0:T(8,128)(2,1)S(1)}, u32[]{:S(2)}, u32[]{:S(2)}) collective-permute-start(bf16[4,384,256]{2,1,0:T(8,128)(2,1)S(1)} %pad_maximum_fusion.own_ref), channel_id=1, source_target_pairs={{0,8},{8,0},{16,24},{24,16},{1,9},{9,1},{17,25},{25,17},{2,10},{10... | collective-permute-start | bytes 2359304 | tf_op jit(solution)/shard_map/ppermute | solution.py:219
  41.0 35.8 %collective-permute-start.26 = (bf16[256,256]{1,0:T(8,128)(2,1)S(1)}, bf16[256,256]{1,0:T(8,128)(2,1)S(1)}, u32[]{:S(2)}, u32[]{:S(2)}) collective-permute-start(bf16[256,256]{1,0:T(8,128)(2,1)S(1)} %bitcast.51), channel_id=1, source_target_pairs={{0,2},{1,3},{2,0},{3,1},{4,6},{5,7},{6,4},{7,5},{8,10},{9,11},{10,... | collective-permute-start | bytes 393224 | tf_op jit(solution)/shard_map/ppermute | solution.py:270
  55.3 22.5 %collective-permute-start.25 = (bf16[256,256]{1,0:T(8,128)(2,1)S(1)}, bf16[256,256]{1,0:T(8,128)(2,1)S(1)}, u32[]{:S(2)}, u32[]{:S(2)}) collective-permute-start(bf16[256,256]{1,0:T(8,128)(2,1)S(1)} %bitcast.47), channel_id=1, source_target_pairs={{0,1},{1,0},{2,3},{3,2},{4,5},{5,4},{6,7},{7,6},{8,9},{9,8},{10,11... | collective-permute-start | bytes 393224 | tf_op jit(solution)/shard_map/ppermute | solution.py:270
  57.1 16.8 %collective-permute-start.12 = (bf16[512,384]{1,0:T(8,128)(2,1)S(1)}, bf16[512,384]{1,0:T(8,128)(2,1)S(1)}, u32[]{:S(2)}, u32[]{:S(2)}) collective-permute-start(bf16[512,384]{1,0:T(8,128)(2,1)S(1)} %collective-permute-done.11), channel_id=1, source_target_pairs={{0,1},{1,0},{2,3},{3,2},{4,5},{5,4},{6,7},{7,6},{8,9},{9,8},{10,11... | collective-permute-start | bytes 1179656 | tf_op jit(solution)/shard_map/ppermute | solution.py:190
  59.0 18.3 %collective-permute-start.27 = (bf16[256,256]{1,0:T(8,128)(2,1)S(1)}, bf16[256,256]{1,0:T(8,128)(2,1)S(1)}, u32[]{:S(2)}, u32[]{:S(2)}) collective-permute-start(bf16[256,256]{1,0:T(8,128)(2,1)S(1)} %bitcast.49), channel_id=1, source_target_pairs={{0,3},{1,2},{2,1},{3,0},{4,7},{5,6},{6,5},{7,4},{8,11},{9,10},{10,... | collective-permute-start | bytes 393224 | tf_op jit(solution)/shard_map/ppermute | solution.py:270
  74.2 9.5 %collective-permute-start.16 = (bf16[384,256]{1,0:T(8,128)(2,1)S(1)}, bf16[384,256]{1,0:T(8,128)(2,1)S(1)}, u32[]{:S(2)}, u32[]{:S(2)}) collective-permute-start(bf16[384,256]{1,0:T(8,128)(2,1)S(1)} %fusion.1.refs_0_), channel_id=1, source_target_pairs={{0,20},{4,16},{8,28},{12,24},{16,4},{20,0},{24,12},{28,8},{1,21},{... | collective-permute-start | bytes 589832 | tf_op jit(solution)/shard_map/ppermute | solution.py:215
  76.7 7.0 %collective-permute-start.15 = (bf16[384,256]{1,0:T(8,128)(2,1)S(1)}, bf16[384,256]{1,0:T(8,128)(2,1)S(1)}, u32[]{:S(2)}, u32[]{:S(2)}) collective-permute-start(bf16[384,256]{1,0:T(8,128)(2,1)S(1)} %fusion.1.refs_0_), channel_id=1, source_target_pairs={{0,16},{4,20},{8,24},{12,28},{16,0},{20,4},{24,8},{28,12},{1,17},{... | collective-permute-start | bytes 589832 | tf_op jit(solution)/shard_map/ppermute | solution.py:215
  77.3 7.0 %collective-permute-start.14 = (bf16[384,256]{1,0:T(8,128)(2,1)S(1)}, bf16[384,256]{1,0:T(8,128)(2,1)S(1)}, u32[]{:S(2)}, u32[]{:S(2)}) collective-permute-start(bf16[384,256]{1,0:T(8,128)(2,1)S(1)} %fusion.1.refs_0_), channel_id=1, source_target_pairs={{0,4},{4,0},{8,12},{12,8},{16,20},{20,16},{24,28},{28,24},{1,5},{5... | collective-permute-start | bytes 589832 | tf_op jit(solution)/shard_map/ppermute | solution.py:215
  77.8 6.6 %collective-permute-start.31 = (bf16[384,256]{1,0:T(8,128)(2,1)S(1)}, bf16[384,256]{1,0:T(8,128)(2,1)S(1)}, u32[]{:S(2)}, u32[]{:S(2)}) collective-permute-start(bf16[384,256]{1,0:T(8,128)(2,1)S(1)} %fusion.1.refs_0_), channel_id=1, source_target_pairs={{0,8},{8,0},{16,24},{24,16},{1,9},{9,1},{17,25},{25,17},{2,10},{10... | collective-permute-start | bytes 589832 | tf_op jit(solution)/shard_map/ppermute | solution.py:219
  82.3 4.8 %collective-permute-start.28 = (bf16[64,768]{1,0:T(8,128)(2,1)}, bf16[64,768]{1,0:T(8,128)(2,1)S(1)}, u32[]{:S(2)}, u32[]{:S(2)}) collective-permute-start(bf16[64,768]{1,0:T(8,128)(2,1)} %get-tuple-element.20), channel_id=1, source_target_pairs={{0,4},{4,0},{8,12},{12,8},{16,20},{20,16},{24,28},{28,24},{1,5},{5... | collective-permute-start | bytes 294920 | tf_op jit(solution)/shard_map/ppermute | solution.py:287
  83.8 9.1 %collective-permute-start.19 = (bf16[384,256]{1,0:T(8,128)(2,1)S(1)}, bf16[384,256]{1,0:T(8,128)(2,1)S(1)}, u32[]{:S(2)}, u32[]{:S(2)}) collective-permute-start(bf16[384,256]{1,0:T(8,128)(2,1)S(1)} %collective-permute-done.16.refs_2_), channel_id=1, source_target_pairs={{0,8},{8,0},{16,24},{24,16},{1,9},{9,1},{17,25},{25,17},{2,10},{10... | collective-permute-start | bytes 589832 | tf_op jit(solution)/shard_map/ppermute | solution.py:219
  83.8 9.0 %collective-permute-start.18 = (bf16[384,256]{1,0:T(8,128)(2,1)S(1)}, bf16[384,256]{1,0:T(8,128)(2,1)S(1)}, u32[]{:S(2)}, u32[]{:S(2)}) collective-permute-start(bf16[384,256]{1,0:T(8,128)(2,1)S(1)} %collective-permute-done.15.refs_1_), channel_id=1, source_target_pairs={{0,8},{8,0},{16,24},{24,16},{1,9},{9,1},{17,25},{25,17},{2,10},{10... | collective-permute-start | bytes 589832 | tf_op jit(solution)/shard_map/ppermute | solution.py:219
  84.3 8.5 %collective-permute-start.17 = (bf16[384,256]{1,0:T(8,128)(2,1)S(1)}, bf16[384,256]{1,0:T(8,128)(2,1)S(1)}, u32[]{:S(2)}, u32[]{:S(2)}) collective-permute-start(bf16[384,256]{1,0:T(8,128)(2,1)S(1)} %collective-permute-done.14.refs_0_), channel_id=1, source_target_pairs={{0,8},{8,0},{16,24},{24,16},{1,9},{9,1},{17,25},{25,17},{2,10},{10... | collective-permute-start | bytes 589832 | tf_op jit(solution)/shard_map/ppermute | solution.py:219
  84.4 7.1 %collective-permute-start.29 = (bf16[64,768]{1,0:T(8,128)(2,1)}, bf16[64,768]{1,0:T(8,128)(2,1)S(1)}, u32[]{:S(2)}, u32[]{:S(2)}) collective-permute-start(bf16[64,768]{1,0:T(8,128)(2,1)} %get-tuple-element.21), channel_id=1, source_target_pairs={{0,16},{4,20},{8,24},{12,28},{16,0},{20,4},{24,8},{28,12},{1,17},{... | collective-permute-start | bytes 294920 | tf_op jit(solution)/shard_map/ppermute | solution.py:287
  87.1 5.7 %collective-permute-start.30 = (bf16[64,768]{1,0:T(8,128)(2,1)}, bf16[64,768]{1,0:T(8,128)(2,1)S(1)}, u32[]{:S(2)}, u32[]{:S(2)}) collective-permute-start(bf16[64,768]{1,0:T(8,128)(2,1)} %get-tuple-element.22), channel_id=1, source_target_pairs={{0,20},{4,16},{8,28},{12,24},{16,4},{20,0},{24,12},{28,8},{1,21},{... | collective-permute-start | bytes 294920 | tf_op jit(solution)/shard_map/ppermute | solution.py:287
  (20 other events, 109.7 us)

commit v2 on v1

--- a/solution.py
+++ b/solution.py
@@ -94,21 +94,25 @@
     )(at, q, g, *packs)
 
 
-def input_kernel(heads, own_ref, other_ref, *refs):
-    row_refs, out_refs = refs[:heads], refs[heads:]
-    size, sub = own_ref.shape[1], out_refs[0].shape[0]
+def input_kernel(cells, own_ref, other_ref, *refs):
+    row_refs, out_refs = refs[:cells], refs[cells:]
+    sub = row_refs[0].shape[0]
+    heads, size, width = own_ref.shape
+    rows = jnp.concatenate([ref[...] for ref in row_refs], axis=0)
     for j, w_ref in enumerate((own_ref, other_ref)):
-        part = sum(dot(row_refs[r][...], w_ref[r], 1, 1) for r in range(heads))
+        part = sum(
+            dot(rows[:, r * width : (r + 1) * width], w_ref[r], 1, 1) for r in range(heads)
+        )
         for o, out_ref in enumerate(out_refs):
             out_ref[:, j * size : (j + 1) * size] = part[o * sub : (o + 1) * sub].astype(BF16)
 
 
-def input_parts(w_own, w_other, rows, cells):
-    heads, size, sub = len(rows), w_own.shape[1], rows[0].shape[0] // cells
+def input_parts(w_own, w_other, rows):
+    cells, sub, size = len(rows), rows[0].shape[0], w_own.shape[1]
     return pl.pallas_call(
-        functools.partial(input_kernel, heads),
+        functools.partial(input_kernel, cells),
         out_shape=[jax.ShapeDtypeStruct((sub, 2 * size), BF16)] * cells,
-        in_specs=[VMEM] * (heads + 2),
+        in_specs=[VMEM] * (cells + 2),
         name="input_grads",
         cost_estimate=pl.CostEstimate(
             flops=4 * cells * sub * w_own.size, transcendentals=0, bytes_accessed=4 * w_own.size
@@ -259,16 +263,21 @@
         terms.append(lax.ppermute(prev_terms[r - 1], "seq", pairs))
     dkv = sum([t.astype(F32) for t in terms], own_terms).astype(BF16)
 
+    pieces = [lax.dynamic_slice_in_dim(dkv, z * sub, sub, 0)]
+    for r in range(1, heads):
+        piece = lax.dynamic_slice_in_dim(dkv, (z ^ r) * sub, sub, 0)
+        pieces.append(lax.ppermute(piece, "head", swap_pairs(heads, r)))
+    head_rows = cell_gather(jnp.concatenate(pieces, axis=1))
+
     dkv_own = jnp.stack(cell_gather(dkv))
     dkv_other = core_swap(dkv_own)
-    head_rows, both_rows = [], []
+    both_rows = []
     for r in range(heads):
-        own, other = (
+        halves = [
             lax.dynamic_slice_in_dim(t, (z ^ r) * sub, sub, 1).reshape(cells * sub, 2 * HD)
             for t in (dkv_own, dkv_other)
-        )
-        head_rows.append(lax.ppermute(own, "head", swap_pairs(heads, r)) if r else own)
-        both_rows.append(jnp.concatenate([own, other], axis=0))
+        ]
+        both_rows.append(jnp.concatenate(halves, axis=0))
     outer = (z == 0) | (z == heads - 1)
 
     if len(x_slots) > heads:
@@ -282,7 +291,7 @@
     if len(w_slots) > heads:
         w_slots = w_slots[: heads - 1] + [jnp.where(outer, w_slots[heads], w_slots[heads - 1])]
     w_own = jnp.stack(w_slots)
-    parts = list(input_parts(w_own, core_swap(w_own), head_rows, cells))
+    parts = list(input_parts(w_own, core_swap(w_own), head_rows))
     for o in far_first(cells):
         parts[o] = lax.ppermute(parts[o], both, swap_pairs(plane, member(o, 0)))
     rest = [i for i in items if i[0]]

time: 97.8 us -> 93.7 us (0.958)
  starting transfers between devices: 47.1 us -> 33.5 us
  waiting for transfers between devices: 27.8 us -> 38.2 us
  local copies, waits for them, and re-layouts: 5.1 us -> 4.12 us
    ppermute x3, starting transfers between devices: 9.61 us -> 4.45 us  [shards(): pieces.append(lax.ppermute(piece, 'head', swap_pairs(heads, r)))]
    ppermute x3, waiting for transfers between devices: 0.01 us -> 4.89 us  [shards(): pieces.append(lax.ppermute(piece, 'head', swap_pairs(heads, r)))]
    ppermute x6, starting transfers between devices: 11 us -> 6.18 us  [line_exchange(): slots[r] = lax.ppermute(x, 'head', pairs)]
    ppermute x2, starting transfers between devices: 6.29 us -> 2.88 us  [line_exchange(): out.append(lax.ppermute(slots[2], 'head', swap_pairs(n, 1)))]
    ppermute x3, starting transfers between devices: 5.43 us -> 2.55 us  [shards(): parts[o] = lax.ppermute(parts[o], both, swap_pairs(plane, member(o, 0)))]
    ppermute x6 -> x9, starting transfers between devices: 7.11 us -> 9.78 us  [cell_gather(): got[o] = lax.ppermute(x, both, swap_pairs(plane, member(o, 0)))]
    ppermute x1, waiting for transfers between devices: 1.91 us -> 4.47 us  [shards(): terms.append(lax.ppermute(prev_terms[r - 1], 'seq', pairs))]
    ppermute x6 -> x9, waiting for transfers between devices: 0.23 us -> 2.56 us  [cell_gather(): got[o] = lax.ppermute(x, both, swap_pairs(plane, member(o, 0)))]
  transfers between devices with their start and end apart: 32 -> 35, of which waited for: 7 -> 11; matrix products, arithmetic and copies ran while one was open for 4% -> 4% of each run, Pallas kernels for 9% -> 10%
where the time goes in v2:
time: 93.7 us; the launch traced here: 93.3 us
  waiting for transfers between devices  38.2 us (41%)
  starting transfers between devices  33.5 us (36%)
  Pallas kernels  12.6 us (13%)
  local copies, waits for them, and re-layouts  4.12 us (4%)
  other arithmetic  2.6 us (3%)
  matrix products  1.28 us (1%)
  between operations  1.01 us (1%)
    ppermute x6, waiting for transfers between devices, line_exchange(): slots[r] = lax.ppermute(x, 'head', pairs)  13.4 us
    ppermute x9, starting transfers between devices, cell_gather(): got[o] = lax.ppermute(x, both, swap_pairs(plane, member(o, 0)))  9.78 us
    ppermute x2, waiting for transfers between devices, line_exchange(): out.append(lax.ppermute(slots[2], 'head', swap_pairs(n, 1)))  9.74 us
    ppermute x6, starting transfers between devices, line_exchange(): slots[r] = lax.ppermute(x, 'head', pairs)  6.18 us
    pallas_call x2, Pallas kernels, spread(): pl.pallas_call(functools.partial(spread_kernel, tuple((item[:2] for item...  5.66 us
    ppermute x3, waiting for transfers between devices, shards(): pieces.append(lax.ppermute(piece, 'head', swap_pairs(heads, r)))  4.89 us
    ppermute x1, waiting for transfers between devices, shards(): terms.append(lax.ppermute(prev_terms[r - 1], 'seq', pairs))  4.47 us
    ppermute x3, starting transfers between devices, shards(): pieces.append(lax.ppermute(piece, 'head', swap_pairs(heads, r)))  4.45 us
  transfers between devices with their start and end apart: 35, of which 11 were waited for; matrix products, arithmetic and copies ran while one was open for 4% of the time, Pallas kernels for 10%

profile of v2, /device:TPU:0, one launch (start us, length us, event | category | flops | bytes accessed | tf_op | source)
XLA Modules:
  0.0 93.3 jit_solution(9025578392336742304)
XLA Ops:
  0.6 0.7 convert_element_type.12
  1.4 0.9 pad_maximum_fusion.5.refs_0_
  2.3 3.0 %collective-permute-start = (bf16[257,256]{1,0:T(8,128)(2,1)S(1)}, bf16[257,256]{1,0:T(8,128)(2,1)S(1)}, u32[]{:S(2)}, u32[]{:S(2)}) collective-permute-start(bf16[257,256]{1,0:T(8,128)(2,1)S(1)} %pad_maximum_fusion.5.refs_0_), channel_id=1, source_target_pairs={{0,4},{4,0},{1,5},{5,1},{2,6},{6,2},{3,7},{7,3},{8,12},{12,8},{9,1... | collective-permute-start | bytes 394760 | tf_op jit(solution)/shard_map/ppermute | solution.py:237
  5.3 1.0 %constant_dynamic-slice_fusion.4 = (bf16[384,128]{1,0:T(8,128)(2,1)S(1)}, bf16[384,128]{1,0:T(8,128)(2,1)S(1)}) fusion(bf16[3072,128]{1,0:T(8,128)(2,1)} %param.15, s32[]{:T(128)S(6)} %select_n.83, bf16[3072,128]{1,0:T(8,128)(2,1)} %param.14), kind=kLoop, calls=%fused_computation.37 | loop fusion | bytes 393220 | tf_op jit(solution)/shard_map/dynamic_slice | solution.py:253
  6.3 2.7 %collective-permute-start.21 = (bf16[384,256]{1,0:T(8,128)(2,1)S(1)}, bf16[384,256]{1,0:T(8,128)(2,1)S(1)}, u32[]{:S(2)}, u32[]{:S(2)}) collective-permute-start(bf16[384,256]{1,0:T(8,128)(2,1)S(1)} %get-tuple-element.43), channel_id=1, source_target_pairs={{0,2},{1,3},{2,0},{3,1},{4,6},{5,7},{6,4},{7,5},{8,10},{9,11},{10,... | collective-permute-start | bytes 589832 | tf_op jit(solution)/shard_map/ppermute | solution.py:191
  9.6 2.4 %collective-permute-start.3 = (bf16[64,768]{1,0:T(8,128)(2,1)S(1)}, bf16[64,768]{1,0:T(8,128)(2,1)S(1)}, u32[]{:S(2)}, u32[]{:S(2)}) collective-permute-start(bf16[64,768]{1,0:T(8,128)(2,1)S(1)} %get-tuple-element.40), channel_id=1, source_target_pairs={{0,20},{4,16},{8,28},{12,24},{16,4},{20,0},{24,12},{28,8},{1,21},{... | collective-permute-start | bytes 294920 | tf_op jit(solution)/shard_map/ppermute | solution.py:244
  13.9 4.0 %attention.1 = (bf16[256,384]{1,0:T(8,128)(2,1)}, f32[256,256]{1,0:T(8,128)}, bf16[256,256]{1,0:T(8,128)(2,1)}) custom-call(s32[4]{0:T(128)} %pad_add_fusion.at_ref, bf16[256,384]{1,0:T(8,128)(2,1)} %bitcast.55, bf16[256,384]{1,0:T(8,128)(2,1)} %bitcast.56, bf16[257,256]{1,0:T(8,128)(2,1)} %copy-done.13, bf16[257,256]{1,0:T(8,128)(2,1)} %copy-done.20), custom_call_target="tpu_custom_call" | custom-call | flops 503316480 | bytes 786432 | tf_op jit(solution)/shard_map/attention/pallas_call | solution.py:84
  18.6 4.5 %collective-permute-done.5 = bf16[256,256]{1,0:T(8,128)(2,1)S(1)} collective-permute-done((bf16[256,256]{1,0:T(8,128)(2,1)}, bf16[256,256]{1,0:T(8,128)(2,1)S(1)}, u32[]{:S(2)}, u32[]{:S(2)}) %collective-permute-start.5) | collective-permute-done | bytes 131104 | tf_op jit(solution)/shard_map/ppermute | solution.py:263
  23.1 1.6 %collective-permute-start.8 = (bf16[256,256]{1,0:T(8,128)(2,1)S(1)}, bf16[256,256]{1,0:T(8,128)(2,1)S(1)}, u32[]{:S(2)}, u32[]{:S(2)}) collective-permute-start(bf16[256,256]{1,0:T(8,128)(2,1)S(1)} %add_convert_fusion), channel_id=1, source_target_pairs={{0,20},{4,16},{8,28},{12,24},{16,4},{20,0},{24,12},{28,8},{1,21},{... | collective-permute-start | bytes 393224 | tf_op jit(solution)/shard_map/ppermute | solution.py:219
  25.2 1.5 %collective-permute-start.6 = (bf16[256,256]{1,0:T(8,128)(2,1)S(1)}, bf16[256,256]{1,0:T(8,128)(2,1)S(1)}, u32[]{:S(2)}, u32[]{:S(2)}) collective-permute-start(bf16[256,256]{1,0:T(8,128)(2,1)S(1)} %add_convert_fusion), channel_id=1, source_target_pairs={{0,4},{4,0},{8,12},{12,8},{16,20},{20,16},{24,28},{28,24},{1,5},{5... | collective-permute-start | bytes 393224 | tf_op jit(solution)/shard_map/ppermute | solution.py:219
  26.7 0.7 collective-permute-start.23
  27.4 2.9 %collective-permute-start.22 = (bf16[384,256]{1,0:T(8,128)(2,1)S(1)}, bf16[384,256]{1,0:T(8,128)(2,1)S(1)}, u32[]{:S(2)}, u32[]{:S(2)}) collective-permute-start(bf16[384,256]{1,0:T(8,128)(2,1)S(1)} %collective-permute-done.21), channel_id=1, source_target_pairs={{0,1},{1,0},{2,3},{3,2},{4,5},{5,4},{6,7},{7,6},{8,9},{9,8},{10,11... | collective-permute-start | bytes 589832 | tf_op jit(solution)/shard_map/ppermute | solution.py:194
  30.3 3.0 %collective-permute-start.27 = (bf16[64,256]{1,0:T(8,128)(2,1)S(1)}, bf16[64,256]{1,0:T(8,128)(2,1)S(1)}, u32[]{:S(2)}, u32[]{:S(2)}) collective-permute-start(bf16[64,256]{1,0:T(8,128)(2,1)S(1)} %get-tuple-element.45), channel_id=1, source_target_pairs={{0,3},{1,2},{2,1},{3,0},{4,7},{5,6},{6,5},{7,4},{8,11},{9,10},{10,... | collective-permute-start | bytes 98312 | tf_op jit(solution)/shard_map/ppermute | solution.py:269
  33.3 1.5 %collective-permute-start.25 = (bf16[64,256]{1,0:T(8,128)(2,1)S(1)}, bf16[64,256]{1,0:T(8,128)(2,1)S(1)}, u32[]{:S(2)}, u32[]{:S(2)}) collective-permute-start(bf16[64,256]{1,0:T(8,128)(2,1)S(1)} %get-tuple-element.47), channel_id=1, source_target_pairs={{0,1},{1,0},{2,3},{3,2},{4,5},{5,4},{6,7},{7,6},{8,9},{9,8},{10,11... | collective-permute-start | bytes 98312 | tf_op jit(solution)/shard_map/ppermute | solution.py:269
  34.8 4.9 %collective-permute-done.27 = bf16[64,256]{1,0:T(8,128)(2,1)S(1)} collective-permute-done((bf16[64,256]{1,0:T(8,128)(2,1)S(1)}, bf16[64,256]{1,0:T(8,128)(2,1)S(1)}, u32[]{:S(2)}, u32[]{:S(2)}) %collective-permute-start.27) | collective-permute-done | bytes 32800 | tf_op jit(solution)/shard_map/ppermute | solution.py:269
  40.1 1.9 %collective-permute-start.10 = (bf16[512,384]{1,0:T(8,128)(2,1)S(1)}, bf16[512,384]{1,0:T(8,128)(2,1)S(1)}, u32[]{:S(2)}, u32[]{:S(2)}) collective-permute-start(bf16[512,384]{1,0:T(8,128)(2,1)S(1)} %pad_maximum_fusion.3), channel_id=1, source_target_pairs={{0,1},{1,0},{2,3},{3,2},{4,5},{5,4},{6,7},{7,6},{8,9},{9,8},{10,11... | collective-permute-start | bytes 1179656 | tf_op jit(solution)/shard_map/ppermute | solution.py:191
  42.0 0.7 collective-permute-start.13
  42.7 6.7 %collective-permute-done.20 = bf16[384,256]{1,0:T(8,128)(2,1)S(1)} collective-permute-done((bf16[384,256]{1,0:T(8,128)(2,1)S(1)}, bf16[384,256]{1,0:T(8,128)(2,1)S(1)}, u32[]{:S(2)}, u32[]{:S(2)}) %collective-permute-start.20) | collective-permute-done | bytes 196640 | tf_op jit(solution)/shard_map/ppermute | solution.py:191
  49.3 1.7 %collective-permute-start.30 = (bf16[64,1024]{1,0:T(8,128)(2,1)S(1)}, bf16[64,1024]{1,0:T(8,128)(2,1)S(1)}, u32[]{:S(2)}, u32[]{:S(2)}) collective-permute-start(bf16[64,1024]{1,0:T(8,128)(2,1)S(1)} %pad_maximum_fusion.6.refs_0_), channel_id=1, source_target_pairs={{0,20},{4,16},{8,28},{12,24},{16,4},{20,0},{24,12},{28,8},{1,21},{... | collective-permute-start | bytes 393224 | tf_op jit(solution)/shard_map/ppermute | solution.py:219
  51.6 6.1 %collective-permute-done.11 = bf16[512,384]{1,0:T(8,128)(2,1)S(1)} collective-permute-done((bf16[512,384]{1,0:T(8,128)(2,1)S(1)}, bf16[512,384]{1,0:T(8,128)(2,1)S(1)}, u32[]{:S(2)}, u32[]{:S(2)}) %collective-permute-start.11) | collective-permute-done | bytes 393248 | tf_op jit(solution)/shard_map/ppermute | solution.py:191
  59.9 9.7 %collective-permute-done.12 = bf16[512,384]{1,0:T(8,128)(2,1)S(1)} collective-permute-done((bf16[512,384]{1,0:T(8,128)(2,1)S(1)}, bf16[512,384]{1,0:T(8,128)(2,1)S(1)}, u32[]{:S(2)}, u32[]{:S(2)}) %collective-permute-start.12) | collective-permute-done | bytes 393248 | tf_op jit(solution)/shard_map/ppermute | solution.py:194
  70.0 1.5 %collective-permute-start.16 = (bf16[384,256]{1,0:T(8,128)(2,1)S(1)}, bf16[384,256]{1,0:T(8,128)(2,1)S(1)}, u32[]{:S(2)}, u32[]{:S(2)}) collective-permute-start(bf16[384,256]{1,0:T(8,128)(2,1)S(1)} %fusion.1.refs_0_), channel_id=1, source_target_pairs={{0,20},{4,16},{8,28},{12,24},{16,4},{20,0},{24,12},{28,8},{1,21},{... | collective-permute-start | bytes 589832 | tf_op jit(solution)/shard_map/ppermute | solution.py:219
  72.1 1.5 %collective-permute-start.14 = (bf16[384,256]{1,0:T(8,128)(2,1)S(1)}, bf16[384,256]{1,0:T(8,128)(2,1)S(1)}, u32[]{:S(2)}, u32[]{:S(2)}) collective-permute-start(bf16[384,256]{1,0:T(8,128)(2,1)S(1)} %fusion.1.refs_0_), channel_id=1, source_target_pairs={{0,4},{4,0},{8,12},{12,8},{16,20},{20,16},{24,28},{28,24},{1,5},{5... | collective-permute-start | bytes 589832 | tf_op jit(solution)/shard_map/ppermute | solution.py:219
  74.3 0.9 copy-done.1
  75.1 2.9 %input_grads.1 = (bf16[64,768]{1,0:T(8,128)(2,1)}, bf16[64,768]{1,0:T(8,128)(2,1)}, bf16[64,768]{1,0:T(8,128)(2,1)}, bf16[64,768]{1,0:T(8,128)(2,1)}) custom-call(bf16[4,384,256]{2,1,0:T(8,128)(2,1)} %copy-done, bf16[4,384,256]{2,1,0:T(8,128)(2,1)} %copy-done.1, bf16[64,1024]{1,0:T(8,128)(2,1)} %copy-done.2, bf16[64,1024]{1,0:T(8,128)(2,1)} %copy-done.16, ...), custom_call_target="tpu_custom_call" | custom-call | flops 402653184 | bytes 1572864 | tf_op jit(solution)/shard_map/input_grads/pallas_call | solution.py:112
  78.8 2.3 %collective-permute-done.15.refs_1_ = bf16[384,256]{1,0:T(8,128)(2,1)S(1)} collective-permute-done((bf16[384,256]{1,0:T(8,128)(2,1)S(1)}, bf16[384,256]{1,0:T(8,128)(2,1)S(1)}, u32[]{:S(2)}, u32[]{:S(2)}) %collective-permute-start.15) | collective-permute-done | bytes 196640 | tf_op jit(solution)/shard_map/ppermute | solution.py:219
  81.7 0.8 collective-permute-start.32
  83.0 1.2 %collective-permute-start.33 = (bf16[64,768]{1,0:T(8,128)(2,1)}, bf16[64,768]{1,0:T(8,128)(2,1)S(1)}, u32[]{:S(2)}, u32[]{:S(2)}) collective-permute-start(bf16[64,768]{1,0:T(8,128)(2,1)} %get-tuple-element.22), channel_id=1, source_target_pairs={{0,20},{4,16},{8,28},{12,24},{16,4},{20,0},{24,12},{28,8},{1,21},{... | collective-permute-start | bytes 294920 | tf_op jit(solution)/shard_map/ppermute | solution.py:296
  84.3 1.9 %shard_map.111 = (f32[3072,128]{1,0:T(8,128)}, f32[3072,128]{1,0:T(8,128)}) custom-call(s32[4]{0:T(128)} %pad_add_fusion.at_ref, bf16[384,256]{1,0:T(8,128)(2,1)} %copy-done.11, bf16[384,256]{1,0:T(8,128)(2,1)} %copy-done.12), custom_call_target="tpu_custom_call" | custom-call | tf_op jit(solution)/shard_map/pallas_call | solution.py:166
  86.2 1.5 %collective-permute-done.32.refs_8_ = bf16[64,768]{1,0:T(8,128)(2,1)S(1)} collective-permute-done((bf16[64,768]{1,0:T(8,128)(2,1)}, bf16[64,768]{1,0:T(8,128)(2,1)S(1)}, u32[]{:S(2)}, u32[]{:S(2)}) %collective-permute-start.32) | collective-permute-done | bytes 98336 | tf_op jit(solution)/shard_map/ppermute | solution.py:296
  87.7 1.1 %collective-permute-done.33.refs_9_ = bf16[64,768]{1,0:T(8,128)(2,1)S(1)} collective-permute-done((bf16[64,768]{1,0:T(8,128)(2,1)}, bf16[64,768]{1,0:T(8,128)(2,1)S(1)}, u32[]{:S(2)}, u32[]{:S(2)}) %collective-permute-start.33) | collective-permute-done | bytes 98336 | tf_op jit(solution)/shard_map/ppermute | solution.py:296
  89.6 3.7 %shard_map.112 = (f32[3072,128]{1,0:T(8,128)}, f32[3072,128]{1,0:T(8,128)}, bf16[64,3072]{1,0:T(8,128)(2,1)}) custom-call(s32[4]{0:T(128)} %pad_add_fusion.at_ref, bf16[384,256]{1,0:T(8,128)(2,1)} %copy-done.7, bf16[384,256]{1,0:T(8,128)(2,1)} %copy-done.6, bf16[384,256]{1,0:T(8,128)(2,1)} %copy-done.5, ...), custom_call_target="tpu_custom_call", output_to_operand_aliasing={{0}: (11, {}), {1}: (12, {})} | custom-call | tf_op jit(solution)/shard_map/pallas_call | solution.py:166
  (105 shorter events, 11.1 us)
Async XLA Ops:
  2.3 10.9 %collective-permute-start = (bf16[257,256]{1,0:T(8,128)(2,1)S(1)}, bf16[257,256]{1,0:T(8,128)(2,1)S(1)}, u32[]{:S(2)}, u32[]{:S(2)}) collective-permute-start(bf16[257,256]{1,0:T(8,128)(2,1)S(1)} %pad_maximum_fusion.5.refs_0_), channel_id=1, source_target_pairs={{0,4},{4,0},{1,5},{5,1},{2,6},{6,2},{3,7},{7,3},{8,12},{12,8},{9,1... | collective-permute-start | bytes 394760 | tf_op jit(solution)/shard_map/ppermute | solution.py:237
  6.3 20.4 %collective-permute-start.21 = (bf16[384,256]{1,0:T(8,128)(2,1)S(1)}, bf16[384,256]{1,0:T(8,128)(2,1)S(1)}, u32[]{:S(2)}, u32[]{:S(2)}) collective-permute-start(bf16[384,256]{1,0:T(8,128)(2,1)S(1)} %get-tuple-element.43), channel_id=1, source_target_pairs={{0,2},{1,3},{2,0},{3,1},{4,6},{5,7},{6,4},{7,5},{8,10},{9,11},{10,... | collective-permute-start | bytes 589832 | tf_op jit(solution)/shard_map/ppermute | solution.py:191
  9.0 9.4 %collective-permute-start.1 = (bf16[64,768]{1,0:T(8,128)(2,1)S(1)}, bf16[64,768]{1,0:T(8,128)(2,1)S(1)}, u32[]{:S(2)}, u32[]{:S(2)}) collective-permute-start(bf16[64,768]{1,0:T(8,128)(2,1)S(1)} %get-tuple-element.39), channel_id=1, source_target_pairs={{0,4},{4,0},{8,12},{12,8},{16,20},{20,16},{24,28},{28,24},{1,5},{5... | collective-permute-start | bytes 294920 | tf_op jit(solution)/shard_map/ppermute | solution.py:244
  9.6 8.8 %collective-permute-start.3 = (bf16[64,768]{1,0:T(8,128)(2,1)S(1)}, bf16[64,768]{1,0:T(8,128)(2,1)S(1)}, u32[]{:S(2)}, u32[]{:S(2)}) collective-permute-start(bf16[64,768]{1,0:T(8,128)(2,1)S(1)} %get-tuple-element.40), channel_id=1, source_target_pairs={{0,20},{4,16},{8,28},{12,24},{16,4},{20,0},{24,12},{28,8},{1,21},{... | collective-permute-start | bytes 294920 | tf_op jit(solution)/shard_map/ppermute | solution.py:244
  12.1 6.4 %collective-permute-start.2 = (bf16[64,768]{1,0:T(8,128)(2,1)S(1)}, bf16[64,768]{1,0:T(8,128)(2,1)S(1)}, u32[]{:S(2)}, u32[]{:S(2)}) collective-permute-start(bf16[64,768]{1,0:T(8,128)(2,1)S(1)} %get-tuple-element.41), channel_id=1, source_target_pairs={{0,16},{4,20},{8,24},{12,28},{16,0},{20,4},{24,8},{28,12},{1,17},{... | collective-permute-start | bytes 294920 | tf_op jit(solution)/shard_map/ppermute | solution.py:244
  18.5 8.8 %collective-permute-start.4 = (bf16[256,384]{1,0:T(8,128)(2,1)S(1)}, bf16[256,384]{1,0:T(8,128)(2,1)S(1)}, u32[]{:S(2)}, u32[]{:S(2)}) collective-permute-start(bf16[256,384]{1,0:T(8,128)(2,1)S(1)} %get-tuple-element.37), channel_id=1, source_target_pairs={{0,8},{8,0},{16,24},{24,16},{1,9},{9,1},{17,25},{25,17},{2,10},{10... | collective-permute-start | bytes 589832 | tf_op jit(solution)/shard_map/ppermute | solution.py:223
  23.1 7.2 %collective-permute-start.8 = (bf16[256,256]{1,0:T(8,128)(2,1)S(1)}, bf16[256,256]{1,0:T(8,128)(2,1)S(1)}, u32[]{:S(2)}, u32[]{:S(2)}) collective-permute-start(bf16[256,256]{1,0:T(8,128)(2,1)S(1)} %add_convert_fusion), channel_id=1, source_target_pairs={{0,20},{4,16},{8,28},{12,24},{16,4},{20,0},{24,12},{28,8},{1,21},{... | collective-permute-start | bytes 393224 | tf_op jit(solution)/shard_map/ppermute | solution.py:219
  24.7 8.6 %collective-permute-start.7 = (bf16[256,256]{1,0:T(8,128)(2,1)S(1)}, bf16[256,256]{1,0:T(8,128)(2,1)S(1)}, u32[]{:S(2)}, u32[]{:S(2)}) collective-permute-start(bf16[256,256]{1,0:T(8,128)(2,1)S(1)} %add_convert_fusion), channel_id=1, source_target_pairs={{0,16},{4,20},{8,24},{12,28},{16,0},{20,4},{24,8},{28,12},{1,17},{... | collective-permute-start | bytes 393224 | tf_op jit(solution)/shard_map/ppermute | solution.py:219
  25.2 8.1 %collective-permute-start.6 = (bf16[256,256]{1,0:T(8,128)(2,1)S(1)}, bf16[256,256]{1,0:T(8,128)(2,1)S(1)}, u32[]{:S(2)}, u32[]{:S(2)}) collective-permute-start(bf16[256,256]{1,0:T(8,128)(2,1)S(1)} %add_convert_fusion), channel_id=1, source_target_pairs={{0,4},{4,0},{8,12},{12,8},{16,20},{20,16},{24,28},{28,24},{1,5},{5... | collective-permute-start | bytes 393224 | tf_op jit(solution)/shard_map/ppermute | solution.py:219
  26.7 13.4 %collective-permute-start.23 = (bf16[384,256]{1,0:T(8,128)(2,1)S(1)}, bf16[384,256]{1,0:T(8,128)(2,1)S(1)}, u32[]{:S(2)}, u32[]{:S(2)}) collective-permute-start(bf16[384,256]{1,0:T(8,128)(2,1)S(1)} %get-tuple-element.43), channel_id=1, source_target_pairs={{0,0},{1,2},{2,1},{3,3},{4,4},{5,6},{6,5},{7,7},{8,8},{9,10},{10,9... | collective-permute-start | bytes 589832 | tf_op jit(solution)/shard_map/ppermute | solution.py:191
  27.4 14.6 %collective-permute-start.22 = (bf16[384,256]{1,0:T(8,128)(2,1)S(1)}, bf16[384,256]{1,0:T(8,128)(2,1)S(1)}, u32[]{:S(2)}, u32[]{:S(2)}) collective-permute-start(bf16[384,256]{1,0:T(8,128)(2,1)S(1)} %collective-permute-done.21), channel_id=1, source_target_pairs={{0,1},{1,0},{2,3},{3,2},{4,5},{5,4},{6,7},{7,6},{8,9},{9,8},{10,11... | collective-permute-start | bytes 589832 | tf_op jit(solution)/shard_map/ppermute | solution.py:194
  30.3 9.4 %collective-permute-start.27 = (bf16[64,256]{1,0:T(8,128)(2,1)S(1)}, bf16[64,256]{1,0:T(8,128)(2,1)S(1)}, u32[]{:S(2)}, u32[]{:S(2)}) collective-permute-start(bf16[64,256]{1,0:T(8,128)(2,1)S(1)} %get-tuple-element.45), channel_id=1, source_target_pairs={{0,3},{1,2},{2,1},{3,0},{4,7},{5,6},{6,5},{7,4},{8,11},{9,10},{10,... | collective-permute-start | bytes 98312 | tf_op jit(solution)/shard_map/ppermute | solution.py:269
  33.3 6.4 %collective-permute-start.26 = (bf16[64,256]{1,0:T(8,128)(2,1)S(1)}, bf16[64,256]{1,0:T(8,128)(2,1)S(1)}, u32[]{:S(2)}, u32[]{:S(2)}) collective-permute-start(bf16[64,256]{1,0:T(8,128)(2,1)S(1)} %get-tuple-element.46), channel_id=1, source_target_pairs={{0,2},{1,3},{2,0},{3,1},{4,6},{5,7},{6,4},{7,5},{8,10},{9,11},{10,... | collective-permute-start | bytes 98312 | tf_op jit(solution)/shard_map/ppermute | solution.py:269
  33.3 6.8 %collective-permute-start.25 = (bf16[64,256]{1,0:T(8,128)(2,1)S(1)}, bf16[64,256]{1,0:T(8,128)(2,1)S(1)}, u32[]{:S(2)}, u32[]{:S(2)}) collective-permute-start(bf16[64,256]{1,0:T(8,128)(2,1)S(1)} %get-tuple-element.47), channel_id=1, source_target_pairs={{0,1},{1,0},{2,3},{3,2},{4,5},{5,4},{6,7},{7,6},{8,9},{9,8},{10,11... | collective-permute-start | bytes 98312 | tf_op jit(solution)/shard_map/ppermute | solution.py:269
  39.7 9.6 %collective-permute-start.20 = (bf16[384,256]{1,0:T(8,128)(2,1)S(1)}, bf16[384,256]{1,0:T(8,128)(2,1)S(1)}, u32[]{:S(2)}, u32[]{:S(2)}) collective-permute-start(bf16[384,256]{1,0:T(8,128)(2,1)S(1)} %get-tuple-element.43), channel_id=1, source_target_pairs={{0,1},{1,0},{2,3},{3,2},{4,5},{5,4},{6,7},{7,6},{8,9},{9,8},{10,11... | collective-permute-start | bytes 589832 | tf_op jit(solution)/shard_map/ppermute | solution.py:191
  39.7 18.0 %collective-permute-start.11 = (bf16[512,384]{1,0:T(8,128)(2,1)S(1)}, bf16[512,384]{1,0:T(8,128)(2,1)S(1)}, u32[]{:S(2)}, u32[]{:S(2)}) collective-permute-start(bf16[512,384]{1,0:T(8,128)(2,1)S(1)} %pad_maximum_fusion.3), channel_id=1, source_target_pairs={{0,2},{1,3},{2,0},{3,1},{4,6},{5,7},{6,4},{7,5},{8,10},{9,11},{10,... | collective-permute-start | bytes 1179656 | tf_op jit(solution)/shard_map/ppermute | solution.py:191
  40.1 11.1 %collective-permute-start.9 = (bf16[4,256,256]{2,1,0:T(8,128)(2,1)S(1)}, bf16[4,256,256]{2,1,0:T(8,128)(2,1)S(1)}, u32[]{:S(2)}, u32[]{:S(2)}) collective-permute-start(bf16[4,256,256]{2,1,0:T(8,128)(2,1)S(1)} %pad_maximum_fusion.1), channel_id=1, source_target_pairs={{0,8},{8,0},{16,24},{24,16},{1,9},{9,1},{17,25},{25,17},{2,10},{10... | collective-permute-start | bytes 1572872 | tf_op jit(solution)/shard_map/ppermute | solution.py:223
  40.1 18.6 %collective-permute-start.10 = (bf16[512,384]{1,0:T(8,128)(2,1)S(1)}, bf16[512,384]{1,0:T(8,128)(2,1)S(1)}, u32[]{:S(2)}, u32[]{:S(2)}) collective-permute-start(bf16[512,384]{1,0:T(8,128)(2,1)S(1)} %pad_maximum_fusion.3), channel_id=1, source_target_pairs={{0,1},{1,0},{2,3},{3,2},{4,5},{5,4},{6,7},{7,6},{8,9},{9,8},{10,11... | collective-permute-start | bytes 1179656 | tf_op jit(solution)/shard_map/ppermute | solution.py:191
  42.0 17.4 %collective-permute-start.13 = (bf16[512,384]{1,0:T(8,128)(2,1)S(1)}, bf16[512,384]{1,0:T(8,128)(2,1)S(1)}, u32[]{:S(2)}, u32[]{:S(2)}) collective-permute-start(bf16[512,384]{1,0:T(8,128)(2,1)S(1)} %pad_maximum_fusion.3), channel_id=1, source_target_pairs={{0,0},{1,2},{2,1},{3,3},{4,4},{5,6},{6,5},{7,7},{8,8},{9,10},{10,9... | collective-permute-start | bytes 1179656 | tf_op jit(solution)/shard_map/ppermute | solution.py:191
  49.3 22.2 %collective-permute-start.30 = (bf16[64,1024]{1,0:T(8,128)(2,1)S(1)}, bf16[64,1024]{1,0:T(8,128)(2,1)S(1)}, u32[]{:S(2)}, u32[]{:S(2)}) collective-permute-start(bf16[64,1024]{1,0:T(8,128)(2,1)S(1)} %pad_maximum_fusion.6.refs_0_), channel_id=1, source_target_pairs={{0,20},{4,16},{8,28},{12,24},{16,4},{20,0},{24,12},{28,8},{1,21},{... | collective-permute-start | bytes 393224 | tf_op jit(solution)/shard_map/ppermute | solution.py:219
  51.2 20.9 %collective-permute-start.29 = (bf16[64,1024]{1,0:T(8,128)(2,1)S(1)}, bf16[64,1024]{1,0:T(8,128)(2,1)S(1)}, u32[]{:S(2)}, u32[]{:S(2)}) collective-permute-start(bf16[64,1024]{1,0:T(8,128)(2,1)S(1)} %pad_maximum_fusion.6.refs_0_), channel_id=1, source_target_pairs={{0,16},{4,20},{8,24},{12,28},{16,0},{20,4},{24,8},{28,12},{1,17},{... | collective-permute-start | bytes 393224 | tf_op jit(solution)/shard_map/ppermute | solution.py:219
  57.7 15.9 %collective-permute-start.24 = (bf16[4,384,256]{2,1,0:T(8,128)(2,1)S(1)}, bf16[4,384,256]{2,1,0:T(8,128)(2,1)S(1)}, u32[]{:S(2)}, u32[]{:S(2)}) collective-permute-start(bf16[4,384,256]{2,1,0:T(8,128)(2,1)S(1)} %pad_maximum_fusion.own_ref), channel_id=1, source_target_pairs={{0,8},{8,0},{16,24},{24,16},{1,9},{9,1},{17,25},{25,17},{2,10},{10... | collective-permute-start | bytes 2359304 | tf_op jit(solution)/shard_map/ppermute | solution.py:223
  58.7 11.0 %collective-permute-start.12 = (bf16[512,384]{1,0:T(8,128)(2,1)S(1)}, bf16[512,384]{1,0:T(8,128)(2,1)S(1)}, u32[]{:S(2)}, u32[]{:S(2)}) collective-permute-start(bf16[512,384]{1,0:T(8,128)(2,1)S(1)} %collective-permute-done.11), channel_id=1, source_target_pairs={{0,1},{1,0},{2,3},{3,2},{4,5},{5,4},{6,7},{7,6},{8,9},{9,8},{10,11... | collective-permute-start | bytes 1179656 | tf_op jit(solution)/shard_map/ppermute | solution.py:194
  59.3 14.3 %collective-permute-start.28 = (bf16[64,1024]{1,0:T(8,128)(2,1)S(1)}, bf16[64,1024]{1,0:T(8,128)(2,1)S(1)}, u32[]{:S(2)}, u32[]{:S(2)}) collective-permute-start(bf16[64,1024]{1,0:T(8,128)(2,1)S(1)} %pad_maximum_fusion.6.refs_0_), channel_id=1, source_target_pairs={{0,4},{4,0},{8,12},{12,8},{16,20},{20,16},{24,28},{28,24},{1,5},{5... | collective-permute-start | bytes 393224 | tf_op jit(solution)/shard_map/ppermute | solution.py:219
  70.0 8.8 %collective-permute-start.16 = (bf16[384,256]{1,0:T(8,128)(2,1)S(1)}, bf16[384,256]{1,0:T(8,128)(2,1)S(1)}, u32[]{:S(2)}, u32[]{:S(2)}) collective-permute-start(bf16[384,256]{1,0:T(8,128)(2,1)S(1)} %fusion.1.refs_0_), channel_id=1, source_target_pairs={{0,20},{4,16},{8,28},{12,24},{16,4},{20,0},{24,12},{28,8},{1,21},{... | collective-permute-start | bytes 589832 | tf_op jit(solution)/shard_map/ppermute | solution.py:219
  71.5 9.6 %collective-permute-start.15 = (bf16[384,256]{1,0:T(8,128)(2,1)S(1)}, bf16[384,256]{1,0:T(8,128)(2,1)S(1)}, u32[]{:S(2)}, u32[]{:S(2)}) collective-permute-start(bf16[384,256]{1,0:T(8,128)(2,1)S(1)} %fusion.1.refs_0_), channel_id=1, source_target_pairs={{0,16},{4,20},{8,24},{12,28},{16,0},{20,4},{24,8},{28,12},{1,17},{... | collective-permute-start | bytes 589832 | tf_op jit(solution)/shard_map/ppermute | solution.py:219
  72.1 9.1 %collective-permute-start.14 = (bf16[384,256]{1,0:T(8,128)(2,1)S(1)}, bf16[384,256]{1,0:T(8,128)(2,1)S(1)}, u32[]{:S(2)}, u32[]{:S(2)}) collective-permute-start(bf16[384,256]{1,0:T(8,128)(2,1)S(1)} %fusion.1.refs_0_), channel_id=1, source_target_pairs={{0,4},{4,0},{8,12},{12,8},{16,20},{20,16},{24,28},{28,24},{1,5},{5... | collective-permute-start | bytes 589832 | tf_op jit(solution)/shard_map/ppermute | solution.py:219
  73.6 8.0 %collective-permute-start.34 = (bf16[384,256]{1,0:T(8,128)(2,1)S(1)}, bf16[384,256]{1,0:T(8,128)(2,1)S(1)}, u32[]{:S(2)}, u32[]{:S(2)}) collective-permute-start(bf16[384,256]{1,0:T(8,128)(2,1)S(1)} %fusion.1.refs_0_), channel_id=1, source_target_pairs={{0,8},{8,0},{16,24},{24,16},{1,9},{9,1},{17,25},{25,17},{2,10},{10... | collective-permute-start | bytes 589832 | tf_op jit(solution)/shard_map/ppermute | solution.py:223
  78.8 10.0 %collective-permute-start.19 = (bf16[384,256]{1,0:T(8,128)(2,1)S(1)}, bf16[384,256]{1,0:T(8,128)(2,1)S(1)}, u32[]{:S(2)}, u32[]{:S(2)}) collective-permute-start(bf16[384,256]{1,0:T(8,128)(2,1)S(1)} %collective-permute-done.16.refs_2_), channel_id=1, source_target_pairs={{0,8},{8,0},{16,24},{24,16},{1,9},{9,1},{17,25},{25,17},{2,10},{10... | collective-permute-start | bytes 589832 | tf_op jit(solution)/shard_map/ppermute | solution.py:223
  81.1 7.7 %collective-permute-start.18 = (bf16[384,256]{1,0:T(8,128)(2,1)S(1)}, bf16[384,256]{1,0:T(8,128)(2,1)S(1)}, u32[]{:S(2)}, u32[]{:S(2)}) collective-permute-start(bf16[384,256]{1,0:T(8,128)(2,1)S(1)} %collective-permute-done.15.refs_1_), channel_id=1, source_target_pairs={{0,8},{8,0},{16,24},{24,16},{1,9},{9,1},{17,25},{25,17},{2,10},{10... | collective-permute-start | bytes 589832 | tf_op jit(solution)/shard_map/ppermute | solution.py:223
  81.2 7.6 %collective-permute-start.17 = (bf16[384,256]{1,0:T(8,128)(2,1)S(1)}, bf16[384,256]{1,0:T(8,128)(2,1)S(1)}, u32[]{:S(2)}, u32[]{:S(2)}) collective-permute-start(bf16[384,256]{1,0:T(8,128)(2,1)S(1)} %collective-permute-done.14.refs_0_), channel_id=1, source_target_pairs={{0,8},{8,0},{16,24},{24,16},{1,9},{9,1},{17,25},{25,17},{2,10},{10... | collective-permute-start | bytes 589832 | tf_op jit(solution)/shard_map/ppermute | solution.py:223
  81.7 6.0 %collective-permute-start.32 = (bf16[64,768]{1,0:T(8,128)(2,1)}, bf16[64,768]{1,0:T(8,128)(2,1)S(1)}, u32[]{:S(2)}, u32[]{:S(2)}) collective-permute-start(bf16[64,768]{1,0:T(8,128)(2,1)} %get-tuple-element.21), channel_id=1, source_target_pairs={{0,16},{4,20},{8,24},{12,28},{16,0},{20,4},{24,8},{28,12},{1,17},{... | collective-permute-start | bytes 294920 | tf_op jit(solution)/shard_map/ppermute | solution.py:296
  (24 other events, 124.6 us)

commit v3 on v2

--- a/solution.py
+++ b/solution.py
@@ -94,32 +94,6 @@
     )(at, q, g, *packs)
 
 
-def input_kernel(cells, own_ref, other_ref, *refs):
-    row_refs, out_refs = refs[:cells], refs[cells:]
-    sub = row_refs[0].shape[0]
-    heads, size, width = own_ref.shape
-    rows = jnp.concatenate([ref[...] for ref in row_refs], axis=0)
-    for j, w_ref in enumerate((own_ref, other_ref)):
-        part = sum(
-            dot(rows[:, r * width : (r + 1) * width], w_ref[r], 1, 1) for r in range(heads)
-        )
-        for o, out_ref in enumerate(out_refs):
-            out_ref[:, j * size : (j + 1) * size] = part[o * sub : (o + 1) * sub].astype(BF16)
-
-
-def input_parts(w_own, w_other, rows):
-    cells, sub, size = len(rows), rows[0].shape[0], w_own.shape[1]
-    return pl.pallas_call(
-        functools.partial(input_kernel, cells),
-        out_shape=[jax.ShapeDtypeStruct((sub, 2 * size), BF16)] * cells,
-        in_specs=[VMEM] * (cells + 2),
-        name="input_grads",
-        cost_estimate=pl.CostEstimate(
-            flops=4 * cells * sub * w_own.size, transcendentals=0, bytes_accessed=4 * w_own.size
-        ),
-    )(w_own, w_other, *rows)
-
-
 def place(at, pieces):
     cells, (sub, slab) = len(pieces), pieces[0].shape
     out = jnp.zeros((sub, slab * cells), BF16)
@@ -267,7 +241,8 @@
     for r in range(1, heads):
         piece = lax.dynamic_slice_in_dim(dkv, (z ^ r) * sub, sub, 0)
         pieces.append(lax.ppermute(piece, "head", swap_pairs(heads, r)))
-    head_rows = cell_gather(jnp.concatenate(pieces, axis=1))
+    pieces = jnp.concatenate(pieces, axis=1)
+    head_rows = cell_gather(pieces)
 
     dkv_own = jnp.stack(cell_gather(dkv))
     dkv_other = core_swap(dkv_own)
@@ -290,8 +265,9 @@
 
     if len(w_slots) > heads:
         w_slots = w_slots[: heads - 1] + [jnp.where(outer, w_slots[heads], w_slots[heads - 1])]
-    w_own = jnp.stack(w_slots)
-    parts = list(input_parts(w_own, core_swap(w_own), head_rows))
+    w_own = jnp.concatenate(w_slots, axis=1)
+    w_both = jnp.concatenate([w_own, core_swap(w_own)], axis=0)
+    parts = [dot(t, w_both, 1, 1).astype(BF16) for t in head_rows]
     for o in far_first(cells):
         parts[o] = lax.ppermute(parts[o], both, swap_pairs(plane, member(o, 0)))
     rest = [i for i in items if i[0]]

time: 93.7 us -> 99.8 us (1.065)
  matrix products: 1.28 us -> 4.32 us
  Pallas kernels: 12.6 us -> 9.67 us
  starting transfers between devices: 33.5 us -> 36.3 us
  waiting for transfers between devices: 38.2 us -> 40 us
    ppermute x9, waiting for transfers between devices: 2.56 us -> 9.07 us  [cell_gather(): got[o] = lax.ppermute(x, both, swap_pairs(plane, member(o, 0)))]
    dot_general x4 -> x8, matrix products: 1.28 us -> 4.32 us  [dot(): lax.dot_general(a, b, (((ca,), (cb,)), ((), ())), preferred_element_type=...]
    pallas_call x1 -> x0, Pallas kernels: 2.92 us -> none  [input_parts(): pl.pallas_call(functools.partial(input_kernel, cells), out_shape=[jax.Sha...]
    ppermute x3, waiting for transfers between devices: 3.12 us -> 0.21 us  [shards(): parts[o] = lax.ppermute(parts[o], both, swap_pairs(plane, member(o, 0)))]
    ppermute x6, waiting for transfers between devices: 13.4 us -> 15.5 us  [line_exchange(): slots[r] = lax.ppermute(x, 'head', pairs)]
    ppermute x3, waiting for transfers between devices: 4.89 us -> 2.91 us  [shards(): pieces.append(lax.ppermute(piece, 'head', swap_pairs(heads, r)))]
    ppermute x6, starting transfers between devices: 6.18 us -> 7.78 us  [line_exchange(): slots[r] = lax.ppermute(x, 'head', pairs)]
    ppermute x1, waiting for transfers between devices: 4.47 us -> 3.05 us  [shards(): terms.append(lax.ppermute(prev_terms[r - 1], 'seq', pairs))]
  transfers between devices with their start and end apart: 35 -> 35, of which waited for: 11 -> 11; matrix products, arithmetic and copies ran while one was open for 4% -> 9% of each run, Pallas kernels for 10% -> 6%
where the time goes in v3:
time: 99.8 us; the launch traced here: 99.4 us
  waiting for transfers between devices  40 us (40%)
  starting transfers between devices  36.3 us (36%)
  Pallas kernels  9.67 us (10%)
  local copies, waits for them, and re-layouts  4.61 us (5%)
  matrix products  4.32 us (4%)
  other arithmetic  3.39 us (3%)
  between operations  1.06 us (1%)
    ppermute x6, waiting for transfers between devices, line_exchange(): slots[r] = lax.ppermute(x, 'head', pairs)  15.5 us
    ppermute x9, starting transfers between devices, cell_gather(): got[o] = lax.ppermute(x, both, swap_pairs(plane, member(o, 0)))  11 us
    ppermute x2, waiting for transfers between devices, line_exchange(): out.append(lax.ppermute(slots[2], 'head', swap_pairs(n, 1)))  9.31 us
    ppermute x9, waiting for transfers between devices, cell_gather(): got[o] = lax.ppermute(x, both, swap_pairs(plane, member(o, 0)))  9.07 us
    ppermute x6, starting transfers between devices, line_exchange(): slots[r] = lax.ppermute(x, 'head', pairs)  7.78 us
    pallas_call x2, Pallas kernels, spread(): pl.pallas_call(functools.partial(spread_kernel, tuple((item[:2] for item...  5.66 us
    ppermute x3, starting transfers between devices, shards(): pieces.append(lax.ppermute(piece, 'head', swap_pairs(heads, r)))  4.45 us
    dot_general x8, matrix products, dot(): lax.dot_general(a, b, (((ca,), (cb,)), ((), ())), preferred_element_type=...  4.32 us
  transfers between devices with their start and end apart: 35, of which 11 were waited for; matrix products, arithmetic and copies ran while one was open for 9% of the time, Pallas kernels for 6%

profile of v3, /device:TPU:0, one launch (start us, length us, event | category | flops | bytes accessed | tf_op | source)
XLA Modules:
  0.0 99.4 jit_solution(13990630528345761915)
XLA Ops:
  2.2 3.0 %collective-permute-start = (bf16[257,256]{1,0:T(8,128)(2,1)S(1)}, bf16[257,256]{1,0:T(8,128)(2,1)S(1)}, u32[]{:S(2)}, u32[]{:S(2)}) collective-permute-start(bf16[257,256]{1,0:T(8,128)(2,1)S(1)} %pad_maximum_fusion.5.refs_0_), channel_id=1, source_target_pairs={{0,4},{4,0},{1,5},{5,1},{2,6},{6,2},{3,7},{7,3},{8,12},{12,8},{9,1... | collective-permute-start | bytes 394760 | tf_op jit(solution)/shard_map/ppermute | solution.py:211
  5.2 1.1 %dynamic-slice_bitcast_fusion.3 = (bf16[64,768]{1,0:T(8,128)(2,1)S(1)}, bf16[64,768]{1,0:T(8,128)(2,1)S(1)}, bf16[64,768]{1,0:T(8,128)(2,1)S(1)}, bf16[64,768]{1,0:T(8,128)(2,1)S(1)}) fusion(bf16[1,64,3072]{2,1,0:T(8,128)(2,1)} %param.13, s32[]{:T(128)S(6)} %select_n.71, s32[]{:T(128)S(6)} %select_n.72, s32[]{:T(128)S(6)} %select_n.74, s32[]{:T(128)S(6)} %select_n.73), kind=kLoop, calls=%fused_computation.36 | loop fusion | bytes 786448 | tf_op jit(solution)/shard_map/dynamic_slice | solution.py:216
  6.5 2.9 %collective-permute-start.3 = (bf16[64,768]{1,0:T(8,128)(2,1)S(1)}, bf16[64,768]{1,0:T(8,128)(2,1)S(1)}, u32[]{:S(2)}, u32[]{:S(2)}) collective-permute-start(bf16[64,768]{1,0:T(8,128)(2,1)S(1)} %get-tuple-element.36), channel_id=1, source_target_pairs={{0,20},{4,16},{8,28},{12,24},{16,4},{20,0},{24,12},{28,8},{1,21},{... | collective-permute-start | bytes 294920 | tf_op jit(solution)/shard_map/ppermute | solution.py:218
  9.9 0.9 constant_dynamic-update-slice_fusion.3
  10.8 0.9 constant_dynamic-update-slice_fusion.2
  13.1 4.3 %collective-permute-start.24 = (bf16[384,256]{1,0:T(8,128)(2,1)S(1)}, bf16[384,256]{1,0:T(8,128)(2,1)S(1)}, u32[]{:S(2)}, u32[]{:S(2)}) collective-permute-start(bf16[384,256]{1,0:T(8,128)(2,1)S(1)} %pad_maximum_fusion.4), channel_id=1, source_target_pairs={{0,2},{1,3},{2,0},{3,1},{4,6},{5,7},{6,4},{7,5},{8,10},{9,11},{10,... | collective-permute-start | bytes 589832 | tf_op jit(solution)/shard_map/ppermute | solution.py:165
  18.2 4.0 %attention.1 = (bf16[256,384]{1,0:T(8,128)(2,1)}, f32[256,256]{1,0:T(8,128)}, bf16[256,256]{1,0:T(8,128)(2,1)}) custom-call(s32[4]{0:T(128)} %pad_add_fusion.at_ref, bf16[256,384]{1,0:T(8,128)(2,1)} %bitcast.50, bf16[256,384]{1,0:T(8,128)(2,1)} %bitcast.51, bf16[257,256]{1,0:T(8,128)(2,1)} %copy-done.8, bf16[257,256]{1,0:T(8,128)(2,1)} %copy-done.12), custom_call_target="tpu_custom_call" | custom-call | flops 503316480 | bytes 786432 | tf_op jit(solution)/shard_map/attention/pallas_call | solution.py:84
  22.9 1.5 %collective-permute-done.23 = bf16[384,256]{1,0:T(8,128)(2,1)S(1)} collective-permute-done((bf16[384,256]{1,0:T(8,128)(2,1)S(1)}, bf16[384,256]{1,0:T(8,128)(2,1)S(1)}, u32[]{:S(2)}, u32[]{:S(2)}) %collective-permute-start.23) | collective-permute-done | bytes 196640 | tf_op jit(solution)/shard_map/ppermute | solution.py:165
  24.4 3.0 %collective-permute-done.5 = bf16[256,256]{1,0:T(8,128)(2,1)S(1)} collective-permute-done((bf16[256,256]{1,0:T(8,128)(2,1)}, bf16[256,256]{1,0:T(8,128)(2,1)S(1)}, u32[]{:S(2)}, u32[]{:S(2)}) %collective-permute-start.5) | collective-permute-done | bytes 131104 | tf_op jit(solution)/shard_map/ppermute | solution.py:237
  27.4 1.0 add_convert_fusion
  28.4 1.6 %collective-permute-start.8 = (bf16[256,256]{1,0:T(8,128)(2,1)S(1)}, bf16[256,256]{1,0:T(8,128)(2,1)S(1)}, u32[]{:S(2)}, u32[]{:S(2)}) collective-permute-start(bf16[256,256]{1,0:T(8,128)(2,1)S(1)} %add_convert_fusion), channel_id=1, source_target_pairs={{0,20},{4,16},{8,28},{12,24},{16,4},{20,0},{24,12},{28,8},{1,21},{... | collective-permute-start | bytes 393224 | tf_op jit(solution)/shard_map/ppermute | solution.py:193
  30.5 1.5 %collective-permute-start.6 = (bf16[256,256]{1,0:T(8,128)(2,1)S(1)}, bf16[256,256]{1,0:T(8,128)(2,1)S(1)}, u32[]{:S(2)}, u32[]{:S(2)}) collective-permute-start(bf16[256,256]{1,0:T(8,128)(2,1)S(1)} %add_convert_fusion), channel_id=1, source_target_pairs={{0,4},{4,0},{8,12},{12,8},{16,20},{20,16},{24,28},{28,24},{1,5},{5... | collective-permute-start | bytes 393224 | tf_op jit(solution)/shard_map/ppermute | solution.py:193
  32.0 2.4 %collective-permute-done.8 = bf16[256,256]{1,0:T(8,128)(2,1)S(1)} collective-permute-done((bf16[256,256]{1,0:T(8,128)(2,1)S(1)}, bf16[256,256]{1,0:T(8,128)(2,1)S(1)}, u32[]{:S(2)}, u32[]{:S(2)}) %collective-permute-start.8) | collective-permute-done | bytes 131104 | tf_op jit(solution)/shard_map/ppermute | solution.py:193
  34.4 1.8 %collective-permute-start.25 = (bf16[384,256]{1,0:T(8,128)(2,1)S(1)}, bf16[384,256]{1,0:T(8,128)(2,1)S(1)}, u32[]{:S(2)}, u32[]{:S(2)}) collective-permute-start(bf16[384,256]{1,0:T(8,128)(2,1)S(1)} %collective-permute-done.24), channel_id=1, source_target_pairs={{0,1},{1,0},{2,3},{3,2},{4,5},{5,4},{6,7},{7,6},{8,9},{9,8},{10,11... | collective-permute-start | bytes 589832 | tf_op jit(solution)/shard_map/ppermute | solution.py:168
  36.3 2.5 %collective-permute-start.22 = (bf16[64,256]{1,0:T(8,128)(2,1)S(1)}, bf16[64,256]{1,0:T(8,128)(2,1)S(1)}, u32[]{:S(2)}, u32[]{:S(2)}) collective-permute-start(bf16[64,256]{1,0:T(8,128)(2,1)S(1)} %get-tuple-element.39), channel_id=1, source_target_pairs={{0,3},{1,2},{2,1},{3,0},{4,7},{5,6},{6,5},{7,4},{8,11},{9,10},{10,... | collective-permute-start | bytes 98312 | tf_op jit(solution)/shard_map/ppermute | solution.py:243
  39.2 1.7 %collective-permute-start.20 = (bf16[64,256]{1,0:T(8,128)(2,1)S(1)}, bf16[64,256]{1,0:T(8,128)(2,1)S(1)}, u32[]{:S(2)}, u32[]{:S(2)}) collective-permute-start(bf16[64,256]{1,0:T(8,128)(2,1)S(1)} %get-tuple-element.41), channel_id=1, source_target_pairs={{0,1},{1,0},{2,3},{3,2},{4,5},{5,4},{6,7},{7,6},{8,9},{9,8},{10,11... | collective-permute-start | bytes 98312 | tf_op jit(solution)/shard_map/ppermute | solution.py:243
  40.8 1.9 %collective-permute-done.22 = bf16[64,256]{1,0:T(8,128)(2,1)S(1)} collective-permute-done((bf16[64,256]{1,0:T(8,128)(2,1)S(1)}, bf16[64,256]{1,0:T(8,128)(2,1)S(1)}, u32[]{:S(2)}, u32[]{:S(2)}) %collective-permute-start.22) | collective-permute-done | bytes 32800 | tf_op jit(solution)/shard_map/ppermute | solution.py:243
  42.8 1.0 collective-permute-done.21
  44.0 1.8 %collective-permute-start.10 = (bf16[512,384]{1,0:T(8,128)(2,1)S(1)}, bf16[512,384]{1,0:T(8,128)(2,1)S(1)}, u32[]{:S(2)}, u32[]{:S(2)}) collective-permute-start(bf16[512,384]{1,0:T(8,128)(2,1)S(1)} %pad_maximum_fusion.3), channel_id=1, source_target_pairs={{0,1},{1,0},{2,3},{3,2},{4,5},{5,4},{6,7},{7,6},{8,9},{9,8},{10,11... | collective-permute-start | bytes 1179656 | tf_op jit(solution)/shard_map/ppermute | solution.py:165
  46.5 1.7 %collective-permute-start.30 = (bf16[64,1024]{1,0:T(8,128)(2,1)S(1)}, bf16[64,1024]{1,0:T(8,128)(2,1)S(1)}, u32[]{:S(2)}, u32[]{:S(2)}) collective-permute-start(bf16[64,1024]{1,0:T(8,128)(2,1)S(1)} %pad_maximum_fusion.6), channel_id=1, source_target_pairs={{0,16},{4,20},{8,24},{12,28},{16,0},{20,4},{24,8},{28,12},{1,17},{... | collective-permute-start | bytes 393224 | tf_op jit(solution)/shard_map/ppermute | solution.py:193
  49.0 14.0 %collective-permute-done.11 = bf16[512,384]{1,0:T(8,128)(2,1)S(1)} collective-permute-done((bf16[512,384]{1,0:T(8,128)(2,1)S(1)}, bf16[512,384]{1,0:T(8,128)(2,1)S(1)}, u32[]{:S(2)}, u32[]{:S(2)}) %collective-permute-start.11) | collective-permute-done | bytes 393248 | tf_op jit(solution)/shard_map/ppermute | solution.py:165
  64.0 1.6 %collective-permute-start.32 = (bf16[64,1024]{1,0:T(8,128)(2,1)S(1)}, bf16[64,1024]{1,0:T(8,128)(2,1)S(1)}, u32[]{:S(2)}, u32[]{:S(2)}) collective-permute-start(bf16[64,1024]{1,0:T(8,128)(2,1)S(1)} %pad_maximum_fusion.6), channel_id=1, source_target_pairs={{0,20},{4,16},{8,28},{12,24},{16,4},{20,0},{24,12},{28,8},{1,21},{... | collective-permute-start | bytes 393224 | tf_op jit(solution)/shard_map/ppermute | solution.py:193
  65.6 9.3 %collective-permute-done.12 = bf16[512,384]{1,0:T(8,128)(2,1)S(1)} collective-permute-done((bf16[512,384]{1,0:T(8,128)(2,1)S(1)}, bf16[512,384]{1,0:T(8,128)(2,1)S(1)}, u32[]{:S(2)}, u32[]{:S(2)}) %collective-permute-start.12) | collective-permute-done | bytes 393248 | tf_op jit(solution)/shard_map/ppermute | solution.py:168
  75.3 1.6 %collective-permute-start.16 = (bf16[384,256]{1,0:T(8,128)(2,1)S(1)}, bf16[384,256]{1,0:T(8,128)(2,1)S(1)}, u32[]{:S(2)}, u32[]{:S(2)}) collective-permute-start(bf16[384,256]{1,0:T(8,128)(2,1)S(1)} %fusion.1.refs_0_), channel_id=1, source_target_pairs={{0,20},{4,16},{8,28},{12,24},{16,4},{20,0},{24,12},{28,8},{1,21},{... | collective-permute-start | bytes 589832 | tf_op jit(solution)/shard_map/ppermute | solution.py:193
  77.9 1.6 %collective-permute-start.14 = (bf16[384,256]{1,0:T(8,128)(2,1)S(1)}, bf16[384,256]{1,0:T(8,128)(2,1)S(1)}, u32[]{:S(2)}, u32[]{:S(2)}) collective-permute-start(bf16[384,256]{1,0:T(8,128)(2,1)S(1)} %fusion.1.refs_0_), channel_id=1, source_target_pairs={{0,4},{4,0},{8,12},{12,8},{16,20},{20,16},{24,28},{28,24},{1,5},{5... | collective-permute-start | bytes 589832 | tf_op jit(solution)/shard_map/ppermute | solution.py:193
  80.2 1.6 %collective-permute-start.33 = (bf16[64,768]{1,0:T(8,128)(2,1)S(1)}, bf16[64,768]{1,0:T(8,128)(2,1)S(1)}, u32[]{:S(2)}, u32[]{:S(2)}) collective-permute-start(bf16[64,768]{1,0:T(8,128)(2,1)S(1)} %convolution_convert_fusion), channel_id=1, source_target_pairs={{0,20},{4,16},{8,28},{12,24},{16,4},{20,0},{24,12},{28,8},{1,21},{... | collective-permute-start | bytes 294920 | tf_op jit(solution)/shard_map/ppermute | solution.py:272
  81.8 2.4 %collective-permute-done.16.refs_2_ = bf16[384,256]{1,0:T(8,128)(2,1)S(1)} collective-permute-done((bf16[384,256]{1,0:T(8,128)(2,1)S(1)}, bf16[384,256]{1,0:T(8,128)(2,1)S(1)}, u32[]{:S(2)}, u32[]{:S(2)}) %collective-permute-start.16) | collective-permute-done | bytes 196640 | tf_op jit(solution)/shard_map/ppermute | solution.py:193
  84.1 4.1 %collective-permute-done.15.refs_1_ = bf16[384,256]{1,0:T(8,128)(2,1)S(1)} collective-permute-done((bf16[384,256]{1,0:T(8,128)(2,1)S(1)}, bf16[384,256]{1,0:T(8,128)(2,1)S(1)}, u32[]{:S(2)}, u32[]{:S(2)}) %collective-permute-start.15) | collective-permute-done | bytes 196640 | tf_op jit(solution)/shard_map/ppermute | solution.py:193
  89.9 1.6 %collective-permute-start.29 = (bf16[64,768]{1,0:T(8,128)(2,1)S(1)}, bf16[64,768]{1,0:T(8,128)(2,1)S(1)}, u32[]{:S(2)}, u32[]{:S(2)}) collective-permute-start(bf16[64,768]{1,0:T(8,128)(2,1)S(1)} %convolution_convert_fusion.2), channel_id=1, source_target_pairs={{0,4},{4,0},{8,12},{12,8},{16,20},{20,16},{24,28},{28,24},{1,5},{5... | collective-permute-start | bytes 294920 | tf_op jit(solution)/shard_map/ppermute | solution.py:272
  91.5 1.2 %convolution_convert_fusion.3.refs_6_ = bf16[64,768]{1,0:T(8,128)(2,1)} fusion(bf16[384,1024]{1,0:T(8,128)(2,1)S(1)} %collective-permute-done.27, bf16[384,1024]{1,0:T(8,128)(2,1)S(1)} %select_dynamic-update-slice_fusion, bf16[64,256]{1,0:T(8,128)(2,1)S(1)} %collective-permute-done.22, bf16[64,256]{1,0:T(8,128)(2,1)S(1)} %collective-permute-done.21, ...), kind=kOutput, calls=%fused_computation.8 | convolution fusion | flops 104382464 | bytes 1802240 | tf_op jit(solution)/shard_map/dot_general | solution.py:20
  92.8 1.9 %shard_map.111 = (f32[3072,128]{1,0:T(8,128)}, f32[3072,128]{1,0:T(8,128)}) custom-call(s32[4]{0:T(128)} %pad_add_fusion.at_ref, bf16[384,256]{1,0:T(8,128)(2,1)} %copy-done.6, bf16[384,256]{1,0:T(8,128)(2,1)} %copy-done.7), custom_call_target="tpu_custom_call" | custom-call | tf_op jit(solution)/shard_map/pallas_call | solution.py:140
  95.7 3.7 %shard_map.112 = (f32[3072,128]{1,0:T(8,128)}, f32[3072,128]{1,0:T(8,128)}, bf16[64,3072]{1,0:T(8,128)(2,1)}) custom-call(s32[4]{0:T(128)} %pad_add_fusion.at_ref, bf16[384,256]{1,0:T(8,128)(2,1)} %copy-done.2, bf16[384,256]{1,0:T(8,128)(2,1)} %copy-done.1, bf16[384,256]{1,0:T(8,128)(2,1)} %copy-done, ...), custom_call_target="tpu_custom_call", output_to_operand_aliasing={{0}: (11, {}), {1}: (12, {})} | custom-call | tf_op jit(solution)/shard_map/pallas_call | solution.py:140
  (94 shorter events, 13.2 us)
Async XLA Ops:
  2.2 15.4 %collective-permute-start = (bf16[257,256]{1,0:T(8,128)(2,1)S(1)}, bf16[257,256]{1,0:T(8,128)(2,1)S(1)}, u32[]{:S(2)}, u32[]{:S(2)}) collective-permute-start(bf16[257,256]{1,0:T(8,128)(2,1)S(1)} %pad_maximum_fusion.5.refs_0_), channel_id=1, source_target_pairs={{0,4},{4,0},{1,5},{5,1},{2,6},{6,2},{3,7},{7,3},{8,12},{12,8},{9,1... | collective-permute-start | bytes 394760 | tf_op jit(solution)/shard_map/ppermute | solution.py:211
  6.3 6.8 %collective-permute-start.1 = (bf16[64,768]{1,0:T(8,128)(2,1)S(1)}, bf16[64,768]{1,0:T(8,128)(2,1)S(1)}, u32[]{:S(2)}, u32[]{:S(2)}) collective-permute-start(bf16[64,768]{1,0:T(8,128)(2,1)S(1)} %get-tuple-element.35), channel_id=1, source_target_pairs={{0,4},{4,0},{8,12},{12,8},{16,20},{20,16},{24,28},{28,24},{1,5},{5... | collective-permute-start | bytes 294920 | tf_op jit(solution)/shard_map/ppermute | solution.py:218
  6.5 10.9 %collective-permute-start.3 = (bf16[64,768]{1,0:T(8,128)(2,1)S(1)}, bf16[64,768]{1,0:T(8,128)(2,1)S(1)}, u32[]{:S(2)}, u32[]{:S(2)}) collective-permute-start(bf16[64,768]{1,0:T(8,128)(2,1)S(1)} %get-tuple-element.36), channel_id=1, source_target_pairs={{0,20},{4,16},{8,28},{12,24},{16,4},{20,0},{24,12},{28,8},{1,21},{... | collective-permute-start | bytes 294920 | tf_op jit(solution)/shard_map/ppermute | solution.py:218
  9.4 8.2 %collective-permute-start.2 = (bf16[64,768]{1,0:T(8,128)(2,1)S(1)}, bf16[64,768]{1,0:T(8,128)(2,1)S(1)}, u32[]{:S(2)}, u32[]{:S(2)}) collective-permute-start(bf16[64,768]{1,0:T(8,128)(2,1)S(1)} %get-tuple-element.37), channel_id=1, source_target_pairs={{0,16},{4,20},{8,24},{12,28},{16,0},{20,4},{24,8},{28,12},{1,17},{... | collective-permute-start | bytes 294920 | tf_op jit(solution)/shard_map/ppermute | solution.py:218
  11.8 34.0 %collective-permute-start.26 = (bf16[384,256]{1,0:T(8,128)(2,1)S(1)}, bf16[384,256]{1,0:T(8,128)(2,1)S(1)}, u32[]{:S(2)}, u32[]{:S(2)}) collective-permute-start(bf16[384,256]{1,0:T(8,128)(2,1)S(1)} %pad_maximum_fusion.4), channel_id=1, source_target_pairs={{0,0},{1,2},{2,1},{3,3},{4,4},{5,6},{6,5},{7,7},{8,8},{9,10},{10,9... | collective-permute-start | bytes 589832 | tf_op jit(solution)/shard_map/ppermute | solution.py:165
  13.1 17.4 %collective-permute-start.24 = (bf16[384,256]{1,0:T(8,128)(2,1)S(1)}, bf16[384,256]{1,0:T(8,128)(2,1)S(1)}, u32[]{:S(2)}, u32[]{:S(2)}) collective-permute-start(bf16[384,256]{1,0:T(8,128)(2,1)S(1)} %pad_maximum_fusion.4), channel_id=1, source_target_pairs={{0,2},{1,3},{2,0},{3,1},{4,6},{5,7},{6,4},{7,5},{8,10},{9,11},{10,... | collective-permute-start | bytes 589832 | tf_op jit(solution)/shard_map/ppermute | solution.py:165
  17.4 7.0 %collective-permute-start.23 = (bf16[384,256]{1,0:T(8,128)(2,1)S(1)}, bf16[384,256]{1,0:T(8,128)(2,1)S(1)}, u32[]{:S(2)}, u32[]{:S(2)}) collective-permute-start(bf16[384,256]{1,0:T(8,128)(2,1)S(1)} %pad_maximum_fusion.4), channel_id=1, source_target_pairs={{0,1},{1,0},{2,3},{3,2},{4,5},{5,4},{6,7},{7,6},{8,9},{9,8},{10,11... | collective-permute-start | bytes 589832 | tf_op jit(solution)/shard_map/ppermute | solution.py:165
  22.3 5.2 %collective-permute-start.5 = (bf16[256,256]{1,0:T(8,128)(2,1)}, bf16[256,256]{1,0:T(8,128)(2,1)S(1)}, u32[]{:S(2)}, u32[]{:S(2)}) collective-permute-start(bf16[256,256]{1,0:T(8,128)(2,1)} %get-tuple-element.14), channel_id=1, source_target_pairs={{0,4},{4,0},{1,5},{5,1},{2,6},{6,2},{3,7},{7,3},{8,12},{12,8},{9,1... | collective-permute-start | bytes 393224 | tf_op jit(solution)/shard_map/ppermute | solution.py:237
  22.8 16.3 %collective-permute-start.4 = (bf16[256,384]{1,0:T(8,128)(2,1)S(1)}, bf16[256,384]{1,0:T(8,128)(2,1)S(1)}, u32[]{:S(2)}, u32[]{:S(2)}) collective-permute-start(bf16[256,384]{1,0:T(8,128)(2,1)S(1)} %get-tuple-element.33), channel_id=1, source_target_pairs={{0,8},{8,0},{16,24},{24,16},{1,9},{9,1},{17,25},{25,17},{2,10},{10... | collective-permute-start | bytes 589832 | tf_op jit(solution)/shard_map/ppermute | solution.py:197
  28.4 6.0 %collective-permute-start.8 = (bf16[256,256]{1,0:T(8,128)(2,1)S(1)}, bf16[256,256]{1,0:T(8,128)(2,1)S(1)}, u32[]{:S(2)}, u32[]{:S(2)}) collective-permute-start(bf16[256,256]{1,0:T(8,128)(2,1)S(1)} %add_convert_fusion), channel_id=1, source_target_pairs={{0,20},{4,16},{8,28},{12,24},{16,4},{20,0},{24,12},{28,8},{1,21},{... | collective-permute-start | bytes 393224 | tf_op jit(solution)/shard_map/ppermute | solution.py:193
  30.0 6.3 %collective-permute-start.7 = (bf16[256,256]{1,0:T(8,128)(2,1)S(1)}, bf16[256,256]{1,0:T(8,128)(2,1)S(1)}, u32[]{:S(2)}, u32[]{:S(2)}) collective-permute-start(bf16[256,256]{1,0:T(8,128)(2,1)S(1)} %add_convert_fusion), channel_id=1, source_target_pairs={{0,16},{4,20},{8,24},{12,28},{16,0},{20,4},{24,8},{28,12},{1,17},{... | collective-permute-start | bytes 393224 | tf_op jit(solution)/shard_map/ppermute | solution.py:193
  30.5 8.3 %collective-permute-start.6 = (bf16[256,256]{1,0:T(8,128)(2,1)S(1)}, bf16[256,256]{1,0:T(8,128)(2,1)S(1)}, u32[]{:S(2)}, u32[]{:S(2)}) collective-permute-start(bf16[256,256]{1,0:T(8,128)(2,1)S(1)} %add_convert_fusion), channel_id=1, source_target_pairs={{0,4},{4,0},{8,12},{12,8},{16,20},{20,16},{24,28},{28,24},{1,5},{5... | collective-permute-start | bytes 393224 | tf_op jit(solution)/shard_map/ppermute | solution.py:193
  34.4 12.0 %collective-permute-start.25 = (bf16[384,256]{1,0:T(8,128)(2,1)S(1)}, bf16[384,256]{1,0:T(8,128)(2,1)S(1)}, u32[]{:S(2)}, u32[]{:S(2)}) collective-permute-start(bf16[384,256]{1,0:T(8,128)(2,1)S(1)} %collective-permute-done.24), channel_id=1, source_target_pairs={{0,1},{1,0},{2,3},{3,2},{4,5},{5,4},{6,7},{7,6},{8,9},{9,8},{10,11... | collective-permute-start | bytes 589832 | tf_op jit(solution)/shard_map/ppermute | solution.py:168
  36.3 6.5 %collective-permute-start.22 = (bf16[64,256]{1,0:T(8,128)(2,1)S(1)}, bf16[64,256]{1,0:T(8,128)(2,1)S(1)}, u32[]{:S(2)}, u32[]{:S(2)}) collective-permute-start(bf16[64,256]{1,0:T(8,128)(2,1)S(1)} %get-tuple-element.39), channel_id=1, source_target_pairs={{0,3},{1,2},{2,1},{3,0},{4,7},{5,6},{6,5},{7,4},{8,11},{9,10},{10,... | collective-permute-start | bytes 98312 | tf_op jit(solution)/shard_map/ppermute | solution.py:243
  42.8 5.5 %collective-permute-start.9 = (bf16[4,256,256]{2,1,0:T(8,128)(2,1)S(1)}, bf16[4,256,256]{2,1,0:T(8,128)(2,1)S(1)}, u32[]{:S(2)}, u32[]{:S(2)}) collective-permute-start(bf16[4,256,256]{2,1,0:T(8,128)(2,1)S(1)} %pad_maximum_fusion.1), channel_id=1, source_target_pairs={{0,8},{8,0},{16,24},{24,16},{1,9},{9,1},{17,25},{25,17},{2,10},{10... | collective-permute-start | bytes 1572872 | tf_op jit(solution)/shard_map/ppermute | solution.py:197
  43.8 19.2 %collective-permute-start.11 = (bf16[512,384]{1,0:T(8,128)(2,1)S(1)}, bf16[512,384]{1,0:T(8,128)(2,1)S(1)}, u32[]{:S(2)}, u32[]{:S(2)}) collective-permute-start(bf16[512,384]{1,0:T(8,128)(2,1)S(1)} %pad_maximum_fusion.3), channel_id=1, source_target_pairs={{0,2},{1,3},{2,0},{3,1},{4,6},{5,7},{6,4},{7,5},{8,10},{9,11},{10,... | collective-permute-start | bytes 1179656 | tf_op jit(solution)/shard_map/ppermute | solution.py:165
  44.0 19.3 %collective-permute-start.10 = (bf16[512,384]{1,0:T(8,128)(2,1)S(1)}, bf16[512,384]{1,0:T(8,128)(2,1)S(1)}, u32[]{:S(2)}, u32[]{:S(2)}) collective-permute-start(bf16[512,384]{1,0:T(8,128)(2,1)S(1)} %pad_maximum_fusion.3), channel_id=1, source_target_pairs={{0,1},{1,0},{2,3},{3,2},{4,5},{5,4},{6,7},{7,6},{8,9},{9,8},{10,11... | collective-permute-start | bytes 1179656 | tf_op jit(solution)/shard_map/ppermute | solution.py:165
  45.8 18.2 %collective-permute-start.13 = (bf16[512,384]{1,0:T(8,128)(2,1)S(1)}, bf16[512,384]{1,0:T(8,128)(2,1)S(1)}, u32[]{:S(2)}, u32[]{:S(2)}) collective-permute-start(bf16[512,384]{1,0:T(8,128)(2,1)S(1)} %pad_maximum_fusion.3), channel_id=1, source_target_pairs={{0,0},{1,2},{2,1},{3,3},{4,4},{5,6},{6,5},{7,7},{8,8},{9,10},{10,9... | collective-permute-start | bytes 1179656 | tf_op jit(solution)/shard_map/ppermute | solution.py:165
  46.5 33.7 %collective-permute-start.30 = (bf16[64,1024]{1,0:T(8,128)(2,1)S(1)}, bf16[64,1024]{1,0:T(8,128)(2,1)S(1)}, u32[]{:S(2)}, u32[]{:S(2)}) collective-permute-start(bf16[64,1024]{1,0:T(8,128)(2,1)S(1)} %pad_maximum_fusion.6), channel_id=1, source_target_pairs={{0,16},{4,20},{8,24},{12,28},{16,0},{20,4},{24,8},{28,12},{1,17},{... | collective-permute-start | bytes 393224 | tf_op jit(solution)/shard_map/ppermute | solution.py:193
  48.3 27.0 %collective-permute-start.28 = (bf16[64,1024]{1,0:T(8,128)(2,1)S(1)}, bf16[64,1024]{1,0:T(8,128)(2,1)S(1)}, u32[]{:S(2)}, u32[]{:S(2)}) collective-permute-start(bf16[64,1024]{1,0:T(8,128)(2,1)S(1)} %pad_maximum_fusion.6), channel_id=1, source_target_pairs={{0,4},{4,0},{8,12},{12,8},{16,20},{20,16},{24,28},{28,24},{1,5},{5... | collective-permute-start | bytes 393224 | tf_op jit(solution)/shard_map/ppermute | solution.py:193
  63.0 13.9 %collective-permute-start.27 = (bf16[384,1024]{1,0:T(8,128)(2,1)S(1)}, bf16[384,1024]{1,0:T(8,128)(2,1)S(1)}, u32[]{:S(2)}, u32[]{:S(2)}) collective-permute-start(bf16[384,1024]{1,0:T(8,128)(2,1)S(1)} %select_dynamic-update-slice_fusion), channel_id=1, source_target_pairs={{0,8},{8,0},{16,24},{24,16},{1,9},{9,1},{17,25},{25,17},{2,10},{10... | collective-permute-start | bytes 2359304 | tf_op jit(solution)/shard_map/ppermute | solution.py:197
  63.3 11.6 %collective-permute-start.12 = (bf16[512,384]{1,0:T(8,128)(2,1)S(1)}, bf16[512,384]{1,0:T(8,128)(2,1)S(1)}, u32[]{:S(2)}, u32[]{:S(2)}) collective-permute-start(bf16[512,384]{1,0:T(8,128)(2,1)S(1)} %collective-permute-done.11), channel_id=1, source_target_pairs={{0,1},{1,0},{2,3},{3,2},{4,5},{5,4},{6,7},{7,6},{8,9},{9,8},{10,11... | collective-permute-start | bytes 1179656 | tf_op jit(solution)/shard_map/ppermute | solution.py:168
  64.0 13.9 %collective-permute-start.32 = (bf16[64,1024]{1,0:T(8,128)(2,1)S(1)}, bf16[64,1024]{1,0:T(8,128)(2,1)S(1)}, u32[]{:S(2)}, u32[]{:S(2)}) collective-permute-start(bf16[64,1024]{1,0:T(8,128)(2,1)S(1)} %pad_maximum_fusion.6), channel_id=1, source_target_pairs={{0,20},{4,16},{8,28},{12,24},{16,4},{20,0},{24,12},{28,8},{1,21},{... | collective-permute-start | bytes 393224 | tf_op jit(solution)/shard_map/ppermute | solution.py:193
  75.2 14.1 %collective-permute-start.34 = (bf16[384,256]{1,0:T(8,128)(2,1)S(1)}, bf16[384,256]{1,0:T(8,128)(2,1)S(1)}, u32[]{:S(2)}, u32[]{:S(2)}) collective-permute-start(bf16[384,256]{1,0:T(8,128)(2,1)S(1)} %fusion.1.refs_0_), channel_id=1, source_target_pairs={{0,8},{8,0},{16,24},{24,16},{1,9},{9,1},{17,25},{25,17},{2,10},{10... | collective-permute-start | bytes 589832 | tf_op jit(solution)/shard_map/ppermute | solution.py:197
  75.3 8.8 %collective-permute-start.16 = (bf16[384,256]{1,0:T(8,128)(2,1)S(1)}, bf16[384,256]{1,0:T(8,128)(2,1)S(1)}, u32[]{:S(2)}, u32[]{:S(2)}) collective-permute-start(bf16[384,256]{1,0:T(8,128)(2,1)S(1)} %fusion.1.refs_0_), channel_id=1, source_target_pairs={{0,20},{4,16},{8,28},{12,24},{16,4},{20,0},{24,12},{28,8},{1,21},{... | collective-permute-start | bytes 589832 | tf_op jit(solution)/shard_map/ppermute | solution.py:193
  76.9 11.3 %collective-permute-start.15 = (bf16[384,256]{1,0:T(8,128)(2,1)S(1)}, bf16[384,256]{1,0:T(8,128)(2,1)S(1)}, u32[]{:S(2)}, u32[]{:S(2)}) collective-permute-start(bf16[384,256]{1,0:T(8,128)(2,1)S(1)} %fusion.1.refs_0_), channel_id=1, source_target_pairs={{0,16},{4,20},{8,24},{12,28},{16,0},{20,4},{24,8},{28,12},{1,17},{... | collective-permute-start | bytes 589832 | tf_op jit(solution)/shard_map/ppermute | solution.py:193
  77.9 10.5 %collective-permute-start.14 = (bf16[384,256]{1,0:T(8,128)(2,1)S(1)}, bf16[384,256]{1,0:T(8,128)(2,1)S(1)}, u32[]{:S(2)}, u32[]{:S(2)}) collective-permute-start(bf16[384,256]{1,0:T(8,128)(2,1)S(1)} %fusion.1.refs_0_), channel_id=1, source_target_pairs={{0,4},{4,0},{8,12},{12,8},{16,20},{20,16},{24,28},{28,24},{1,5},{5... | collective-permute-start | bytes 589832 | tf_op jit(solution)/shard_map/ppermute | solution.py:193
  80.2 9.7 %collective-permute-start.33 = (bf16[64,768]{1,0:T(8,128)(2,1)S(1)}, bf16[64,768]{1,0:T(8,128)(2,1)S(1)}, u32[]{:S(2)}, u32[]{:S(2)}) collective-permute-start(bf16[64,768]{1,0:T(8,128)(2,1)S(1)} %convolution_convert_fusion), channel_id=1, source_target_pairs={{0,20},{4,16},{8,28},{12,24},{16,4},{20,0},{24,12},{28,8},{1,21},{... | collective-permute-start | bytes 294920 | tf_op jit(solution)/shard_map/ppermute | solution.py:272
  84.1 10.7 %collective-permute-start.19 = (bf16[384,256]{1,0:T(8,128)(2,1)S(1)}, bf16[384,256]{1,0:T(8,128)(2,1)S(1)}, u32[]{:S(2)}, u32[]{:S(2)}) collective-permute-start(bf16[384,256]{1,0:T(8,128)(2,1)S(1)} %collective-permute-done.16.refs_2_), channel_id=1, source_target_pairs={{0,8},{8,0},{16,24},{24,16},{1,9},{9,1},{17,25},{25,17},{2,10},{10... | collective-permute-start | bytes 589832 | tf_op jit(solution)/shard_map/ppermute | solution.py:197
  88.2 6.6 %collective-permute-start.18 = (bf16[384,256]{1,0:T(8,128)(2,1)S(1)}, bf16[384,256]{1,0:T(8,128)(2,1)S(1)}, u32[]{:S(2)}, u32[]{:S(2)}) collective-permute-start(bf16[384,256]{1,0:T(8,128)(2,1)S(1)} %collective-permute-done.15.refs_1_), channel_id=1, source_target_pairs={{0,8},{8,0},{16,24},{24,16},{1,9},{9,1},{17,25},{25,17},{2,10},{10... | collective-permute-start | bytes 589832 | tf_op jit(solution)/shard_map/ppermute | solution.py:197
  88.4 6.4 %collective-permute-start.17 = (bf16[384,256]{1,0:T(8,128)(2,1)S(1)}, bf16[384,256]{1,0:T(8,128)(2,1)S(1)}, u32[]{:S(2)}, u32[]{:S(2)}) collective-permute-start(bf16[384,256]{1,0:T(8,128)(2,1)S(1)} %collective-permute-done.14.refs_0_), channel_id=1, source_target_pairs={{0,8},{8,0},{16,24},{24,16},{1,9},{9,1},{17,25},{25,17},{2,10},{10... | collective-permute-start | bytes 589832 | tf_op jit(solution)/shard_map/ppermute | solution.py:197
  89.4 5.4 %collective-permute-start.31 = (bf16[64,768]{1,0:T(8,128)(2,1)S(1)}, bf16[64,768]{1,0:T(8,128)(2,1)S(1)}, u32[]{:S(2)}, u32[]{:S(2)}) collective-permute-start(bf16[64,768]{1,0:T(8,128)(2,1)S(1)} %convolution_convert_fusion.1), channel_id=1, source_target_pairs={{0,16},{4,20},{8,24},{12,28},{16,0},{20,4},{24,8},{28,12},{1,17},{... | collective-permute-start | bytes 294920 | tf_op jit(solution)/shard_map/ppermute | solution.py:272
  (16 other events, 65.0 us)

commit v4 on v3

--- a/solution.py
+++ b/solution.py
@@ -226,7 +226,7 @@
     w_slice = jnp.concatenate(
         [lax.dynamic_slice_in_dim(w, own_slice, size, 0) for w in (key_proj, value_proj)], axis=1
     )
-    w_slots = line_exchange(w_slice)
+    w_slots = line_exchange(lax.optimization_barrier(w_slice))
     x_slots = line_exchange(x_plane)
     at = scalars(z, cell, core, s)
 
@@ -244,7 +244,8 @@
     pieces = jnp.concatenate(pieces, axis=1)
     head_rows = cell_gather(pieces)
 
-    dkv_own = jnp.stack(cell_gather(dkv))
+    gathered = cell_gather(dkv)
+    dkv_own = jnp.stack(gathered)
     dkv_other = core_swap(dkv_own)
     both_rows = []
     for r in range(heads):
@@ -266,7 +267,8 @@
     if len(w_slots) > heads:
         w_slots = w_slots[: heads - 1] + [jnp.where(outer, w_slots[heads], w_slots[heads - 1])]
     w_own = jnp.concatenate(w_slots, axis=1)
-    w_both = jnp.concatenate([w_own, core_swap(w_own)], axis=0)
+    w_other = core_swap(w_own)
+    w_both = jnp.concatenate([w_own, w_other], axis=0)
     parts = [dot(t, w_both, 1, 1).astype(BF16) for t in head_rows]
     for o in far_first(cells):
         parts[o] = lax.ppermute(parts[o], both, swap_pairs(plane, member(o, 0)))

time: 99.8 us -> 94.3 us (0.945)
  waiting for transfers between devices: 40 us -> 37.1 us
    ppermute x9, waiting for transfers between devices: 9.07 us -> 3.71 us  [cell_gather(): got[o] = lax.ppermute(x, both, swap_pairs(plane, member(o, 0)))]
    ppermute x6, waiting for transfers between devices: 15.5 us -> 13.2 us  [line_exchange(): slots[r] = lax.ppermute(x, 'head', pairs)]
    ppermute x3, waiting for transfers between devices: 2.91 us -> 4.88 us  [shards(): pieces.append(lax.ppermute(piece, 'head', swap_pairs(heads, r)))]
    unnamed x30 -> x28, local copies, waits for them, and re-layouts: 3.39 us -> 1.48 us
    ppermute x3, waiting for transfers between devices: 0.21 us -> 2.08 us  [shards(): parts[o] = lax.ppermute(parts[o], both, swap_pairs(plane, member(o, 0)))]
    ppermute x6, starting transfers between devices: 7.78 us -> 6.18 us  [line_exchange(): slots[r] = lax.ppermute(x, 'head', pairs)]
    ppermute x1, waiting for transfers between devices: 3.05 us -> 4.47 us  [shards(): terms.append(lax.ppermute(prev_terms[r - 1], 'seq', pairs))]
  transfers between devices with their start and end apart: 35 -> 35, of which waited for: 11 -> 10; matrix products, arithmetic and copies ran while one was open for 9% -> 8% of each run, Pallas kernels for 6% -> 6%
where the time goes in v4:
time: 94.3 us; the launch traced here: 94 us
  waiting for transfers between devices  37.1 us (39%)
  starting transfers between devices  35.5 us (38%)
  Pallas kernels  9.67 us (10%)
  matrix products  4.33 us (5%)
  local copies, waits for them, and re-layouts  3.63 us (4%)
  other arithmetic  2.66 us (3%)
  between operations  1.05 us (1%)
    ppermute x6, waiting for transfers between devices, line_exchange(): slots[r] = lax.ppermute(x, 'head', pairs)  13.2 us
    ppermute x9, starting transfers between devices, cell_gather(): got[o] = lax.ppermute(x, both, swap_pairs(plane, member(o, 0)))  11.1 us
    ppermute x2, waiting for transfers between devices, line_exchange(): out.append(lax.ppermute(slots[2], 'head', swap_pairs(n, 1)))  8.74 us
    ppermute x6, starting transfers between devices, line_exchange(): slots[r] = lax.ppermute(x, 'head', pairs)  6.18 us
    pallas_call x2, Pallas kernels, spread(): pl.pallas_call(functools.partial(spread_kernel, tuple((item[:2] for item...  5.65 us
    ppermute x3, waiting for transfers between devices, shards(): pieces.append(lax.ppermute(piece, 'head', swap_pairs(heads, r)))  4.88 us
    ppermute x1, waiting for transfers between devices, shards(): terms.append(lax.ppermute(prev_terms[r - 1], 'seq', pairs))  4.47 us
    ppermute x3, starting transfers between devices, shards(): pieces.append(lax.ppermute(piece, 'head', swap_pairs(heads, r)))  4.45 us
  transfers between devices with their start and end apart: 35, of which 10 were waited for; matrix products, arithmetic and copies ran while one was open for 8% of the time, Pallas kernels for 6%

profile of v4, /device:TPU:0, one launch (start us, length us, event | category | flops | bytes accessed | tf_op | source)
XLA Modules:
  0.0 94.0 jit_solution(12207877472935934006)
XLA Ops:
  0.6 0.7 convert_element_type.24
  1.3 0.9 pad_maximum_fusion.6.refs_0_
  2.2 3.0 %collective-permute-start = (bf16[257,256]{1,0:T(8,128)(2,1)S(1)}, bf16[257,256]{1,0:T(8,128)(2,1)S(1)}, u32[]{:S(2)}, u32[]{:S(2)}) collective-permute-start(bf16[257,256]{1,0:T(8,128)(2,1)S(1)} %pad_maximum_fusion.6.refs_0_), channel_id=1, source_target_pairs={{0,4},{4,0},{1,5},{5,1},{2,6},{6,2},{3,7},{7,3},{8,12},{12,8},{9,1... | collective-permute-start | bytes 394760 | tf_op jit(solution)/shard_map/ppermute | solution.py:211
  5.2 1.0 %constant_dynamic-slice_fusion = (bf16[384,128]{1,0:T(8,128)(2,1)S(1)}, bf16[384,128]{1,0:T(8,128)(2,1)S(1)}) fusion(bf16[3072,128]{1,0:T(8,128)(2,1)} %param.15, s32[]{:T(128)S(6)} %select_n.83, bf16[3072,128]{1,0:T(8,128)(2,1)} %param.14), kind=kLoop, calls=%fused_computation.38 | loop fusion | bytes 393220 | tf_op jit(solution)/shard_map/dynamic_slice | solution.py:227
  6.2 2.7 %collective-permute-start.24 = (bf16[384,256]{1,0:T(8,128)(2,1)S(1)}, bf16[384,256]{1,0:T(8,128)(2,1)S(1)}, u32[]{:S(2)}, u32[]{:S(2)}) collective-permute-start(bf16[384,256]{1,0:T(8,128)(2,1)S(1)} %pad_maximum_fusion.5), channel_id=1, source_target_pairs={{0,2},{1,3},{2,0},{3,1},{4,6},{5,7},{6,4},{7,5},{8,10},{9,11},{10,... | collective-permute-start | bytes 589832 | tf_op jit(solution)/shard_map/ppermute | solution.py:165
  8.9 1.1 %dynamic-slice_bitcast_fusion.3 = (bf16[64,768]{1,0:T(8,128)(2,1)S(1)}, bf16[64,768]{1,0:T(8,128)(2,1)S(1)}, bf16[64,768]{1,0:T(8,128)(2,1)S(1)}, bf16[64,768]{1,0:T(8,128)(2,1)S(1)}) fusion(bf16[1,64,3072]{2,1,0:T(8,128)(2,1)} %param.13, s32[]{:T(128)S(6)} %select_n.71, s32[]{:T(128)S(6)} %select_n.72, s32[]{:T(128)S(6)} %select_n.74, s32[]{:T(128)S(6)} %select_n.73), kind=kLoop, calls=%fused_computation.37 | loop fusion | bytes 786448 | tf_op jit(solution)/shard_map/dynamic_slice | solution.py:216
  10.6 2.4 %collective-permute-start.3 = (bf16[64,768]{1,0:T(8,128)(2,1)S(1)}, bf16[64,768]{1,0:T(8,128)(2,1)S(1)}, u32[]{:S(2)}, u32[]{:S(2)}) collective-permute-start(bf16[64,768]{1,0:T(8,128)(2,1)S(1)} %get-tuple-element.32), channel_id=1, source_target_pairs={{0,20},{4,16},{8,28},{12,24},{16,4},{20,0},{24,12},{28,8},{1,21},{... | collective-permute-start | bytes 294920 | tf_op jit(solution)/shard_map/ppermute | solution.py:218
  14.8 4.0 %attention.1 = (bf16[256,384]{1,0:T(8,128)(2,1)}, f32[256,256]{1,0:T(8,128)}, bf16[256,256]{1,0:T(8,128)(2,1)}) custom-call(s32[4]{0:T(128)} %pad_add_fusion.at_ref, bf16[256,384]{1,0:T(8,128)(2,1)} %bitcast.54, bf16[256,384]{1,0:T(8,128)(2,1)} %bitcast.55, bf16[257,256]{1,0:T(8,128)(2,1)} %copy-done.9, bf16[257,256]{1,0:T(8,128)(2,1)} %copy-done.13), custom_call_target="tpu_custom_call" | custom-call | flops 503316480 | bytes 786432 | tf_op jit(solution)/shard_map/attention/pallas_call | solution.py:84
  19.5 4.5 %collective-permute-done.5 = bf16[256,256]{1,0:T(8,128)(2,1)S(1)} collective-permute-done((bf16[256,256]{1,0:T(8,128)(2,1)}, bf16[256,256]{1,0:T(8,128)(2,1)S(1)}, u32[]{:S(2)}, u32[]{:S(2)}) %collective-permute-start.5) | collective-permute-done | bytes 131104 | tf_op jit(solution)/shard_map/ppermute | solution.py:237
  24.0 1.6 %collective-permute-start.8 = (bf16[256,256]{1,0:T(8,128)(2,1)S(1)}, bf16[256,256]{1,0:T(8,128)(2,1)S(1)}, u32[]{:S(2)}, u32[]{:S(2)}) collective-permute-start(bf16[256,256]{1,0:T(8,128)(2,1)S(1)} %add_convert_fusion), channel_id=1, source_target_pairs={{0,20},{4,16},{8,28},{12,24},{16,4},{20,0},{24,12},{28,8},{1,21},{... | collective-permute-start | bytes 393224 | tf_op jit(solution)/shard_map/ppermute | solution.py:193
  26.1 1.5 %collective-permute-start.6 = (bf16[256,256]{1,0:T(8,128)(2,1)S(1)}, bf16[256,256]{1,0:T(8,128)(2,1)S(1)}, u32[]{:S(2)}, u32[]{:S(2)}) collective-permute-start(bf16[256,256]{1,0:T(8,128)(2,1)S(1)} %add_convert_fusion), channel_id=1, source_target_pairs={{0,4},{4,0},{8,12},{12,8},{16,20},{20,16},{24,28},{28,24},{1,5},{5... | collective-permute-start | bytes 393224 | tf_op jit(solution)/shard_map/ppermute | solution.py:193
  28.3 2.9 %collective-permute-start.25 = (bf16[384,256]{1,0:T(8,128)(2,1)S(1)}, bf16[384,256]{1,0:T(8,128)(2,1)S(1)}, u32[]{:S(2)}, u32[]{:S(2)}) collective-permute-start(bf16[384,256]{1,0:T(8,128)(2,1)S(1)} %collective-permute-done.24), channel_id=1, source_target_pairs={{0,1},{1,0},{2,3},{3,2},{4,5},{5,4},{6,7},{7,6},{8,9},{9,8},{10,11... | collective-permute-start | bytes 589832 | tf_op jit(solution)/shard_map/ppermute | solution.py:168
  31.2 3.0 %collective-permute-start.22 = (bf16[64,256]{1,0:T(8,128)(2,1)S(1)}, bf16[64,256]{1,0:T(8,128)(2,1)S(1)}, u32[]{:S(2)}, u32[]{:S(2)}) collective-permute-start(bf16[64,256]{1,0:T(8,128)(2,1)S(1)} %get-tuple-element.35), channel_id=1, source_target_pairs={{0,3},{1,2},{2,1},{3,0},{4,7},{5,6},{6,5},{7,4},{8,11},{9,10},{10,... | collective-permute-start | bytes 98312 | tf_op jit(solution)/shard_map/ppermute | solution.py:243
  34.2 1.5 %collective-permute-start.20 = (bf16[64,256]{1,0:T(8,128)(2,1)S(1)}, bf16[64,256]{1,0:T(8,128)(2,1)S(1)}, u32[]{:S(2)}, u32[]{:S(2)}) collective-permute-start(bf16[64,256]{1,0:T(8,128)(2,1)S(1)} %get-tuple-element.37), channel_id=1, source_target_pairs={{0,1},{1,0},{2,3},{3,2},{4,5},{5,4},{6,7},{7,6},{8,9},{9,8},{10,11... | collective-permute-start | bytes 98312 | tf_op jit(solution)/shard_map/ppermute | solution.py:243
  35.8 4.9 %collective-permute-done.22 = bf16[64,256]{1,0:T(8,128)(2,1)S(1)} collective-permute-done((bf16[64,256]{1,0:T(8,128)(2,1)S(1)}, bf16[64,256]{1,0:T(8,128)(2,1)S(1)}, u32[]{:S(2)}, u32[]{:S(2)}) %collective-permute-start.22) | collective-permute-done | bytes 32800 | tf_op jit(solution)/shard_map/ppermute | solution.py:243
  41.0 1.9 %collective-permute-start.10 = (bf16[512,384]{1,0:T(8,128)(2,1)S(1)}, bf16[512,384]{1,0:T(8,128)(2,1)S(1)}, u32[]{:S(2)}, u32[]{:S(2)}) collective-permute-start(bf16[512,384]{1,0:T(8,128)(2,1)S(1)} %pad_maximum_fusion.4), channel_id=1, source_target_pairs={{0,1},{1,0},{2,3},{3,2},{4,5},{5,4},{6,7},{7,6},{8,9},{9,8},{10,11... | collective-permute-start | bytes 1179656 | tf_op jit(solution)/shard_map/ppermute | solution.py:165
  42.9 0.7 collective-permute-start.13
  43.6 6.7 %collective-permute-done.23 = bf16[384,256]{1,0:T(8,128)(2,1)S(1)} collective-permute-done((bf16[384,256]{1,0:T(8,128)(2,1)S(1)}, bf16[384,256]{1,0:T(8,128)(2,1)S(1)}, u32[]{:S(2)}, u32[]{:S(2)}) %collective-permute-start.23) | collective-permute-done | bytes 196640 | tf_op jit(solution)/shard_map/ppermute | solution.py:165
  50.2 1.7 %collective-permute-start.30 = (bf16[64,1024]{1,0:T(8,128)(2,1)S(1)}, bf16[64,1024]{1,0:T(8,128)(2,1)S(1)}, u32[]{:S(2)}, u32[]{:S(2)}) collective-permute-start(bf16[64,1024]{1,0:T(8,128)(2,1)S(1)} %pad_maximum_fusion.7), channel_id=1, source_target_pairs={{0,16},{4,20},{8,24},{12,28},{16,0},{20,4},{24,8},{28,12},{1,17},{... | collective-permute-start | bytes 393224 | tf_op jit(solution)/shard_map/ppermute | solution.py:193
  52.7 6.0 %collective-permute-done.11 = bf16[512,384]{1,0:T(8,128)(2,1)S(1)} collective-permute-done((bf16[512,384]{1,0:T(8,128)(2,1)S(1)}, bf16[512,384]{1,0:T(8,128)(2,1)S(1)}, u32[]{:S(2)}, u32[]{:S(2)}) %collective-permute-start.11) | collective-permute-done | bytes 393248 | tf_op jit(solution)/shard_map/ppermute | solution.py:165
  60.2 1.6 %collective-permute-start.32 = (bf16[64,1024]{1,0:T(8,128)(2,1)S(1)}, bf16[64,1024]{1,0:T(8,128)(2,1)S(1)}, u32[]{:S(2)}, u32[]{:S(2)}) collective-permute-start(bf16[64,1024]{1,0:T(8,128)(2,1)S(1)} %pad_maximum_fusion.7), channel_id=1, source_target_pairs={{0,20},{4,16},{8,28},{12,24},{16,4},{20,0},{24,12},{28,8},{1,21},{... | collective-permute-start | bytes 393224 | tf_op jit(solution)/shard_map/ppermute | solution.py:193
  61.9 8.7 %collective-permute-done.12 = bf16[512,384]{1,0:T(8,128)(2,1)S(1)} collective-permute-done((bf16[512,384]{1,0:T(8,128)(2,1)S(1)}, bf16[512,384]{1,0:T(8,128)(2,1)S(1)}, u32[]{:S(2)}, u32[]{:S(2)}) %collective-permute-start.12) | collective-permute-done | bytes 393248 | tf_op jit(solution)/shard_map/ppermute | solution.py:168
  71.0 1.5 %collective-permute-start.16 = (bf16[384,256]{1,0:T(8,128)(2,1)S(1)}, bf16[384,256]{1,0:T(8,128)(2,1)S(1)}, u32[]{:S(2)}, u32[]{:S(2)}) collective-permute-start(bf16[384,256]{1,0:T(8,128)(2,1)S(1)} %fusion.1.refs_0_), channel_id=1, source_target_pairs={{0,20},{4,16},{8,28},{12,24},{16,4},{20,0},{24,12},{28,8},{1,21},{... | collective-permute-start | bytes 589832 | tf_op jit(solution)/shard_map/ppermute | solution.py:193
  74.0 1.6 %collective-permute-start.14 = (bf16[384,256]{1,0:T(8,128)(2,1)S(1)}, bf16[384,256]{1,0:T(8,128)(2,1)S(1)}, u32[]{:S(2)}, u32[]{:S(2)}) collective-permute-start(bf16[384,256]{1,0:T(8,128)(2,1)S(1)} %fusion.1.refs_0_), channel_id=1, source_target_pairs={{0,4},{4,0},{8,12},{12,8},{16,20},{20,16},{24,28},{28,24},{1,5},{5... | collective-permute-start | bytes 589832 | tf_op jit(solution)/shard_map/ppermute | solution.py:193
  77.3 1.5 %collective-permute-start.31 = (bf16[64,768]{1,0:T(8,128)(2,1)S(1)}, bf16[64,768]{1,0:T(8,128)(2,1)S(1)}, u32[]{:S(2)}, u32[]{:S(2)}) collective-permute-start(bf16[64,768]{1,0:T(8,128)(2,1)S(1)} %convolution_convert_fusion.1), channel_id=1, source_target_pairs={{0,16},{4,20},{8,24},{12,28},{16,0},{20,4},{24,8},{28,12},{1,17},{... | collective-permute-start | bytes 294920 | tf_op jit(solution)/shard_map/ppermute | solution.py:274
  78.9 0.9 %collective-permute-done.16.refs_2_ = bf16[384,256]{1,0:T(8,128)(2,1)S(1)} collective-permute-done((bf16[384,256]{1,0:T(8,128)(2,1)S(1)}, bf16[384,256]{1,0:T(8,128)(2,1)S(1)}, u32[]{:S(2)}, u32[]{:S(2)}) %collective-permute-start.16) | collective-permute-done | bytes 196640 | tf_op jit(solution)/shard_map/ppermute | solution.py:193
  79.8 1.4 %collective-permute-start.33 = (bf16[64,768]{1,0:T(8,128)(2,1)S(1)}, bf16[64,768]{1,0:T(8,128)(2,1)S(1)}, u32[]{:S(2)}, u32[]{:S(2)}) collective-permute-start(bf16[64,768]{1,0:T(8,128)(2,1)S(1)} %convolution_convert_fusion), channel_id=1, source_target_pairs={{0,20},{4,16},{8,28},{12,24},{16,4},{20,0},{24,12},{28,8},{1,21},{... | collective-permute-start | bytes 294920 | tf_op jit(solution)/shard_map/ppermute | solution.py:274
  81.3 2.3 %collective-permute-done.15.refs_1_ = bf16[384,256]{1,0:T(8,128)(2,1)S(1)} collective-permute-done((bf16[384,256]{1,0:T(8,128)(2,1)S(1)}, bf16[384,256]{1,0:T(8,128)(2,1)S(1)}, u32[]{:S(2)}, u32[]{:S(2)}) %collective-permute-start.15) | collective-permute-done | bytes 196640 | tf_op jit(solution)/shard_map/ppermute | solution.py:193
  84.0 2.1 %collective-permute-done.29.refs_7_ = bf16[64,768]{1,0:T(8,128)(2,1)S(1)} collective-permute-done((bf16[64,768]{1,0:T(8,128)(2,1)S(1)}, bf16[64,768]{1,0:T(8,128)(2,1)S(1)}, u32[]{:S(2)}, u32[]{:S(2)}) %collective-permute-start.29) | collective-permute-done | bytes 98336 | tf_op jit(solution)/shard_map/ppermute | solution.py:274
  86.1 1.2 %convolution_convert_fusion.3.refs_6_ = bf16[64,768]{1,0:T(8,128)(2,1)} fusion(bf16[768,1024]{1,0:T(8,128)(2,1)S(1)} %pad_maximum_fusion, bf16[64,256]{1,0:T(8,128)(2,1)S(1)} %collective-permute-done.22, bf16[64,256]{1,0:T(8,128)(2,1)S(1)} %collective-permute-done.21, bf16[64,256]{1,0:T(8,128)(2,1)S(1)} %collective-permute-done.20, ...), kind=kOutput, calls=%fused_computation.8 | convolution fusion | flops 101236736 | bytes 1802240 | tf_op jit(solution)/shard_map/dot_general | solution.py:20
  87.4 1.9 %shard_map.111 = (f32[3072,128]{1,0:T(8,128)}, f32[3072,128]{1,0:T(8,128)}) custom-call(s32[4]{0:T(128)} %pad_add_fusion.at_ref, bf16[384,256]{1,0:T(8,128)(2,1)} %copy-done.7, bf16[384,256]{1,0:T(8,128)(2,1)} %copy-done.8), custom_call_target="tpu_custom_call" | custom-call | tf_op jit(solution)/shard_map/pallas_call | solution.py:140
  90.3 3.7 %shard_map.112 = (f32[3072,128]{1,0:T(8,128)}, f32[3072,128]{1,0:T(8,128)}, bf16[64,3072]{1,0:T(8,128)(2,1)}) custom-call(s32[4]{0:T(128)} %pad_add_fusion.at_ref, bf16[384,256]{1,0:T(8,128)(2,1)} %copy-done.3, bf16[384,256]{1,0:T(8,128)(2,1)} %copy-done.2, bf16[384,256]{1,0:T(8,128)(2,1)} %copy-done.1, ...), custom_call_target="tpu_custom_call", output_to_operand_aliasing={{0}: (11, {}), {1}: (12, {})} | custom-call | tf_op jit(solution)/shard_map/pallas_call | solution.py:140
  (95 shorter events, 11.9 us)
Async XLA Ops:
  2.2 11.9 %collective-permute-start = (bf16[257,256]{1,0:T(8,128)(2,1)S(1)}, bf16[257,256]{1,0:T(8,128)(2,1)S(1)}, u32[]{:S(2)}, u32[]{:S(2)}) collective-permute-start(bf16[257,256]{1,0:T(8,128)(2,1)S(1)} %pad_maximum_fusion.6.refs_0_), channel_id=1, source_target_pairs={{0,4},{4,0},{1,5},{5,1},{2,6},{6,2},{3,7},{7,3},{8,12},{12,8},{9,1... | collective-permute-start | bytes 394760 | tf_op jit(solution)/shard_map/ppermute | solution.py:211
  6.2 21.4 %collective-permute-start.24 = (bf16[384,256]{1,0:T(8,128)(2,1)S(1)}, bf16[384,256]{1,0:T(8,128)(2,1)S(1)}, u32[]{:S(2)}, u32[]{:S(2)}) collective-permute-start(bf16[384,256]{1,0:T(8,128)(2,1)S(1)} %pad_maximum_fusion.5), channel_id=1, source_target_pairs={{0,2},{1,3},{2,0},{3,1},{4,6},{5,7},{6,4},{7,5},{8,10},{9,11},{10,... | collective-permute-start | bytes 589832 | tf_op jit(solution)/shard_map/ppermute | solution.py:165
  10.0 9.4 %collective-permute-start.1 = (bf16[64,768]{1,0:T(8,128)(2,1)S(1)}, bf16[64,768]{1,0:T(8,128)(2,1)S(1)}, u32[]{:S(2)}, u32[]{:S(2)}) collective-permute-start(bf16[64,768]{1,0:T(8,128)(2,1)S(1)} %get-tuple-element.31), channel_id=1, source_target_pairs={{0,4},{4,0},{8,12},{12,8},{16,20},{20,16},{24,28},{28,24},{1,5},{5... | collective-permute-start | bytes 294920 | tf_op jit(solution)/shard_map/ppermute | solution.py:218
  10.6 8.8 %collective-permute-start.3 = (bf16[64,768]{1,0:T(8,128)(2,1)S(1)}, bf16[64,768]{1,0:T(8,128)(2,1)S(1)}, u32[]{:S(2)}, u32[]{:S(2)}) collective-permute-start(bf16[64,768]{1,0:T(8,128)(2,1)S(1)} %get-tuple-element.32), channel_id=1, source_target_pairs={{0,20},{4,16},{8,28},{12,24},{16,4},{20,0},{24,12},{28,8},{1,21},{... | collective-permute-start | bytes 294920 | tf_op jit(solution)/shard_map/ppermute | solution.py:218
  13.0 6.3 %collective-permute-start.2 = (bf16[64,768]{1,0:T(8,128)(2,1)S(1)}, bf16[64,768]{1,0:T(8,128)(2,1)S(1)}, u32[]{:S(2)}, u32[]{:S(2)}) collective-permute-start(bf16[64,768]{1,0:T(8,128)(2,1)S(1)} %get-tuple-element.33), channel_id=1, source_target_pairs={{0,16},{4,20},{8,24},{12,28},{16,0},{20,4},{24,8},{28,12},{1,17},{... | collective-permute-start | bytes 294920 | tf_op jit(solution)/shard_map/ppermute | solution.py:218
  19.4 8.8 %collective-permute-start.4 = (bf16[256,384]{1,0:T(8,128)(2,1)S(1)}, bf16[256,384]{1,0:T(8,128)(2,1)S(1)}, u32[]{:S(2)}, u32[]{:S(2)}) collective-permute-start(bf16[256,384]{1,0:T(8,128)(2,1)S(1)} %get-tuple-element.29), channel_id=1, source_target_pairs={{0,8},{8,0},{16,24},{24,16},{1,9},{9,1},{17,25},{25,17},{2,10},{10... | collective-permute-start | bytes 589832 | tf_op jit(solution)/shard_map/ppermute | solution.py:197
  24.0 7.2 %collective-permute-start.8 = (bf16[256,256]{1,0:T(8,128)(2,1)S(1)}, bf16[256,256]{1,0:T(8,128)(2,1)S(1)}, u32[]{:S(2)}, u32[]{:S(2)}) collective-permute-start(bf16[256,256]{1,0:T(8,128)(2,1)S(1)} %add_convert_fusion), channel_id=1, source_target_pairs={{0,20},{4,16},{8,28},{12,24},{16,4},{20,0},{24,12},{28,8},{1,21},{... | collective-permute-start | bytes 393224 | tf_op jit(solution)/shard_map/ppermute | solution.py:193
  25.6 8.6 %collective-permute-start.7 = (bf16[256,256]{1,0:T(8,128)(2,1)S(1)}, bf16[256,256]{1,0:T(8,128)(2,1)S(1)}, u32[]{:S(2)}, u32[]{:S(2)}) collective-permute-start(bf16[256,256]{1,0:T(8,128)(2,1)S(1)} %add_convert_fusion), channel_id=1, source_target_pairs={{0,16},{4,20},{8,24},{12,28},{16,0},{20,4},{24,8},{28,12},{1,17},{... | collective-permute-start | bytes 393224 | tf_op jit(solution)/shard_map/ppermute | solution.py:193
  26.1 8.1 %collective-permute-start.6 = (bf16[256,256]{1,0:T(8,128)(2,1)S(1)}, bf16[256,256]{1,0:T(8,128)(2,1)S(1)}, u32[]{:S(2)}, u32[]{:S(2)}) collective-permute-start(bf16[256,256]{1,0:T(8,128)(2,1)S(1)} %add_convert_fusion), channel_id=1, source_target_pairs={{0,4},{4,0},{8,12},{12,8},{16,20},{20,16},{24,28},{28,24},{1,5},{5... | collective-permute-start | bytes 393224 | tf_op jit(solution)/shard_map/ppermute | solution.py:193
  27.6 13.4 %collective-permute-start.26 = (bf16[384,256]{1,0:T(8,128)(2,1)S(1)}, bf16[384,256]{1,0:T(8,128)(2,1)S(1)}, u32[]{:S(2)}, u32[]{:S(2)}) collective-permute-start(bf16[384,256]{1,0:T(8,128)(2,1)S(1)} %pad_maximum_fusion.5), channel_id=1, source_target_pairs={{0,0},{1,2},{2,1},{3,3},{4,4},{5,6},{6,5},{7,7},{8,8},{9,10},{10,9... | collective-permute-start | bytes 589832 | tf_op jit(solution)/shard_map/ppermute | solution.py:165
  28.3 14.6 %collective-permute-start.25 = (bf16[384,256]{1,0:T(8,128)(2,1)S(1)}, bf16[384,256]{1,0:T(8,128)(2,1)S(1)}, u32[]{:S(2)}, u32[]{:S(2)}) collective-permute-start(bf16[384,256]{1,0:T(8,128)(2,1)S(1)} %collective-permute-done.24), channel_id=1, source_target_pairs={{0,1},{1,0},{2,3},{3,2},{4,5},{5,4},{6,7},{7,6},{8,9},{9,8},{10,11... | collective-permute-start | bytes 589832 | tf_op jit(solution)/shard_map/ppermute | solution.py:168
  31.2 9.4 %collective-permute-start.22 = (bf16[64,256]{1,0:T(8,128)(2,1)S(1)}, bf16[64,256]{1,0:T(8,128)(2,1)S(1)}, u32[]{:S(2)}, u32[]{:S(2)}) collective-permute-start(bf16[64,256]{1,0:T(8,128)(2,1)S(1)} %get-tuple-element.35), channel_id=1, source_target_pairs={{0,3},{1,2},{2,1},{3,0},{4,7},{5,6},{6,5},{7,4},{8,11},{9,10},{10,... | collective-permute-start | bytes 98312 | tf_op jit(solution)/shard_map/ppermute | solution.py:243
  34.2 6.4 %collective-permute-start.21 = (bf16[64,256]{1,0:T(8,128)(2,1)S(1)}, bf16[64,256]{1,0:T(8,128)(2,1)S(1)}, u32[]{:S(2)}, u32[]{:S(2)}) collective-permute-start(bf16[64,256]{1,0:T(8,128)(2,1)S(1)} %get-tuple-element.36), channel_id=1, source_target_pairs={{0,2},{1,3},{2,0},{3,1},{4,6},{5,7},{6,4},{7,5},{8,10},{9,11},{10,... | collective-permute-start | bytes 98312 | tf_op jit(solution)/shard_map/ppermute | solution.py:243
  34.2 6.8 %collective-permute-start.20 = (bf16[64,256]{1,0:T(8,128)(2,1)S(1)}, bf16[64,256]{1,0:T(8,128)(2,1)S(1)}, u32[]{:S(2)}, u32[]{:S(2)}) collective-permute-start(bf16[64,256]{1,0:T(8,128)(2,1)S(1)} %get-tuple-element.37), channel_id=1, source_target_pairs={{0,1},{1,0},{2,3},{3,2},{4,5},{5,4},{6,7},{7,6},{8,9},{9,8},{10,11... | collective-permute-start | bytes 98312 | tf_op jit(solution)/shard_map/ppermute | solution.py:243
  40.6 9.6 %collective-permute-start.23 = (bf16[384,256]{1,0:T(8,128)(2,1)S(1)}, bf16[384,256]{1,0:T(8,128)(2,1)S(1)}, u32[]{:S(2)}, u32[]{:S(2)}) collective-permute-start(bf16[384,256]{1,0:T(8,128)(2,1)S(1)} %pad_maximum_fusion.5), channel_id=1, source_target_pairs={{0,1},{1,0},{2,3},{3,2},{4,5},{5,4},{6,7},{7,6},{8,9},{9,8},{10,11... | collective-permute-start | bytes 589832 | tf_op jit(solution)/shard_map/ppermute | solution.py:165
  40.6 18.0 %collective-permute-start.11 = (bf16[512,384]{1,0:T(8,128)(2,1)S(1)}, bf16[512,384]{1,0:T(8,128)(2,1)S(1)}, u32[]{:S(2)}, u32[]{:S(2)}) collective-permute-start(bf16[512,384]{1,0:T(8,128)(2,1)S(1)} %pad_maximum_fusion.4), channel_id=1, source_target_pairs={{0,2},{1,3},{2,0},{3,1},{4,6},{5,7},{6,4},{7,5},{8,10},{9,11},{10,... | collective-permute-start | bytes 1179656 | tf_op jit(solution)/shard_map/ppermute | solution.py:165
  41.0 11.1 %collective-permute-start.9 = (bf16[4,256,256]{2,1,0:T(8,128)(2,1)S(1)}, bf16[4,256,256]{2,1,0:T(8,128)(2,1)S(1)}, u32[]{:S(2)}, u32[]{:S(2)}) collective-permute-start(bf16[4,256,256]{2,1,0:T(8,128)(2,1)S(1)} %pad_maximum_fusion.2), channel_id=1, source_target_pairs={{0,8},{8,0},{16,24},{24,16},{1,9},{9,1},{17,25},{25,17},{2,10},{10... | collective-permute-start | bytes 1572872 | tf_op jit(solution)/shard_map/ppermute | solution.py:197
  41.0 18.6 %collective-permute-start.10 = (bf16[512,384]{1,0:T(8,128)(2,1)S(1)}, bf16[512,384]{1,0:T(8,128)(2,1)S(1)}, u32[]{:S(2)}, u32[]{:S(2)}) collective-permute-start(bf16[512,384]{1,0:T(8,128)(2,1)S(1)} %pad_maximum_fusion.4), channel_id=1, source_target_pairs={{0,1},{1,0},{2,3},{3,2},{4,5},{5,4},{6,7},{7,6},{8,9},{9,8},{10,11... | collective-permute-start | bytes 1179656 | tf_op jit(solution)/shard_map/ppermute | solution.py:165
  42.9 17.4 %collective-permute-start.13 = (bf16[512,384]{1,0:T(8,128)(2,1)S(1)}, bf16[512,384]{1,0:T(8,128)(2,1)S(1)}, u32[]{:S(2)}, u32[]{:S(2)}) collective-permute-start(bf16[512,384]{1,0:T(8,128)(2,1)S(1)} %pad_maximum_fusion.4), channel_id=1, source_target_pairs={{0,0},{1,2},{2,1},{3,3},{4,4},{5,6},{6,5},{7,7},{8,8},{9,10},{10,9... | collective-permute-start | bytes 1179656 | tf_op jit(solution)/shard_map/ppermute | solution.py:165
  50.2 25.9 %collective-permute-start.30 = (bf16[64,1024]{1,0:T(8,128)(2,1)S(1)}, bf16[64,1024]{1,0:T(8,128)(2,1)S(1)}, u32[]{:S(2)}, u32[]{:S(2)}) collective-permute-start(bf16[64,1024]{1,0:T(8,128)(2,1)S(1)} %pad_maximum_fusion.7), channel_id=1, source_target_pairs={{0,16},{4,20},{8,24},{12,28},{16,0},{20,4},{24,8},{28,12},{1,17},{... | collective-permute-start | bytes 393224 | tf_op jit(solution)/shard_map/ppermute | solution.py:193
  52.1 21.8 %collective-permute-start.28 = (bf16[64,1024]{1,0:T(8,128)(2,1)S(1)}, bf16[64,1024]{1,0:T(8,128)(2,1)S(1)}, u32[]{:S(2)}, u32[]{:S(2)}) collective-permute-start(bf16[64,1024]{1,0:T(8,128)(2,1)S(1)} %pad_maximum_fusion.7), channel_id=1, source_target_pairs={{0,4},{4,0},{8,12},{12,8},{16,20},{20,16},{24,28},{28,24},{1,5},{5... | collective-permute-start | bytes 393224 | tf_op jit(solution)/shard_map/ppermute | solution.py:193
  58.7 12.4 %collective-permute-start.27 = (bf16[384,1024]{1,0:T(8,128)(2,1)S(1)}, bf16[384,1024]{1,0:T(8,128)(2,1)S(1)}, u32[]{:S(2)}, u32[]{:S(2)}) collective-permute-start(bf16[384,1024]{1,0:T(8,128)(2,1)S(1)} %pad_maximum_fusion.1), channel_id=1, source_target_pairs={{0,8},{8,0},{16,24},{24,16},{1,9},{9,1},{17,25},{25,17},{2,10},{10... | collective-permute-start | bytes 2359304 | tf_op jit(solution)/shard_map/ppermute | solution.py:197
  59.6 11.0 %collective-permute-start.12 = (bf16[512,384]{1,0:T(8,128)(2,1)S(1)}, bf16[512,384]{1,0:T(8,128)(2,1)S(1)}, u32[]{:S(2)}, u32[]{:S(2)}) collective-permute-start(bf16[512,384]{1,0:T(8,128)(2,1)S(1)} %collective-permute-done.11), channel_id=1, source_target_pairs={{0,1},{1,0},{2,3},{3,2},{4,5},{5,4},{6,7},{7,6},{8,9},{9,8},{10,11... | collective-permute-start | bytes 1179656 | tf_op jit(solution)/shard_map/ppermute | solution.py:168
  60.2 12.5 %collective-permute-start.32 = (bf16[64,1024]{1,0:T(8,128)(2,1)S(1)}, bf16[64,1024]{1,0:T(8,128)(2,1)S(1)}, u32[]{:S(2)}, u32[]{:S(2)}) collective-permute-start(bf16[64,1024]{1,0:T(8,128)(2,1)S(1)} %pad_maximum_fusion.7), channel_id=1, source_target_pairs={{0,20},{4,16},{8,28},{12,24},{16,4},{20,0},{24,12},{28,8},{1,21},{... | collective-permute-start | bytes 393224 | tf_op jit(solution)/shard_map/ppermute | solution.py:193
  71.0 6.4 %collective-permute-start.34 = (bf16[384,256]{1,0:T(8,128)(2,1)S(1)}, bf16[384,256]{1,0:T(8,128)(2,1)S(1)}, u32[]{:S(2)}, u32[]{:S(2)}) collective-permute-start(bf16[384,256]{1,0:T(8,128)(2,1)S(1)} %fusion.1.refs_0_), channel_id=1, source_target_pairs={{0,8},{8,0},{16,24},{24,16},{1,9},{9,1},{17,25},{25,17},{2,10},{10... | collective-permute-start | bytes 589832 | tf_op jit(solution)/shard_map/ppermute | solution.py:197
  71.0 8.8 %collective-permute-start.16 = (bf16[384,256]{1,0:T(8,128)(2,1)S(1)}, bf16[384,256]{1,0:T(8,128)(2,1)S(1)}, u32[]{:S(2)}, u32[]{:S(2)}) collective-permute-start(bf16[384,256]{1,0:T(8,128)(2,1)S(1)} %fusion.1.refs_0_), channel_id=1, source_target_pairs={{0,20},{4,16},{8,28},{12,24},{16,4},{20,0},{24,12},{28,8},{1,21},{... | collective-permute-start | bytes 589832 | tf_op jit(solution)/shard_map/ppermute | solution.py:193
  72.7 10.8 %collective-permute-start.15 = (bf16[384,256]{1,0:T(8,128)(2,1)S(1)}, bf16[384,256]{1,0:T(8,128)(2,1)S(1)}, u32[]{:S(2)}, u32[]{:S(2)}) collective-permute-start(bf16[384,256]{1,0:T(8,128)(2,1)S(1)} %fusion.1.refs_0_), channel_id=1, source_target_pairs={{0,16},{4,20},{8,24},{12,28},{16,0},{20,4},{24,8},{28,12},{1,17},{... | collective-permute-start | bytes 589832 | tf_op jit(solution)/shard_map/ppermute | solution.py:193
  74.0 10.1 %collective-permute-start.14 = (bf16[384,256]{1,0:T(8,128)(2,1)S(1)}, bf16[384,256]{1,0:T(8,128)(2,1)S(1)}, u32[]{:S(2)}, u32[]{:S(2)}) collective-permute-start(bf16[384,256]{1,0:T(8,128)(2,1)S(1)} %fusion.1.refs_0_), channel_id=1, source_target_pairs={{0,4},{4,0},{8,12},{12,8},{16,20},{20,16},{24,28},{28,24},{1,5},{5... | collective-permute-start | bytes 589832 | tf_op jit(solution)/shard_map/ppermute | solution.py:193
  76.1 10.0 %collective-permute-start.29 = (bf16[64,768]{1,0:T(8,128)(2,1)S(1)}, bf16[64,768]{1,0:T(8,128)(2,1)S(1)}, u32[]{:S(2)}, u32[]{:S(2)}) collective-permute-start(bf16[64,768]{1,0:T(8,128)(2,1)S(1)} %convolution_convert_fusion.2), channel_id=1, source_target_pairs={{0,4},{4,0},{8,12},{12,8},{16,20},{20,16},{24,28},{28,24},{1,5},{5... | collective-permute-start | bytes 294920 | tf_op jit(solution)/shard_map/ppermute | solution.py:274
  77.3 12.0 %collective-permute-start.31 = (bf16[64,768]{1,0:T(8,128)(2,1)S(1)}, bf16[64,768]{1,0:T(8,128)(2,1)S(1)}, u32[]{:S(2)}, u32[]{:S(2)}) collective-permute-start(bf16[64,768]{1,0:T(8,128)(2,1)S(1)} %convolution_convert_fusion.1), channel_id=1, source_target_pairs={{0,16},{4,20},{8,24},{12,28},{16,0},{20,4},{24,8},{28,12},{1,17},{... | collective-permute-start | bytes 294920 | tf_op jit(solution)/shard_map/ppermute | solution.py:274
  79.8 9.5 %collective-permute-start.33 = (bf16[64,768]{1,0:T(8,128)(2,1)S(1)}, bf16[64,768]{1,0:T(8,128)(2,1)S(1)}, u32[]{:S(2)}, u32[]{:S(2)}) collective-permute-start(bf16[64,768]{1,0:T(8,128)(2,1)S(1)} %convolution_convert_fusion), channel_id=1, source_target_pairs={{0,20},{4,16},{8,28},{12,24},{16,4},{20,0},{24,12},{28,8},{1,21},{... | collective-permute-start | bytes 294920 | tf_op jit(solution)/shard_map/ppermute | solution.py:274
  83.5 5.8 %collective-permute-start.19 = (bf16[384,256]{1,0:T(8,128)(2,1)S(1)}, bf16[384,256]{1,0:T(8,128)(2,1)S(1)}, u32[]{:S(2)}, u32[]{:S(2)}) collective-permute-start(bf16[384,256]{1,0:T(8,128)(2,1)S(1)} %collective-permute-done.16.refs_2_), channel_id=1, source_target_pairs={{0,8},{8,0},{16,24},{24,16},{1,9},{9,1},{17,25},{25,17},{2,10},{10... | collective-permute-start | bytes 589832 | tf_op jit(solution)/shard_map/ppermute | solution.py:197
  (17 other events, 72.6 us)
